TPU v7x, 256 devices: a whole 4x4x8 slice. The times are simulated.
256 devices in a mesh: sec: 8 (over x, core), op: 32 (over y, z).
Axes of the slice: x: 4, y: 4, z: 8, core: 2. Of those that a mesh axis runs over, the one named last changes fastest.
Arguments:
- wavefunction: bfloat16 [8, 768, 768], P('sec', 'op'), may hold values from -6 to 6
- left_ops: bfloat16 [8, 96, 768, 768], P('sec', 'op'), may hold values from -0.0234375 to 0.0234375
- right_ops: bfloat16 [8, 96, 768, 768], P('sec', 'op'), may hold values from -0.21875 to 0.21875
- diagonal: float32 [8, 768, 768], P('sec', 'op'), may hold values from 0.15 to 10.2
- sector_sizes: int32 [8], P('sec'), may hold values from 192 to 768
- partner: int32 [8], replicated, may hold values from 0 to 7, as said below
Outputs:
- updated: float32 [8, 768, 768], P('sec', 'op')
- residual: float32 [8, 768, 768], P('sec', 'op')
Inputs may be any that keep to these rules, and one draw needn't show every extreme that they name: `partner`: each sector is named exactly once.
All inputs are finite; a program needn't handle non-finite values.
Results may differ from a plain program's by a relative error of at most 0.0017.
Values may be sent and summed in bfloat16 or wider, within the bound.
No kernel may reach another device: no remote copies, remote signals or barrier semaphores. Data moves between devices by JAX's collectives and lax.ppermute only.
A program may use at most 64 MiB of HBM per device.

v0:
```python
import functools

import jax
import jax.numpy as jnp
from jax import lax
from jax.experimental import pallas as pl
from jax.experimental.pallas import tpu as pltpu
from jax.sharding import Mesh
from jax.sharding import PartitionSpec as P


SEC = ("sec_0", "sec_1")
OP = ("op_0", "op_1")
Y, Z = OP
bf16 = jnp.bfloat16
f32 = jnp.float32
VMEM = pl.BlockSpec(memory_space=pltpu.VMEM)
SMEM = pl.BlockSpec(memory_space=pltpu.SMEM)
HBM = pl.BlockSpec(memory_space=pltpu.HBM)
NN = (((1,), (0,)), ((), ()))
TN = (((0,), (0,)), ((), ()))
NT = (((1,), (1,)), ((), ()))


def other_sectors():
    far, near = (lax.axis_size(name) for name in SEC)
    return [(i, j) for i in range(far) for j in range(near) if i or j]


def from_sector(value, step):
    far, near = (lax.axis_size(name) for name in SEC)
    pairs = [
        (i * near + j, (i + step[0]) % far * near + (j + step[1]) % near)
        for i in range(far)
        for j in range(near)
    ]
    return lax.ppermute(value, SEC, pairs)


def sector_behind(step):
    far, near = (lax.axis_size(name) for name in SEC)
    i = lax.rem(lax.axis_index(SEC[0]) - step[0] + far, far)
    j = lax.rem(lax.axis_index(SEC[1]) - step[1] + near, near)
    return i * near + j


def from_ahead(value, steps):
    peers = lax.axis_size(Y)
    return lax.ppermute(value, Y, [(i, (i - steps) % peers) for i in range(peers)])


def to_ahead(value, steps):
    peers = lax.axis_size(Y)
    return lax.ppermute(value, Y, [(i, (i + steps) % peers) for i in range(peers)])


def along_y(move, values):
    moved = []
    for n, value in enumerate(values, 1):
        moved.append(move(value, n))
    return moved


def live_kernel(size_ref, wave_ref, live_ref, copies_ref):
    rows, width = wave_ref.shape
    size = size_ref[0]
    row = lax.axis_index(OP) * rows + lax.broadcasted_iota(jnp.int32, (rows, width), 0)
    col = lax.broadcasted_iota(jnp.int32, (rows, width), 1)
    wave = wave_ref[...].astype(f32)
    live = jnp.where((row < size) & (col < size), wave, 0.0).astype(bf16)
    live_ref[...] = live
    for z in range(copies_ref.shape[0]):
        copies_ref[z] = live


def choose_kernel(steps, partner_ref, live_ref, *refs):
    got_refs, copies_ref = refs[:-1], refs[-1]
    partner = partner_ref[lax.axis_index(SEC)]

    def place(ref):
        value = ref[...]
        for z in range(copies_ref.shape[0]):
            copies_ref[z] = value

    @pl.when(partner == lax.axis_index(SEC))
    def _():
        place(live_ref)

    for step, ref in zip(steps, got_refs):

        @pl.when(partner == sector_behind(step))
        def _(ref=ref):
            place(ref)


def products(x_refs, operators, outs, scratch, first_dims, second_dims):
    left_hbm, right_hbm = operators
    x_all, half, left_ref, right_ref, arrived = scratch
    count = len(x_refs)
    ahead = lax.axis_index(Y)
    rows = x_refs[0].shape[0]
    terms, width, _ = left_ref.shape
    copies = [
        pltpu.make_async_copy(hbm.at[k], ref.at[k], arrived.at[n, k])
        for n, (hbm, ref) in enumerate(((left_hbm, left_ref), (right_hbm, right_ref)))
        for k in range(terms)
    ]
    copies[0].start()
    copies[1].start()
    for step, ref in enumerate(x_refs):
        place = pl.multiple_of(lax.rem(ahead + step, count) * rows, rows)
        x_all[pl.ds(place, rows), :] = ref[...]
    for k in range(terms):
        copies[k].wait()
        for later in copies[2 * k + 2 : 2 * k + 4]:
            later.start()
        first = lax.dot_general(
            left_ref[k], x_all[...], first_dims, preferred_element_type=f32
        ).astype(bf16)
        for block in range(count):
            place = pl.multiple_of(lax.rem(block - ahead + count, count) * rows, rows)
            half[pl.ds(place, rows), k * width : (k + 1) * width] = first[
                block * rows : (block + 1) * rows
            ]
    for copy in copies[terms:]:
        copy.wait()
    if second_dims == NN:
        right = right_ref[...].reshape(terms * width, width)
        total = lax.dot_general(half[...], right, NN, preferred_element_type=f32)
    else:
        total = None
        for k in range(terms):
            part = lax.dot_general(
                half[:, k * width : (k + 1) * width],
                right_ref[k],
                second_dims,
                preferred_element_type=f32,
            )
            total = part if total is None else total + part
    for step in range(count):
        outs[step][...] = total[step * rows : (step + 1) * rows].astype(outs[step].dtype)


def adjoint_kernel(count, left_hbm, right_hbm, *refs):
    products(
        refs[:count], (left_hbm, right_hbm), refs[count : 2 * count], refs[2 * count :], TN, NN
    )


def direct_kernel(count, left_hbm, right_hbm, *refs):
    products(
        refs[:count], (left_hbm, right_hbm), refs[count : 2 * count], refs[2 * count :], NN, NT
    )


def sums_kernel(count, live_ref, diagonal_ref, *refs):
    x_refs, adjoint_refs, sums_ref = refs[:count], refs[count : 2 * count], refs[2 * count]
    wave = live_ref[...].astype(f32)
    square = wave * wave
    norm = jnp.sum(square, axis=0, keepdims=True)
    mixed = jnp.sum(square * diagonal_ref[...], axis=0, keepdims=True)
    for x_ref, adjoint_ref in zip(x_refs, adjoint_refs):
        pair = x_ref[...].astype(f32) * adjoint_ref[...].astype(f32)
        mixed += 2.0 * jnp.sum(pair, axis=0, keepdims=True)
    mixed = jnp.sum(mixed, axis=1, keepdims=True)
    norm = jnp.sum(norm, axis=1, keepdims=True)
    tile = sums_ref.shape
    row = lax.broadcasted_iota(jnp.int32, tile, 0)
    sums_ref[...] = jnp.where(
        row == 0, jnp.broadcast_to(mixed, tile), jnp.broadcast_to(norm, tile)
    )


def tiles_of(rows, width):
    return [(r, c) for r in range(0, rows, 8) for c in range(0, width, 128)]


def rows_kernel(count, *refs):
    blocks, sums_refs, out_ref = refs[:count], refs[count:-1], refs[-1]
    rows, width = blocks[0].shape
    peers = out_ref.shape[0]
    each = rows // peers
    for pair in range(0, peers, 2):
        part = slice(pair * each, (pair + 2) * each)
        total = blocks[0][part, :].astype(f32)
        for ref in blocks[1:]:
            total += ref[part, :].astype(f32)
        for z in range(2):
            for n, (r, c) in enumerate(tiles_of(each, width)):
                out_ref[pair + z, 8 * n : 8 * n + 8, :] = total[
                    z * each + r : z * each + r + 8, c : c + 128
                ]
    if sums_refs:
        total = sums_refs[0][...]
        for ref in sums_refs[1:]:
            total += ref[...]
        for z in range(peers):
            out_ref[z, out_ref.shape[1] - 8 :, :] = total


def meet_kernel(got_ref, out_ref):
    total = got_ref[0]
    for z in range(1, got_ref.shape[0]):
        total += got_ref[z]
    out_ref[...] = total


def update_kernel(
    steps, partner_ref, size_ref, direct_ref, diagonal_ref, live_ref, *refs
):
    got_refs, (updated_ref, residual_ref, routed) = refs[:-3], refs[-3:]
    rows, width = live_ref.shape
    peers, length, _ = direct_ref.shape
    me = lax.axis_index(SEC)
    sums = None
    for step, got_ref in zip([(0, 0)] + steps, got_refs):
        part = got_ref[length:, :]
        sums = part if sums is None else sums + part

        @pl.when(partner_ref[sector_behind(step)] == me)
        def _(got_ref=got_ref):
            routed[...] = got_ref[:length, :]

    energy = sums[0:1, :] / sums[1:2, :]
    size = size_ref[0]
    base = lax.axis_index(OP) * rows
    for n, (r, c) in enumerate(tiles_of(rows, width)):
        where_row = base + r + lax.broadcasted_iota(jnp.int32, (8, 128), 0)
        where_col = c + lax.broadcasted_iota(jnp.int32, (8, 128), 1)
        wave = live_ref[r : r + 8, c : c + 128].astype(f32)
        diagonal = diagonal_ref[r : r + 8, c : c + 128]
        part = slice(8 * n, 8 * n + 8)
        direct = direct_ref[0, part, :]
        for z in range(1, peers):
            direct += direct_ref[z, part, :]
        sigma = direct + routed[part, :] + diagonal * wave
        sigma = jnp.where((where_row < size) & (where_col < size), sigma, 0.0)
        residual = sigma - energy * wave
        residual_ref[r : r + 8, c : c + 128] = residual
        updated_ref[r : r + 8, c : c + 128] = wave - residual / jnp.maximum(
            jnp.abs(diagonal - energy), 1.0
        )


def run(kernel, outs, specs, scratch=(), flops=0, bytes_accessed=2**20, limit=16):
    return pl.pallas_call(
        kernel,
        out_shape=outs,
        in_specs=specs,
        out_specs=jax.tree.map(lambda _: VMEM, outs),
        scratch_shapes=list(scratch),
        compiler_params=pltpu.CompilerParams(vmem_limit_bytes=limit * 2**20),
        cost_estimate=pl.CostEstimate(
            flops=flops, bytes_accessed=bytes_accessed, transcendentals=0
        ),
    )


def per_device(wavefunction, left_ops, right_ops, diagonal, sector_sizes, partner):
    _, rows, width = wavefunction.shape
    terms = left_ops.shape[1]
    lines, peers = lax.axis_size(Y), lax.axis_size(Z)
    left, right, diag = left_ops[0], right_ops[0], diagonal[0]
    block = peers * rows
    length = rows * width // 128
    steps = other_sectors()

    def shape(*dims, dtype=f32):
        return jax.ShapeDtypeStruct(dims, dtype)

    live, copies = run(
        live_kernel,
        [shape(rows, width, dtype=bf16), shape(peers, rows, width, dtype=bf16)],
        [SMEM, VMEM],
    )(sector_sizes, wavefunction[0])
    own = lax.all_to_all(copies, Z, 0, 0, tiled=True).reshape(block, width)
    others = []
    for step in steps:
        others.append(from_sector(live, step))
    copies = run(
        functools.partial(choose_kernel, steps),
        shape(peers, rows, width, dtype=bf16),
        [SMEM] + [VMEM] * (1 + len(steps)),
    )(partner, live, *others)
    theirs = lax.all_to_all(copies, Z, 0, 0, tiled=True).reshape(block, width)
    own_parts = [own] + along_y(from_ahead, [own] * (lines - 1))
    their_parts = [theirs] + along_y(from_ahead, [theirs] * (lines - 1))

    flops = 4 * terms * width**3
    scratch = [
        pltpu.VMEM((width, width), bf16),
        pltpu.VMEM((width, terms * width), bf16),
        pltpu.VMEM((terms, width, width), bf16),
        pltpu.VMEM((terms, width, width), bf16),
        pltpu.SemaphoreType.DMA((2, terms)),
    ]
    outs = [shape(block, width)] + [shape(block, width, dtype=bf16)] * (lines - 1)
    specs = [HBM, HBM] + [VMEM] * lines
    adjoint = run(
        functools.partial(adjoint_kernel, lines), outs, specs, scratch, flops, limit=50
    )(left, right, *own_parts)
    adjoint_got = along_y(to_ahead, adjoint[1:])
    sums = run(
        functools.partial(sums_kernel, lines), shape(8, 128), [VMEM] * (2 + 2 * lines)
    )(live, diag, *their_parts, *adjoint)
    sums_got = along_y(to_ahead, [sums] * (lines - 1))
    direct = run(
        functools.partial(direct_kernel, lines), outs, specs, scratch, flops, limit=50
    )(left, right, *their_parts)
    direct_got = along_y(to_ahead, direct[1:])

    adjoint_lines = run(
        functools.partial(rows_kernel, lines), shape(peers, length + 8, 128), [VMEM] * (2 * lines)
    )(adjoint[0], *adjoint_got, sums, *sums_got)
    adjoint_lines = lax.all_to_all(adjoint_lines, Z, 0, 0, tiled=True)
    adjoint_mine = run(meet_kernel, shape(length + 8, 128), [VMEM])(adjoint_lines)
    routed = [adjoint_mine] + [from_sector(adjoint_mine, step) for step in steps]
    direct_lines = run(
        functools.partial(rows_kernel, lines), shape(peers, length, 128), [VMEM] * lines
    )(direct[0], *direct_got)
    direct_mine = lax.all_to_all(direct_lines, Z, 0, 0, tiled=True)
    updated, residual = run(
        functools.partial(update_kernel, steps),
        [shape(rows, width)] * 2,
        [SMEM, SMEM] + [VMEM] * (3 + len(routed)),
        [pltpu.VMEM((length, 128), f32)],
    )(partner, sector_sizes, direct_mine, diag, live, *routed)
    return updated[None], residual[None]


def solution(mesh):
    finer = Mesh(mesh.devices.reshape(4, 2, 4, 8), SEC + OP)
    return jax.shard_map(
        per_device,
        mesh=finer,
        in_specs=(
            P(SEC, OP, None),
            P(SEC, OP, None, None),
            P(SEC, OP, None, None),
            P(SEC, OP, None),
            P(SEC),
            P(),
        ),
        out_specs=(P(SEC, OP, None), P(SEC, OP, None)),
        check_vma=False,
    )
```

profile of v0, /device:TPU:32, one launch (start us, length us, event | category | flops | bytes accessed | tf_op | source)
XLA Modules:
  0.0 140.1 jit_solution(5703888780132547265)
XLA Ops:
  2.8 8.6 %all-to-all-start.2 = ((bf16[8,24,768]{2,1,0:T(8,128)(2,1)}), bf16[8,24,768]{2,1,0:T(8,128)(2,1)S(1)}, u32[]{:S(2)}, u32[]{:S(2)}) async-start(bf16[8,24,768]{2,1,0:T(8,128)(2,1)} %get-tuple-element.19), calls=%async_computation.2 | async-start | bytes 589824 | tf_op jit(solution)/shard_map/all_to_all | solution.py:276
  11.4 1.5 %collective-permute-start.1 = (bf16[24,768]{1,0:T(8,128)(2,1)S(1)}, bf16[24,768]{1,0:T(8,128)(2,1)S(1)}, u32[]{:S(2)}, u32[]{:S(2)}) collective-permute-start(bf16[24,768]{1,0:T(8,128)(2,1)S(1)} %get-tuple-element.14.live_ref), channel_id=1, source_target_pairs={{0,64},{32,96},{64,128},{96,160},{128,192},{160,224},{192,0},{224,... | collective-permute-start | bytes 110600 | tf_op jit(solution)/shard_map/ppermute | solution.py:37
  14.2 1.7 %collective-permute-start.3 = (bf16[24,768]{1,0:T(8,128)(2,1)S(1)}, bf16[24,768]{1,0:T(8,128)(2,1)S(1)}, u32[]{:S(2)}, u32[]{:S(2)}) collective-permute-start(bf16[24,768]{1,0:T(8,128)(2,1)S(1)} %get-tuple-element.14.live_ref), channel_id=1, source_target_pairs={{0,128},{32,160},{64,192},{96,224},{128,0},{160,32},{192,64},{224,... | collective-permute-start | bytes 110600 | tf_op jit(solution)/shard_map/ppermute | solution.py:37
  17.3 1.7 %collective-permute-start.5 = (bf16[24,768]{1,0:T(8,128)(2,1)S(1)}, bf16[24,768]{1,0:T(8,128)(2,1)S(1)}, u32[]{:S(2)}, u32[]{:S(2)}) collective-permute-start(bf16[24,768]{1,0:T(8,128)(2,1)S(1)} %get-tuple-element.14.live_ref), channel_id=1, source_target_pairs={{0,192},{32,224},{64,0},{96,32},{128,64},{160,96},{192,128},{224,1... | collective-permute-start | bytes 110600 | tf_op jit(solution)/shard_map/ppermute | solution.py:37
  24.5 7.2 %all-to-all-start = ((bf16[8,24,768]{2,1,0:T(8,128)(2,1)}), bf16[8,24,768]{2,1,0:T(8,128)(2,1)S(1)}, u32[]{:S(2)}, u32[]{:S(2)}) async-start(bf16[8,24,768]{2,1,0:T(8,128)(2,1)} %shard_map.78), calls=%async_computation | async-start | bytes 589824 | tf_op jit(solution)/shard_map/all_to_all | solution.py:285
  31.7 3.0 %collective-permute-start.13 = (bf16[192,768]{1,0:T(8,128)(2,1)S(1)}, bf16[192,768]{1,0:T(8,128)(2,1)S(1)}, u32[]{:S(2)}, u32[]{:S(2)}) collective-permute-start(bf16[192,768]{1,0:T(8,128)(2,1)S(1)} %bitcast.15), channel_id=1, source_target_pairs={{0,24},{8,0},{16,8},{24,16},{1,25},{9,1},{17,9},{25,17},{2,26},{10... | collective-permute-start | bytes 884744 | tf_op jit(solution)/shard_map/ppermute | solution.py:49
  36.3 6.9 %all-to-all-done = bf16[8,24,768]{2,1,0:T(8,128)(2,1)S(1)} async-done(((bf16[8,24,768]{2,1,0:T(8,128)(2,1)}), bf16[8,24,768]{2,1,0:T(8,128)(2,1)S(1)}, u32[]{:S(2)}, u32[]{:S(2)}) %all-to-all-start) | async-done | bytes 294944 | tf_op jit(solution)/shard_map/all_to_all | solution.py:285
  43.2 3.0 %collective-permute-start.7 = (bf16[192,768]{1,0:T(8,128)(2,1)S(1)}, bf16[192,768]{1,0:T(8,128)(2,1)S(1)}, u32[]{:S(2)}, u32[]{:S(2)}) collective-permute-start(bf16[192,768]{1,0:T(8,128)(2,1)S(1)} %bitcast.8), channel_id=1, source_target_pairs={{0,24},{8,0},{16,8},{24,16},{1,25},{9,1},{17,9},{25,17},{2,26},{10... | collective-permute-start | bytes 884744 | tf_op jit(solution)/shard_map/ppermute | solution.py:49
  46.8 1.6 %collective-permute-done.13.refs_1_ = bf16[192,768]{1,0:T(8,128)(2,1)S(1)} collective-permute-done((bf16[192,768]{1,0:T(8,128)(2,1)S(1)}, bf16[192,768]{1,0:T(8,128)(2,1)S(1)}, u32[]{:S(2)}, u32[]{:S(2)}) %collective-permute-start.13) | collective-permute-done | bytes 294944 | tf_op jit(solution)/shard_map/ppermute | solution.py:49
  48.4 4.1 %collective-permute-done.15.refs_3_ = bf16[192,768]{1,0:T(8,128)(2,1)S(1)} collective-permute-done((bf16[192,768]{1,0:T(8,128)(2,1)S(1)}, bf16[192,768]{1,0:T(8,128)(2,1)S(1)}, u32[]{:S(2)}, u32[]{:S(2)}) %collective-permute-start.15) | collective-permute-done | bytes 294944 | tf_op jit(solution)/shard_map/ppermute | solution.py:49
  52.5 10.0 %shard_map.81 = (f32[192,768]{1,0:T(8,128)S(1)}, bf16[192,768]{1,0:T(8,128)(2,1)S(1)}, bf16[192,768]{1,0:T(8,128)(2,1)S(1)}, bf16[192,768]{1,0:T(8,128)(2,1)S(1)}) custom-call(bf16[3,768,768]{2,1,0:T(8,128)(2,1)} %bitcast.20, bf16[3,768,768]{2,1,0:T(8,128)(2,1)} %bitcast.22, bf16[192,768]{1,0:T(8,128)(2,1)S(1)} %bitcast.18, ...), custom_call_target="tpu_custom_call" | custom-call | flops 5435817984 | bytes 1048576 | tf_op jit(solution)/shard_map/pallas_call | solution.py:299
  62.6 2.0 %collective-permute-start.17 = (bf16[192,768]{1,0:T(8,128)(2,1)S(1)}, bf16[192,768]{1,0:T(8,128)(2,1)S(1)}, u32[]{:S(2)}, u32[]{:S(2)}) collective-permute-start(bf16[192,768]{1,0:T(8,128)(2,1)S(1)} %get-tuple-element.22.refs_6_), channel_id=1, source_target_pairs={{0,16},{8,24},{16,0},{24,8},{1,17},{9,25},{17,1},{25,9},{2,18},{10... | collective-permute-start | bytes 884744 | tf_op jit(solution)/shard_map/ppermute | solution.py:54
  64.5 1.8 %collective-permute-start.18 = (bf16[192,768]{1,0:T(8,128)(2,1)S(1)}, bf16[192,768]{1,0:T(8,128)(2,1)S(1)}, u32[]{:S(2)}, u32[]{:S(2)}) collective-permute-start(bf16[192,768]{1,0:T(8,128)(2,1)S(1)} %get-tuple-element.23.refs_7_), channel_id=1, source_target_pairs={{0,24},{8,0},{16,8},{24,16},{1,25},{9,1},{17,9},{25,17},{2,26},{10... | collective-permute-start | bytes 884744 | tf_op jit(solution)/shard_map/ppermute | solution.py:54
  67.0 2.1 %collective-permute-start.20 = (f32[8,128]{1,0:T(8,128)S(1)}, f32[8,128]{1,0:T(8,128)S(1)}, u32[]{:S(2)}, u32[]{:S(2)}) collective-permute-start(f32[8,128]{1,0:T(8,128)S(1)} %shard_map.82.refs_4_), channel_id=1, source_target_pairs={{0,16},{8,24},{16,0},{24,8},{1,17},{9,25},{17,1},{25,9},{2,18},{10... | collective-permute-start | bytes 12296 | tf_op jit(solution)/shard_map/ppermute | solution.py:54
  69.2 9.8 %collective-permute-done.19.refs_5_ = f32[8,128]{1,0:T(8,128)S(1)} collective-permute-done((f32[8,128]{1,0:T(8,128)S(1)}, f32[8,128]{1,0:T(8,128)S(1)}, u32[]{:S(2)}, u32[]{:S(2)}) %collective-permute-start.19) | collective-permute-done | bytes 4128 | tf_op jit(solution)/shard_map/ppermute | solution.py:54
  79.0 3.6 %collective-permute-done.21.refs_7_ = f32[8,128]{1,0:T(8,128)S(1)} collective-permute-done((f32[8,128]{1,0:T(8,128)S(1)}, f32[8,128]{1,0:T(8,128)S(1)}, u32[]{:S(2)}, u32[]{:S(2)}) %collective-permute-start.21) | collective-permute-done | bytes 4128 | tf_op jit(solution)/shard_map/ppermute | solution.py:54
  83.6 7.2 %all-to-all-start.3 = ((f32[8,152,128]{2,1,0:T(8,128)}), f32[8,152,128]{2,1,0:T(8,128)S(1)}, u32[]{:S(2)}, u32[]{:S(2)}) async-start(f32[8,152,128]{2,1,0:T(8,128)} %shard_map.83), calls=%async_computation.3 | async-start | bytes 1245184 | tf_op jit(solution)/shard_map/all_to_all | solution.py:315
  90.8 9.9 %shard_map.79 = (f32[192,768]{1,0:T(8,128)S(1)}, bf16[192,768]{1,0:T(8,128)(2,1)S(1)}, bf16[192,768]{1,0:T(8,128)(2,1)S(1)}, bf16[192,768]{1,0:T(8,128)(2,1)S(1)}) custom-call(bf16[3,768,768]{2,1,0:T(8,128)(2,1)} %bitcast.21, bf16[3,768,768]{2,1,0:T(8,128)(2,1)} %bitcast.23, bf16[192,768]{1,0:T(8,128)(2,1)S(1)} %bitcast.12, ...), custom_call_target="tpu_custom_call" | custom-call | flops 5435817984 | bytes 1048576 | tf_op jit(solution)/shard_map/pallas_call | solution.py:307
  100.8 2.7 %collective-permute-start.11 = (bf16[192,768]{1,0:T(8,128)(2,1)S(1)}, bf16[192,768]{1,0:T(8,128)(2,1)S(1)}, u32[]{:S(2)}, u32[]{:S(2)}) collective-permute-start(bf16[192,768]{1,0:T(8,128)(2,1)S(1)} %get-tuple-element.17), channel_id=1, source_target_pairs={{0,16},{8,24},{16,0},{24,8},{1,17},{9,25},{17,1},{25,9},{2,18},{10... | collective-permute-start | bytes 884744 | tf_op jit(solution)/shard_map/ppermute | solution.py:54
  104.0 10.7 %collective-permute-done.10.refs_1_ = bf16[192,768]{1,0:T(8,128)(2,1)S(1)} collective-permute-done((bf16[192,768]{1,0:T(8,128)(2,1)S(1)}, bf16[192,768]{1,0:T(8,128)(2,1)S(1)}, u32[]{:S(2)}, u32[]{:S(2)}) %collective-permute-start.10) | collective-permute-done | bytes 294944 | tf_op jit(solution)/shard_map/ppermute | solution.py:54
  116.0 7.2 %all-to-all-start.1 = ((f32[8,144,128]{2,1,0:T(8,128)}), f32[8,144,128]{2,1,0:T(8,128)S(1)}, u32[]{:S(2)}, u32[]{:S(2)}) async-start(f32[8,144,128]{2,1,0:T(8,128)} %shard_map.80), calls=%async_computation.1 | async-start | bytes 1179648 | tf_op jit(solution)/shard_map/all_to_all | solution.py:321
  124.6 3.2 %collective-permute-start.25 = (f32[152,128]{1,0:T(8,128)S(1)}, f32[152,128]{1,0:T(8,128)S(1)}, u32[]{:S(2)}, u32[]{:S(2)}) collective-permute-start(f32[152,128]{1,0:T(8,128)S(1)} %shard_map.84.refs_0_), channel_id=1, source_target_pairs={{0,128},{32,160},{64,192},{96,224},{128,0},{160,32},{192,64},{224,... | collective-permute-start | bytes 233480 | tf_op jit(solution)/shard_map/ppermute | solution.py:37
  127.9 2.8 %collective-permute-start.27 = (f32[152,128]{1,0:T(8,128)S(1)}, f32[152,128]{1,0:T(8,128)S(1)}, u32[]{:S(2)}, u32[]{:S(2)}) collective-permute-start(f32[152,128]{1,0:T(8,128)S(1)} %shard_map.84.refs_0_), channel_id=1, source_target_pairs={{0,192},{32,224},{64,0},{96,32},{128,64},{160,96},{192,128},{224,1... | collective-permute-start | bytes 233480 | tf_op jit(solution)/shard_map/ppermute | solution.py:37
  131.4 7.3 %all-to-all-done.1.direct_ref = f32[8,144,128]{2,1,0:T(8,128)S(1)} async-done(((f32[8,144,128]{2,1,0:T(8,128)}), f32[8,144,128]{2,1,0:T(8,128)S(1)}, u32[]{:S(2)}, u32[]{:S(2)}) %all-to-all-start.1) | async-done | bytes 589856 | tf_op jit(solution)/shard_map/all_to_all | solution.py:321
  (59 shorter events, 19.2 us)
Async XLA Ops:
  2.8 21.7 %all-to-all-start.2 = ((bf16[8,24,768]{2,1,0:T(8,128)(2,1)}), bf16[8,24,768]{2,1,0:T(8,128)(2,1)S(1)}, u32[]{:S(2)}, u32[]{:S(2)}) async-start(bf16[8,24,768]{2,1,0:T(8,128)(2,1)} %get-tuple-element.19), calls=%async_computation.2 | async-start | bytes 589824 | tf_op jit(solution)/shard_map/all_to_all | solution.py:276
  11.4 7.7 %collective-permute-start.1 = (bf16[24,768]{1,0:T(8,128)(2,1)S(1)}, bf16[24,768]{1,0:T(8,128)(2,1)S(1)}, u32[]{:S(2)}, u32[]{:S(2)}) collective-permute-start(bf16[24,768]{1,0:T(8,128)(2,1)S(1)} %get-tuple-element.14.live_ref), channel_id=1, source_target_pairs={{0,64},{32,96},{64,128},{96,160},{128,192},{160,224},{192,0},{224,... | collective-permute-start | bytes 110600 | tf_op jit(solution)/shard_map/ppermute | solution.py:37
  24.5 18.7 %all-to-all-start = ((bf16[8,24,768]{2,1,0:T(8,128)(2,1)}), bf16[8,24,768]{2,1,0:T(8,128)(2,1)S(1)}, u32[]{:S(2)}, u32[]{:S(2)}) async-start(bf16[8,24,768]{2,1,0:T(8,128)(2,1)} %shard_map.78), calls=%async_computation | async-start | bytes 589824 | tf_op jit(solution)/shard_map/all_to_all | solution.py:285
  31.7 16.7 %collective-permute-start.13 = (bf16[192,768]{1,0:T(8,128)(2,1)S(1)}, bf16[192,768]{1,0:T(8,128)(2,1)S(1)}, u32[]{:S(2)}, u32[]{:S(2)}) collective-permute-start(bf16[192,768]{1,0:T(8,128)(2,1)S(1)} %bitcast.15), channel_id=1, source_target_pairs={{0,24},{8,0},{16,8},{24,16},{1,25},{9,1},{17,9},{25,17},{2,26},{10... | collective-permute-start | bytes 884744 | tf_op jit(solution)/shard_map/ppermute | solution.py:49
  34.7 13.7 %collective-permute-start.14 = (bf16[192,768]{1,0:T(8,128)(2,1)S(1)}, bf16[192,768]{1,0:T(8,128)(2,1)S(1)}, u32[]{:S(2)}, u32[]{:S(2)}) collective-permute-start(bf16[192,768]{1,0:T(8,128)(2,1)S(1)} %bitcast.16), channel_id=1, source_target_pairs={{0,16},{8,24},{16,0},{24,8},{1,17},{9,25},{17,1},{25,9},{2,18},{10... | collective-permute-start | bytes 884744 | tf_op jit(solution)/shard_map/ppermute | solution.py:49
  35.3 17.2 %collective-permute-start.15 = (bf16[192,768]{1,0:T(8,128)(2,1)S(1)}, bf16[192,768]{1,0:T(8,128)(2,1)S(1)}, u32[]{:S(2)}, u32[]{:S(2)}) collective-permute-start(bf16[192,768]{1,0:T(8,128)(2,1)S(1)} %bitcast.17), channel_id=1, source_target_pairs={{0,8},{8,16},{16,24},{24,0},{1,9},{9,17},{17,25},{25,1},{2,10},{10... | collective-permute-start | bytes 884744 | tf_op jit(solution)/shard_map/ppermute | solution.py:49
  43.2 21.3 %collective-permute-start.7 = (bf16[192,768]{1,0:T(8,128)(2,1)S(1)}, bf16[192,768]{1,0:T(8,128)(2,1)S(1)}, u32[]{:S(2)}, u32[]{:S(2)}) collective-permute-start(bf16[192,768]{1,0:T(8,128)(2,1)S(1)} %bitcast.8), channel_id=1, source_target_pairs={{0,24},{8,0},{16,8},{24,16},{1,25},{9,1},{17,9},{25,17},{2,26},{10... | collective-permute-start | bytes 884744 | tf_op jit(solution)/shard_map/ppermute | solution.py:49
  46.2 20.1 %collective-permute-start.8 = (bf16[192,768]{1,0:T(8,128)(2,1)S(1)}, bf16[192,768]{1,0:T(8,128)(2,1)S(1)}, u32[]{:S(2)}, u32[]{:S(2)}) collective-permute-start(bf16[192,768]{1,0:T(8,128)(2,1)S(1)} %bitcast.9), channel_id=1, source_target_pairs={{0,16},{8,24},{16,0},{24,8},{1,17},{9,25},{17,1},{25,9},{2,18},{10... | collective-permute-start | bytes 884744 | tf_op jit(solution)/shard_map/ppermute | solution.py:49
  48.4 17.9 %collective-permute-start.9 = (bf16[192,768]{1,0:T(8,128)(2,1)S(1)}, bf16[192,768]{1,0:T(8,128)(2,1)S(1)}, u32[]{:S(2)}, u32[]{:S(2)}) collective-permute-start(bf16[192,768]{1,0:T(8,128)(2,1)S(1)} %bitcast.10), channel_id=1, source_target_pairs={{0,8},{8,16},{16,24},{24,0},{1,9},{9,17},{17,25},{25,1},{2,10},{10... | collective-permute-start | bytes 884744 | tf_op jit(solution)/shard_map/ppermute | solution.py:49
  62.5 20.1 %collective-permute-start.16 = (bf16[192,768]{1,0:T(8,128)(2,1)S(1)}, bf16[192,768]{1,0:T(8,128)(2,1)S(1)}, u32[]{:S(2)}, u32[]{:S(2)}) collective-permute-start(bf16[192,768]{1,0:T(8,128)(2,1)S(1)} %get-tuple-element.21.refs_5_), channel_id=1, source_target_pairs={{0,8},{8,16},{16,24},{24,0},{1,9},{9,17},{17,25},{25,1},{2,10},{10... | collective-permute-start | bytes 884744 | tf_op jit(solution)/shard_map/ppermute | solution.py:54
  62.6 20.0 %collective-permute-start.17 = (bf16[192,768]{1,0:T(8,128)(2,1)S(1)}, bf16[192,768]{1,0:T(8,128)(2,1)S(1)}, u32[]{:S(2)}, u32[]{:S(2)}) collective-permute-start(bf16[192,768]{1,0:T(8,128)(2,1)S(1)} %get-tuple-element.22.refs_6_), channel_id=1, source_target_pairs={{0,16},{8,24},{16,0},{24,8},{1,17},{9,25},{17,1},{25,9},{2,18},{10... | collective-permute-start | bytes 884744 | tf_op jit(solution)/shard_map/ppermute | solution.py:54
  64.5 18.0 %collective-permute-start.18 = (bf16[192,768]{1,0:T(8,128)(2,1)S(1)}, bf16[192,768]{1,0:T(8,128)(2,1)S(1)}, u32[]{:S(2)}, u32[]{:S(2)}) collective-permute-start(bf16[192,768]{1,0:T(8,128)(2,1)S(1)} %get-tuple-element.23.refs_7_), channel_id=1, source_target_pairs={{0,24},{8,0},{16,8},{24,16},{1,25},{9,1},{17,9},{25,17},{2,26},{10... | collective-permute-start | bytes 884744 | tf_op jit(solution)/shard_map/ppermute | solution.py:54
  66.6 12.3 %collective-permute-start.19 = (f32[8,128]{1,0:T(8,128)S(1)}, f32[8,128]{1,0:T(8,128)S(1)}, u32[]{:S(2)}, u32[]{:S(2)}) collective-permute-start(f32[8,128]{1,0:T(8,128)S(1)} %shard_map.82.refs_4_), channel_id=1, source_target_pairs={{0,8},{8,16},{16,24},{24,0},{1,9},{9,17},{17,25},{25,1},{2,10},{10... | collective-permute-start | bytes 12296 | tf_op jit(solution)/shard_map/ppermute | solution.py:54
  67.0 11.9 %collective-permute-start.20 = (f32[8,128]{1,0:T(8,128)S(1)}, f32[8,128]{1,0:T(8,128)S(1)}, u32[]{:S(2)}, u32[]{:S(2)}) collective-permute-start(f32[8,128]{1,0:T(8,128)S(1)} %shard_map.82.refs_4_), channel_id=1, source_target_pairs={{0,16},{8,24},{16,0},{24,8},{1,17},{9,25},{17,1},{25,9},{2,18},{10... | collective-permute-start | bytes 12296 | tf_op jit(solution)/shard_map/ppermute | solution.py:54
  83.6 32.4 %all-to-all-start.3 = ((f32[8,152,128]{2,1,0:T(8,128)}), f32[8,152,128]{2,1,0:T(8,128)S(1)}, u32[]{:S(2)}, u32[]{:S(2)}) async-start(f32[8,152,128]{2,1,0:T(8,128)} %shard_map.83), calls=%async_computation.3 | async-start | bytes 1245184 | tf_op jit(solution)/shard_map/all_to_all | solution.py:315
  100.7 14.0 %collective-permute-start.10 = (bf16[192,768]{1,0:T(8,128)(2,1)S(1)}, bf16[192,768]{1,0:T(8,128)(2,1)S(1)}, u32[]{:S(2)}, u32[]{:S(2)}) collective-permute-start(bf16[192,768]{1,0:T(8,128)(2,1)S(1)} %get-tuple-element.16), channel_id=1, source_target_pairs={{0,8},{8,16},{16,24},{24,0},{1,9},{9,17},{17,25},{25,1},{2,10},{10... | collective-permute-start | bytes 884744 | tf_op jit(solution)/shard_map/ppermute | solution.py:54
  100.8 13.9 %collective-permute-start.11 = (bf16[192,768]{1,0:T(8,128)(2,1)S(1)}, bf16[192,768]{1,0:T(8,128)(2,1)S(1)}, u32[]{:S(2)}, u32[]{:S(2)}) collective-permute-start(bf16[192,768]{1,0:T(8,128)(2,1)S(1)} %get-tuple-element.17), channel_id=1, source_target_pairs={{0,16},{8,24},{16,0},{24,8},{1,17},{9,25},{17,1},{25,9},{2,18},{10... | collective-permute-start | bytes 884744 | tf_op jit(solution)/shard_map/ppermute | solution.py:54
  103.4 11.6 %collective-permute-start.12 = (bf16[192,768]{1,0:T(8,128)(2,1)S(1)}, bf16[192,768]{1,0:T(8,128)(2,1)S(1)}, u32[]{:S(2)}, u32[]{:S(2)}) collective-permute-start(bf16[192,768]{1,0:T(8,128)(2,1)S(1)} %get-tuple-element.18), channel_id=1, source_target_pairs={{0,24},{8,0},{16,8},{24,16},{1,25},{9,1},{17,9},{25,17},{2,26},{10... | collective-permute-start | bytes 884744 | tf_op jit(solution)/shard_map/ppermute | solution.py:54
  116.0 22.7 %all-to-all-start.1 = ((f32[8,144,128]{2,1,0:T(8,128)}), f32[8,144,128]{2,1,0:T(8,128)S(1)}, u32[]{:S(2)}, u32[]{:S(2)}) async-start(f32[8,144,128]{2,1,0:T(8,128)} %shard_map.80), calls=%async_computation.1 | async-start | bytes 1179648 | tf_op jit(solution)/shard_map/all_to_all | solution.py:321
  124.5 14.2 %collective-permute-start.24 = (f32[152,128]{1,0:T(8,128)S(1)}, f32[152,128]{1,0:T(8,128)S(1)}, u32[]{:S(2)}, u32[]{:S(2)}) collective-permute-start(f32[152,128]{1,0:T(8,128)S(1)} %shard_map.84.refs_0_), channel_id=1, source_target_pairs={{0,96},{32,64},{64,160},{96,128},{128,224},{160,192},{192,32},{224... | collective-permute-start | bytes 233480 | tf_op jit(solution)/shard_map/ppermute | solution.py:37
  124.6 14.1 %collective-permute-start.25 = (f32[152,128]{1,0:T(8,128)S(1)}, f32[152,128]{1,0:T(8,128)S(1)}, u32[]{:S(2)}, u32[]{:S(2)}) collective-permute-start(f32[152,128]{1,0:T(8,128)S(1)} %shard_map.84.refs_0_), channel_id=1, source_target_pairs={{0,128},{32,160},{64,192},{96,224},{128,0},{160,32},{192,64},{224,... | collective-permute-start | bytes 233480 | tf_op jit(solution)/shard_map/ppermute | solution.py:37
  127.9 10.9 %collective-permute-start.26 = (f32[152,128]{1,0:T(8,128)S(1)}, f32[152,128]{1,0:T(8,128)S(1)}, u32[]{:S(2)}, u32[]{:S(2)}) collective-permute-start(f32[152,128]{1,0:T(8,128)S(1)} %shard_map.84.refs_0_), channel_id=1, source_target_pairs={{0,160},{32,128},{64,224},{96,192},{128,32},{160,0},{192,96},{224,... | collective-permute-start | bytes 233480 | tf_op jit(solution)/shard_map/ppermute | solution.py:37
  127.9 10.9 %collective-permute-start.27 = (f32[152,128]{1,0:T(8,128)S(1)}, f32[152,128]{1,0:T(8,128)S(1)}, u32[]{:S(2)}, u32[]{:S(2)}) collective-permute-start(f32[152,128]{1,0:T(8,128)S(1)} %shard_map.84.refs_0_), channel_id=1, source_target_pairs={{0,192},{32,224},{64,0},{96,32},{128,64},{160,96},{192,128},{224,1... | collective-permute-start | bytes 233480 | tf_op jit(solution)/shard_map/ppermute | solution.py:37
  130.7 8.0 %collective-permute-start.28 = (f32[152,128]{1,0:T(8,128)S(1)}, f32[152,128]{1,0:T(8,128)S(1)}, u32[]{:S(2)}, u32[]{:S(2)}) collective-permute-start(f32[152,128]{1,0:T(8,128)S(1)} %shard_map.84.refs_0_), channel_id=1, source_target_pairs={{0,224},{32,192},{64,32},{96,0},{128,96},{160,64},{192,160},{224,1... | collective-permute-start | bytes 233480 | tf_op jit(solution)/shard_map/ppermute | solution.py:37
  (13 other events, 99.5 us)
where the time goes:
time: 143 us; the launch traced here: 140 us
  starting transfers between devices  64.3 us (45%)
  waiting for transfers between devices  47.3 us (33%)
  Pallas kernels  25.6 us (18%)
  local copies, waits for them, and re-layouts  1.43 us (1%)
    ppermute x9, waiting for transfers between devices, to_ahead(): lax.ppermute(value, Y, [(i, (i + steps) % peers) for i in range(peers)])  24.4 us
    ppermute x14, starting transfers between devices, from_sector(): return lax.ppermute(value, SEC, pairs)  16.2 us
    pallas_call x1, Pallas kernels, per_device(): run(functools.partial(adjoint_kernel, lines), outs, specs, scratch, flops...  9.98 us
    pallas_call x1, Pallas kernels, per_device(): run(functools.partial(direct_kernel, lines), outs, specs, scratch, flops,...  9.9 us
    ppermute x9, starting transfers between devices, to_ahead(): lax.ppermute(value, Y, [(i, (i + steps) % peers) for i in range(peers)])  9.66 us
    all_to_all x1, starting transfers between devices, per_device(): own = lax.all_to_all(copies, Z, 0, 0, tiled=True).reshape(block, width)  8.57 us
    ppermute x6, starting transfers between devices, from_ahead(): lax.ppermute(value, Y, [(i, (i - steps) % peers) for i in range(peers)])  8.26 us
    all_to_all x1, waiting for transfers between devices, per_device(): direct_mine = lax.all_to_all(direct_lines, Z, 0, 0, tiled=True)  7.3 us
  transfers between devices with their start and end apart: 33, of which 12 were waited for; matrix products, arithmetic and copies ran while one was open for 0% of the time, Pallas kernels for 16%

commit v1 on v0

--- a/solution.py
+++ b/solution.py
@@ -100,36 +100,38 @@
     ahead = lax.axis_index(Y)
     rows = x_refs[0].shape[0]
     terms, width, _ = left_ref.shape
+    copies = []
+    for k in range(terms):
+        copies.append((left_hbm, left_ref, 0, k))
+        if k:
+            copies.append((right_hbm, right_ref, 1, k - 1))
+    copies.append((right_hbm, right_ref, 1, terms - 1))
     copies = [
-        pltpu.make_async_copy(hbm.at[k], ref.at[k], arrived.at[n, k])
-        for n, (hbm, ref) in enumerate(((left_hbm, left_ref), (right_hbm, right_ref)))
-        for k in range(terms)
+        pltpu.make_async_copy(hbm.at[k], ref.at[k], arrived.at[side, k])
+        for hbm, ref, side, k in copies
     ]
     copies[0].start()
     copies[1].start()
     for step, ref in enumerate(x_refs):
         place = pl.multiple_of(lax.rem(ahead + step, count) * rows, rows)
         x_all[pl.ds(place, rows), :] = ref[...]
-    for k in range(terms):
-        copies[k].wait()
-        for later in copies[2 * k + 2 : 2 * k + 4]:
-            later.start()
-        first = lax.dot_general(
-            left_ref[k], x_all[...], first_dims, preferred_element_type=f32
-        ).astype(bf16)
-        for block in range(count):
-            place = pl.multiple_of(lax.rem(block - ahead + count, count) * rows, rows)
-            half[pl.ds(place, rows), k * width : (k + 1) * width] = first[
-                block * rows : (block + 1) * rows
-            ]
-    for copy in copies[terms:]:
-        copy.wait()
-    if second_dims == NN:
-        right = right_ref[...].reshape(terms * width, width)
-        total = lax.dot_general(half[...], right, NN, preferred_element_type=f32)
-    else:
-        total = None
-        for k in range(terms):
+    total = None
+    for n in range(2 * terms):
+        copies[n].wait()
+        if n + 2 < 2 * terms:
+            copies[n + 2].start()
+        if n == 0 or (n % 2 and n < 2 * terms - 1):
+            k = (n + 1) // 2
+            first = lax.dot_general(
+                left_ref[k], x_all[...], first_dims, preferred_element_type=f32
+            ).astype(bf16)
+            for block in range(count):
+                place = pl.multiple_of(lax.rem(block - ahead + count, count) * rows, rows)
+                half[pl.ds(place, rows), k * width : (k + 1) * width] = first[
+                    block * rows : (block + 1) * rows
+                ]
+        else:
+            k = n // 2 - 1 if n < 2 * terms - 1 else terms - 1
             part = lax.dot_general(
                 half[:, k * width : (k + 1) * width],
                 right_ref[k],

time: 143 us -> 143 us (level)
  no operation moved by 1% of the time
where the time goes in v1:
time: 143 us; the launch traced here: 141 us
  starting transfers between devices  64.3 us (45%)
  waiting for transfers between devices  47.3 us (33%)
  Pallas kernels  26.3 us (18%)
  local copies, waits for them, and re-layouts  1.43 us (1%)
    ppermute x9, waiting for transfers between devices, to_ahead(): lax.ppermute(value, Y, [(i, (i + steps) % peers) for i in range(peers)])  24.4 us
    ppermute x14, starting transfers between devices, from_sector(): return lax.ppermute(value, SEC, pairs)  16.2 us
    pallas_call x1, Pallas kernels, per_device(): run(functools.partial(adjoint_kernel, lines), outs, specs, scratch, flops...  10.3 us
    pallas_call x1, Pallas kernels, per_device(): run(functools.partial(direct_kernel, lines), outs, specs, scratch, flops,...  10.2 us
    ppermute x9, starting transfers between devices, to_ahead(): lax.ppermute(value, Y, [(i, (i + steps) % peers) for i in range(peers)])  9.66 us
    all_to_all x1, starting transfers between devices, per_device(): own = lax.all_to_all(copies, Z, 0, 0, tiled=True).reshape(block, width)  8.57 us
    ppermute x6, starting transfers between devices, from_ahead(): lax.ppermute(value, Y, [(i, (i - steps) % peers) for i in range(peers)])  8.26 us
    all_to_all x1, waiting for transfers between devices, per_device(): direct_mine = lax.all_to_all(direct_lines, Z, 0, 0, tiled=True)  7.31 us
  transfers between devices with their start and end apart: 33, of which 12 were waited for; matrix products, arithmetic and copies ran while one was open for 0% of the time, Pallas kernels for 16%

profile of v1, /device:TPU:32, one launch (start us, length us, event | category | flops | bytes accessed | tf_op | source)
XLA Modules:
  0.0 140.8 jit_solution(3694580746828349148)
XLA Ops:
  2.8 8.6 %all-to-all-start.2 = ((bf16[8,24,768]{2,1,0:T(8,128)(2,1)}), bf16[8,24,768]{2,1,0:T(8,128)(2,1)S(1)}, u32[]{:S(2)}, u32[]{:S(2)}) async-start(bf16[8,24,768]{2,1,0:T(8,128)(2,1)} %get-tuple-element.19), calls=%async_computation.2 | async-start | bytes 589824 | tf_op jit(solution)/shard_map/all_to_all | solution.py:278
  11.4 1.5 %collective-permute-start.1 = (bf16[24,768]{1,0:T(8,128)(2,1)S(1)}, bf16[24,768]{1,0:T(8,128)(2,1)S(1)}, u32[]{:S(2)}, u32[]{:S(2)}) collective-permute-start(bf16[24,768]{1,0:T(8,128)(2,1)S(1)} %get-tuple-element.14.live_ref), channel_id=1, source_target_pairs={{0,64},{32,96},{64,128},{96,160},{128,192},{160,224},{192,0},{224,... | collective-permute-start | bytes 110600 | tf_op jit(solution)/shard_map/ppermute | solution.py:37
  14.2 1.7 %collective-permute-start.3 = (bf16[24,768]{1,0:T(8,128)(2,1)S(1)}, bf16[24,768]{1,0:T(8,128)(2,1)S(1)}, u32[]{:S(2)}, u32[]{:S(2)}) collective-permute-start(bf16[24,768]{1,0:T(8,128)(2,1)S(1)} %get-tuple-element.14.live_ref), channel_id=1, source_target_pairs={{0,128},{32,160},{64,192},{96,224},{128,0},{160,32},{192,64},{224,... | collective-permute-start | bytes 110600 | tf_op jit(solution)/shard_map/ppermute | solution.py:37
  17.3 1.7 %collective-permute-start.5 = (bf16[24,768]{1,0:T(8,128)(2,1)S(1)}, bf16[24,768]{1,0:T(8,128)(2,1)S(1)}, u32[]{:S(2)}, u32[]{:S(2)}) collective-permute-start(bf16[24,768]{1,0:T(8,128)(2,1)S(1)} %get-tuple-element.14.live_ref), channel_id=1, source_target_pairs={{0,192},{32,224},{64,0},{96,32},{128,64},{160,96},{192,128},{224,1... | collective-permute-start | bytes 110600 | tf_op jit(solution)/shard_map/ppermute | solution.py:37
  24.5 7.2 %all-to-all-start = ((bf16[8,24,768]{2,1,0:T(8,128)(2,1)}), bf16[8,24,768]{2,1,0:T(8,128)(2,1)S(1)}, u32[]{:S(2)}, u32[]{:S(2)}) async-start(bf16[8,24,768]{2,1,0:T(8,128)(2,1)} %shard_map.78), calls=%async_computation | async-start | bytes 589824 | tf_op jit(solution)/shard_map/all_to_all | solution.py:287
  31.7 3.0 %collective-permute-start.13 = (bf16[192,768]{1,0:T(8,128)(2,1)S(1)}, bf16[192,768]{1,0:T(8,128)(2,1)S(1)}, u32[]{:S(2)}, u32[]{:S(2)}) collective-permute-start(bf16[192,768]{1,0:T(8,128)(2,1)S(1)} %bitcast.15), channel_id=1, source_target_pairs={{0,24},{8,0},{16,8},{24,16},{1,25},{9,1},{17,9},{25,17},{2,26},{10... | collective-permute-start | bytes 884744 | tf_op jit(solution)/shard_map/ppermute | solution.py:49
  36.3 6.9 %all-to-all-done = bf16[8,24,768]{2,1,0:T(8,128)(2,1)S(1)} async-done(((bf16[8,24,768]{2,1,0:T(8,128)(2,1)}), bf16[8,24,768]{2,1,0:T(8,128)(2,1)S(1)}, u32[]{:S(2)}, u32[]{:S(2)}) %all-to-all-start) | async-done | bytes 294944 | tf_op jit(solution)/shard_map/all_to_all | solution.py:287
  43.2 3.0 %collective-permute-start.7 = (bf16[192,768]{1,0:T(8,128)(2,1)S(1)}, bf16[192,768]{1,0:T(8,128)(2,1)S(1)}, u32[]{:S(2)}, u32[]{:S(2)}) collective-permute-start(bf16[192,768]{1,0:T(8,128)(2,1)S(1)} %bitcast.8), channel_id=1, source_target_pairs={{0,24},{8,0},{16,8},{24,16},{1,25},{9,1},{17,9},{25,17},{2,26},{10... | collective-permute-start | bytes 884744 | tf_op jit(solution)/shard_map/ppermute | solution.py:49
  46.8 1.6 %collective-permute-done.13.refs_1_ = bf16[192,768]{1,0:T(8,128)(2,1)S(1)} collective-permute-done((bf16[192,768]{1,0:T(8,128)(2,1)S(1)}, bf16[192,768]{1,0:T(8,128)(2,1)S(1)}, u32[]{:S(2)}, u32[]{:S(2)}) %collective-permute-start.13) | collective-permute-done | bytes 294944 | tf_op jit(solution)/shard_map/ppermute | solution.py:49
  48.4 4.1 %collective-permute-done.15.refs_3_ = bf16[192,768]{1,0:T(8,128)(2,1)S(1)} collective-permute-done((bf16[192,768]{1,0:T(8,128)(2,1)S(1)}, bf16[192,768]{1,0:T(8,128)(2,1)S(1)}, u32[]{:S(2)}, u32[]{:S(2)}) %collective-permute-start.15) | collective-permute-done | bytes 294944 | tf_op jit(solution)/shard_map/ppermute | solution.py:49
  52.5 10.3 %shard_map.81 = (f32[192,768]{1,0:T(8,128)S(1)}, bf16[192,768]{1,0:T(8,128)(2,1)S(1)}, bf16[192,768]{1,0:T(8,128)(2,1)S(1)}, bf16[192,768]{1,0:T(8,128)(2,1)S(1)}) custom-call(bf16[3,768,768]{2,1,0:T(8,128)(2,1)} %bitcast.20, bf16[3,768,768]{2,1,0:T(8,128)(2,1)} %bitcast.22, bf16[192,768]{1,0:T(8,128)(2,1)S(1)} %bitcast.18, ...), custom_call_target="tpu_custom_call" | custom-call | flops 5435817984 | bytes 1048576 | tf_op jit(solution)/shard_map/pallas_call | solution.py:301
  62.9 2.0 %collective-permute-start.17 = (bf16[192,768]{1,0:T(8,128)(2,1)S(1)}, bf16[192,768]{1,0:T(8,128)(2,1)S(1)}, u32[]{:S(2)}, u32[]{:S(2)}) collective-permute-start(bf16[192,768]{1,0:T(8,128)(2,1)S(1)} %get-tuple-element.22.refs_6_), channel_id=1, source_target_pairs={{0,16},{8,24},{16,0},{24,8},{1,17},{9,25},{17,1},{25,9},{2,18},{10... | collective-permute-start | bytes 884744 | tf_op jit(solution)/shard_map/ppermute | solution.py:54
  64.9 1.7 %collective-permute-start.18 = (bf16[192,768]{1,0:T(8,128)(2,1)S(1)}, bf16[192,768]{1,0:T(8,128)(2,1)S(1)}, u32[]{:S(2)}, u32[]{:S(2)}) collective-permute-start(bf16[192,768]{1,0:T(8,128)(2,1)S(1)} %get-tuple-element.23.refs_7_), channel_id=1, source_target_pairs={{0,24},{8,0},{16,8},{24,16},{1,25},{9,1},{17,9},{25,17},{2,26},{10... | collective-permute-start | bytes 884744 | tf_op jit(solution)/shard_map/ppermute | solution.py:54
  67.3 2.1 %collective-permute-start.20 = (f32[8,128]{1,0:T(8,128)S(1)}, f32[8,128]{1,0:T(8,128)S(1)}, u32[]{:S(2)}, u32[]{:S(2)}) collective-permute-start(f32[8,128]{1,0:T(8,128)S(1)} %shard_map.82.refs_4_), channel_id=1, source_target_pairs={{0,16},{8,24},{16,0},{24,8},{1,17},{9,25},{17,1},{25,9},{2,18},{10... | collective-permute-start | bytes 12296 | tf_op jit(solution)/shard_map/ppermute | solution.py:54
  69.5 9.8 %collective-permute-done.19.refs_5_ = f32[8,128]{1,0:T(8,128)S(1)} collective-permute-done((f32[8,128]{1,0:T(8,128)S(1)}, f32[8,128]{1,0:T(8,128)S(1)}, u32[]{:S(2)}, u32[]{:S(2)}) %collective-permute-start.19) | collective-permute-done | bytes 4128 | tf_op jit(solution)/shard_map/ppermute | solution.py:54
  79.3 3.6 %collective-permute-done.21.refs_7_ = f32[8,128]{1,0:T(8,128)S(1)} collective-permute-done((f32[8,128]{1,0:T(8,128)S(1)}, f32[8,128]{1,0:T(8,128)S(1)}, u32[]{:S(2)}, u32[]{:S(2)}) %collective-permute-start.21) | collective-permute-done | bytes 4128 | tf_op jit(solution)/shard_map/ppermute | solution.py:54
  83.9 7.2 %all-to-all-start.3 = ((f32[8,152,128]{2,1,0:T(8,128)}), f32[8,152,128]{2,1,0:T(8,128)S(1)}, u32[]{:S(2)}, u32[]{:S(2)}) async-start(f32[8,152,128]{2,1,0:T(8,128)} %shard_map.83), calls=%async_computation.3 | async-start | bytes 1245184 | tf_op jit(solution)/shard_map/all_to_all | solution.py:317
  91.1 10.2 %shard_map.79 = (f32[192,768]{1,0:T(8,128)S(1)}, bf16[192,768]{1,0:T(8,128)(2,1)S(1)}, bf16[192,768]{1,0:T(8,128)(2,1)S(1)}, bf16[192,768]{1,0:T(8,128)(2,1)S(1)}) custom-call(bf16[3,768,768]{2,1,0:T(8,128)(2,1)} %bitcast.21, bf16[3,768,768]{2,1,0:T(8,128)(2,1)} %bitcast.23, bf16[192,768]{1,0:T(8,128)(2,1)S(1)} %bitcast.12, ...), custom_call_target="tpu_custom_call" | custom-call | flops 5435817984 | bytes 1048576 | tf_op jit(solution)/shard_map/pallas_call | solution.py:309
  101.4 2.7 %collective-permute-start.11 = (bf16[192,768]{1,0:T(8,128)(2,1)S(1)}, bf16[192,768]{1,0:T(8,128)(2,1)S(1)}, u32[]{:S(2)}, u32[]{:S(2)}) collective-permute-start(bf16[192,768]{1,0:T(8,128)(2,1)S(1)} %get-tuple-element.17), channel_id=1, source_target_pairs={{0,16},{8,24},{16,0},{24,8},{1,17},{9,25},{17,1},{25,9},{2,18},{10... | collective-permute-start | bytes 884744 | tf_op jit(solution)/shard_map/ppermute | solution.py:54
  104.6 10.7 %collective-permute-done.10.refs_1_ = bf16[192,768]{1,0:T(8,128)(2,1)S(1)} collective-permute-done((bf16[192,768]{1,0:T(8,128)(2,1)S(1)}, bf16[192,768]{1,0:T(8,128)(2,1)S(1)}, u32[]{:S(2)}, u32[]{:S(2)}) %collective-permute-start.10) | collective-permute-done | bytes 294944 | tf_op jit(solution)/shard_map/ppermute | solution.py:54
  116.6 7.2 %all-to-all-start.1 = ((f32[8,144,128]{2,1,0:T(8,128)}), f32[8,144,128]{2,1,0:T(8,128)S(1)}, u32[]{:S(2)}, u32[]{:S(2)}) async-start(f32[8,144,128]{2,1,0:T(8,128)} %shard_map.80), calls=%async_computation.1 | async-start | bytes 1179648 | tf_op jit(solution)/shard_map/all_to_all | solution.py:323
  125.3 3.2 %collective-permute-start.25 = (f32[152,128]{1,0:T(8,128)S(1)}, f32[152,128]{1,0:T(8,128)S(1)}, u32[]{:S(2)}, u32[]{:S(2)}) collective-permute-start(f32[152,128]{1,0:T(8,128)S(1)} %shard_map.84.refs_0_), channel_id=1, source_target_pairs={{0,128},{32,160},{64,192},{96,224},{128,0},{160,32},{192,64},{224,... | collective-permute-start | bytes 233480 | tf_op jit(solution)/shard_map/ppermute | solution.py:37
  128.5 2.8 %collective-permute-start.27 = (f32[152,128]{1,0:T(8,128)S(1)}, f32[152,128]{1,0:T(8,128)S(1)}, u32[]{:S(2)}, u32[]{:S(2)}) collective-permute-start(f32[152,128]{1,0:T(8,128)S(1)} %shard_map.84.refs_0_), channel_id=1, source_target_pairs={{0,192},{32,224},{64,0},{96,32},{128,64},{160,96},{192,128},{224,1... | collective-permute-start | bytes 233480 | tf_op jit(solution)/shard_map/ppermute | solution.py:37
  132.0 7.3 %all-to-all-done.1.direct_ref = f32[8,144,128]{2,1,0:T(8,128)S(1)} async-done(((f32[8,144,128]{2,1,0:T(8,128)}), f32[8,144,128]{2,1,0:T(8,128)S(1)}, u32[]{:S(2)}, u32[]{:S(2)}) %all-to-all-start.1) | async-done | bytes 589856 | tf_op jit(solution)/shard_map/all_to_all | solution.py:323
  (59 shorter events, 19.1 us)
Async XLA Ops:
  2.8 21.7 %all-to-all-start.2 = ((bf16[8,24,768]{2,1,0:T(8,128)(2,1)}), bf16[8,24,768]{2,1,0:T(8,128)(2,1)S(1)}, u32[]{:S(2)}, u32[]{:S(2)}) async-start(bf16[8,24,768]{2,1,0:T(8,128)(2,1)} %get-tuple-element.19), calls=%async_computation.2 | async-start | bytes 589824 | tf_op jit(solution)/shard_map/all_to_all | solution.py:278
  11.4 7.7 %collective-permute-start.1 = (bf16[24,768]{1,0:T(8,128)(2,1)S(1)}, bf16[24,768]{1,0:T(8,128)(2,1)S(1)}, u32[]{:S(2)}, u32[]{:S(2)}) collective-permute-start(bf16[24,768]{1,0:T(8,128)(2,1)S(1)} %get-tuple-element.14.live_ref), channel_id=1, source_target_pairs={{0,64},{32,96},{64,128},{96,160},{128,192},{160,224},{192,0},{224,... | collective-permute-start | bytes 110600 | tf_op jit(solution)/shard_map/ppermute | solution.py:37
  24.5 18.7 %all-to-all-start = ((bf16[8,24,768]{2,1,0:T(8,128)(2,1)}), bf16[8,24,768]{2,1,0:T(8,128)(2,1)S(1)}, u32[]{:S(2)}, u32[]{:S(2)}) async-start(bf16[8,24,768]{2,1,0:T(8,128)(2,1)} %shard_map.78), calls=%async_computation | async-start | bytes 589824 | tf_op jit(solution)/shard_map/all_to_all | solution.py:287
  31.7 16.7 %collective-permute-start.13 = (bf16[192,768]{1,0:T(8,128)(2,1)S(1)}, bf16[192,768]{1,0:T(8,128)(2,1)S(1)}, u32[]{:S(2)}, u32[]{:S(2)}) collective-permute-start(bf16[192,768]{1,0:T(8,128)(2,1)S(1)} %bitcast.15), channel_id=1, source_target_pairs={{0,24},{8,0},{16,8},{24,16},{1,25},{9,1},{17,9},{25,17},{2,26},{10... | collective-permute-start | bytes 884744 | tf_op jit(solution)/shard_map/ppermute | solution.py:49
  34.7 13.7 %collective-permute-start.14 = (bf16[192,768]{1,0:T(8,128)(2,1)S(1)}, bf16[192,768]{1,0:T(8,128)(2,1)S(1)}, u32[]{:S(2)}, u32[]{:S(2)}) collective-permute-start(bf16[192,768]{1,0:T(8,128)(2,1)S(1)} %bitcast.16), channel_id=1, source_target_pairs={{0,16},{8,24},{16,0},{24,8},{1,17},{9,25},{17,1},{25,9},{2,18},{10... | collective-permute-start | bytes 884744 | tf_op jit(solution)/shard_map/ppermute | solution.py:49
  35.3 17.2 %collective-permute-start.15 = (bf16[192,768]{1,0:T(8,128)(2,1)S(1)}, bf16[192,768]{1,0:T(8,128)(2,1)S(1)}, u32[]{:S(2)}, u32[]{:S(2)}) collective-permute-start(bf16[192,768]{1,0:T(8,128)(2,1)S(1)} %bitcast.17), channel_id=1, source_target_pairs={{0,8},{8,16},{16,24},{24,0},{1,9},{9,17},{17,25},{25,1},{2,10},{10... | collective-permute-start | bytes 884744 | tf_op jit(solution)/shard_map/ppermute | solution.py:49
  43.2 21.7 %collective-permute-start.7 = (bf16[192,768]{1,0:T(8,128)(2,1)S(1)}, bf16[192,768]{1,0:T(8,128)(2,1)S(1)}, u32[]{:S(2)}, u32[]{:S(2)}) collective-permute-start(bf16[192,768]{1,0:T(8,128)(2,1)S(1)} %bitcast.8), channel_id=1, source_target_pairs={{0,24},{8,0},{16,8},{24,16},{1,25},{9,1},{17,9},{25,17},{2,26},{10... | collective-permute-start | bytes 884744 | tf_op jit(solution)/shard_map/ppermute | solution.py:49
  46.2 20.4 %collective-permute-start.8 = (bf16[192,768]{1,0:T(8,128)(2,1)S(1)}, bf16[192,768]{1,0:T(8,128)(2,1)S(1)}, u32[]{:S(2)}, u32[]{:S(2)}) collective-permute-start(bf16[192,768]{1,0:T(8,128)(2,1)S(1)} %bitcast.9), channel_id=1, source_target_pairs={{0,16},{8,24},{16,0},{24,8},{1,17},{9,25},{17,1},{25,9},{2,18},{10... | collective-permute-start | bytes 884744 | tf_op jit(solution)/shard_map/ppermute | solution.py:49
  48.4 18.2 %collective-permute-start.9 = (bf16[192,768]{1,0:T(8,128)(2,1)S(1)}, bf16[192,768]{1,0:T(8,128)(2,1)S(1)}, u32[]{:S(2)}, u32[]{:S(2)}) collective-permute-start(bf16[192,768]{1,0:T(8,128)(2,1)S(1)} %bitcast.10), channel_id=1, source_target_pairs={{0,8},{8,16},{16,24},{24,0},{1,9},{9,17},{17,25},{25,1},{2,10},{10... | collective-permute-start | bytes 884744 | tf_op jit(solution)/shard_map/ppermute | solution.py:49
  62.8 20.1 %collective-permute-start.16 = (bf16[192,768]{1,0:T(8,128)(2,1)S(1)}, bf16[192,768]{1,0:T(8,128)(2,1)S(1)}, u32[]{:S(2)}, u32[]{:S(2)}) collective-permute-start(bf16[192,768]{1,0:T(8,128)(2,1)S(1)} %get-tuple-element.21.refs_5_), channel_id=1, source_target_pairs={{0,8},{8,16},{16,24},{24,0},{1,9},{9,17},{17,25},{25,1},{2,10},{10... | collective-permute-start | bytes 884744 | tf_op jit(solution)/shard_map/ppermute | solution.py:54
  62.9 20.0 %collective-permute-start.17 = (bf16[192,768]{1,0:T(8,128)(2,1)S(1)}, bf16[192,768]{1,0:T(8,128)(2,1)S(1)}, u32[]{:S(2)}, u32[]{:S(2)}) collective-permute-start(bf16[192,768]{1,0:T(8,128)(2,1)S(1)} %get-tuple-element.22.refs_6_), channel_id=1, source_target_pairs={{0,16},{8,24},{16,0},{24,8},{1,17},{9,25},{17,1},{25,9},{2,18},{10... | collective-permute-start | bytes 884744 | tf_op jit(solution)/shard_map/ppermute | solution.py:54
  64.9 18.0 %collective-permute-start.18 = (bf16[192,768]{1,0:T(8,128)(2,1)S(1)}, bf16[192,768]{1,0:T(8,128)(2,1)S(1)}, u32[]{:S(2)}, u32[]{:S(2)}) collective-permute-start(bf16[192,768]{1,0:T(8,128)(2,1)S(1)} %get-tuple-element.23.refs_7_), channel_id=1, source_target_pairs={{0,24},{8,0},{16,8},{24,16},{1,25},{9,1},{17,9},{25,17},{2,26},{10... | collective-permute-start | bytes 884744 | tf_op jit(solution)/shard_map/ppermute | solution.py:54
  66.9 12.3 %collective-permute-start.19 = (f32[8,128]{1,0:T(8,128)S(1)}, f32[8,128]{1,0:T(8,128)S(1)}, u32[]{:S(2)}, u32[]{:S(2)}) collective-permute-start(f32[8,128]{1,0:T(8,128)S(1)} %shard_map.82.refs_4_), channel_id=1, source_target_pairs={{0,8},{8,16},{16,24},{24,0},{1,9},{9,17},{17,25},{25,1},{2,10},{10... | collective-permute-start | bytes 12296 | tf_op jit(solution)/shard_map/ppermute | solution.py:54
  67.3 11.9 %collective-permute-start.20 = (f32[8,128]{1,0:T(8,128)S(1)}, f32[8,128]{1,0:T(8,128)S(1)}, u32[]{:S(2)}, u32[]{:S(2)}) collective-permute-start(f32[8,128]{1,0:T(8,128)S(1)} %shard_map.82.refs_4_), channel_id=1, source_target_pairs={{0,16},{8,24},{16,0},{24,8},{1,17},{9,25},{17,1},{25,9},{2,18},{10... | collective-permute-start | bytes 12296 | tf_op jit(solution)/shard_map/ppermute | solution.py:54
  83.9 32.8 %all-to-all-start.3 = ((f32[8,152,128]{2,1,0:T(8,128)}), f32[8,152,128]{2,1,0:T(8,128)S(1)}, u32[]{:S(2)}, u32[]{:S(2)}) async-start(f32[8,152,128]{2,1,0:T(8,128)} %shard_map.83), calls=%async_computation.3 | async-start | bytes 1245184 | tf_op jit(solution)/shard_map/all_to_all | solution.py:317
  101.3 14.0 %collective-permute-start.10 = (bf16[192,768]{1,0:T(8,128)(2,1)S(1)}, bf16[192,768]{1,0:T(8,128)(2,1)S(1)}, u32[]{:S(2)}, u32[]{:S(2)}) collective-permute-start(bf16[192,768]{1,0:T(8,128)(2,1)S(1)} %get-tuple-element.16), channel_id=1, source_target_pairs={{0,8},{8,16},{16,24},{24,0},{1,9},{9,17},{17,25},{25,1},{2,10},{10... | collective-permute-start | bytes 884744 | tf_op jit(solution)/shard_map/ppermute | solution.py:54
  101.4 13.9 %collective-permute-start.11 = (bf16[192,768]{1,0:T(8,128)(2,1)S(1)}, bf16[192,768]{1,0:T(8,128)(2,1)S(1)}, u32[]{:S(2)}, u32[]{:S(2)}) collective-permute-start(bf16[192,768]{1,0:T(8,128)(2,1)S(1)} %get-tuple-element.17), channel_id=1, source_target_pairs={{0,16},{8,24},{16,0},{24,8},{1,17},{9,25},{17,1},{25,9},{2,18},{10... | collective-permute-start | bytes 884744 | tf_op jit(solution)/shard_map/ppermute | solution.py:54
  104.1 11.6 %collective-permute-start.12 = (bf16[192,768]{1,0:T(8,128)(2,1)S(1)}, bf16[192,768]{1,0:T(8,128)(2,1)S(1)}, u32[]{:S(2)}, u32[]{:S(2)}) collective-permute-start(bf16[192,768]{1,0:T(8,128)(2,1)S(1)} %get-tuple-element.18), channel_id=1, source_target_pairs={{0,24},{8,0},{16,8},{24,16},{1,25},{9,1},{17,9},{25,17},{2,26},{10... | collective-permute-start | bytes 884744 | tf_op jit(solution)/shard_map/ppermute | solution.py:54
  116.6 22.7 %all-to-all-start.1 = ((f32[8,144,128]{2,1,0:T(8,128)}), f32[8,144,128]{2,1,0:T(8,128)S(1)}, u32[]{:S(2)}, u32[]{:S(2)}) async-start(f32[8,144,128]{2,1,0:T(8,128)} %shard_map.80), calls=%async_computation.1 | async-start | bytes 1179648 | tf_op jit(solution)/shard_map/all_to_all | solution.py:323
  125.1 14.2 %collective-permute-start.24 = (f32[152,128]{1,0:T(8,128)S(1)}, f32[152,128]{1,0:T(8,128)S(1)}, u32[]{:S(2)}, u32[]{:S(2)}) collective-permute-start(f32[152,128]{1,0:T(8,128)S(1)} %shard_map.84.refs_0_), channel_id=1, source_target_pairs={{0,96},{32,64},{64,160},{96,128},{128,224},{160,192},{192,32},{224... | collective-permute-start | bytes 233480 | tf_op jit(solution)/shard_map/ppermute | solution.py:37
  125.3 14.1 %collective-permute-start.25 = (f32[152,128]{1,0:T(8,128)S(1)}, f32[152,128]{1,0:T(8,128)S(1)}, u32[]{:S(2)}, u32[]{:S(2)}) collective-permute-start(f32[152,128]{1,0:T(8,128)S(1)} %shard_map.84.refs_0_), channel_id=1, source_target_pairs={{0,128},{32,160},{64,192},{96,224},{128,0},{160,32},{192,64},{224,... | collective-permute-start | bytes 233480 | tf_op jit(solution)/shard_map/ppermute | solution.py:37
  128.5 10.9 %collective-permute-start.26 = (f32[152,128]{1,0:T(8,128)S(1)}, f32[152,128]{1,0:T(8,128)S(1)}, u32[]{:S(2)}, u32[]{:S(2)}) collective-permute-start(f32[152,128]{1,0:T(8,128)S(1)} %shard_map.84.refs_0_), channel_id=1, source_target_pairs={{0,160},{32,128},{64,224},{96,192},{128,32},{160,0},{192,96},{224,... | collective-permute-start | bytes 233480 | tf_op jit(solution)/shard_map/ppermute | solution.py:37
  128.5 10.9 %collective-permute-start.27 = (f32[152,128]{1,0:T(8,128)S(1)}, f32[152,128]{1,0:T(8,128)S(1)}, u32[]{:S(2)}, u32[]{:S(2)}) collective-permute-start(f32[152,128]{1,0:T(8,128)S(1)} %shard_map.84.refs_0_), channel_id=1, source_target_pairs={{0,192},{32,224},{64,0},{96,32},{128,64},{160,96},{192,128},{224,1... | collective-permute-start | bytes 233480 | tf_op jit(solution)/shard_map/ppermute | solution.py:37
  131.3 8.0 %collective-permute-start.28 = (f32[152,128]{1,0:T(8,128)S(1)}, f32[152,128]{1,0:T(8,128)S(1)}, u32[]{:S(2)}, u32[]{:S(2)}) collective-permute-start(f32[152,128]{1,0:T(8,128)S(1)} %shard_map.84.refs_0_), channel_id=1, source_target_pairs={{0,224},{32,192},{64,32},{96,0},{128,96},{160,64},{192,160},{224,1... | collective-permute-start | bytes 233480 | tf_op jit(solution)/shard_map/ppermute | solution.py:37
  (13 other events, 99.8 us)

commit v2 on v1

--- a/solution.py
+++ b/solution.py
@@ -59,6 +59,14 @@
     for n, value in enumerate(values, 1):
         moved.append(move(value, n))
     return moved
+
+
+def three_parts(total):
+    high = total.astype(bf16)
+    rest = total - high.astype(f32)
+    middle = rest.astype(bf16)
+    low = (rest - middle.astype(f32)).astype(bf16)
+    return high, middle, low
 
 
 def live_kernel(size_ref, wave_ref, live_ref, copies_ref):
@@ -156,7 +164,7 @@
 
 
 def sums_kernel(count, live_ref, diagonal_ref, *refs):
-    x_refs, adjoint_refs, sums_ref = refs[:count], refs[count : 2 * count], refs[2 * count]
+    x_refs, adjoint_refs, outs = refs[:count], refs[count : 2 * count], refs[2 * count :]
     wave = live_ref[...].astype(f32)
     square = wave * wave
     norm = jnp.sum(square, axis=0, keepdims=True)
@@ -166,11 +174,22 @@
         mixed += 2.0 * jnp.sum(pair, axis=0, keepdims=True)
     mixed = jnp.sum(mixed, axis=1, keepdims=True)
     norm = jnp.sum(norm, axis=1, keepdims=True)
+    sums_ref, sent_refs = outs[0], outs[1:]
     tile = sums_ref.shape
     row = lax.broadcasted_iota(jnp.int32, tile, 0)
     sums_ref[...] = jnp.where(
         row == 0, jnp.broadcast_to(mixed, tile), jnp.broadcast_to(norm, tile)
     )
+    rows, width = adjoint_refs[1].shape
+    tail = (sent_refs[0].shape[0] - rows, width)
+    row = lax.broadcasted_iota(jnp.int32, tail, 0)
+    extra = jnp.zeros(tail, f32)
+    for place, part in enumerate(three_parts(mixed) + three_parts(norm)):
+        extra = jnp.where(row == place, jnp.broadcast_to(part.astype(f32), tail), extra)
+    extra = extra.astype(bf16)
+    for adjoint_ref, sent_ref in zip(adjoint_refs[1:], sent_refs):
+        sent_ref[:rows, :] = adjoint_ref[...]
+        sent_ref[rows:, :] = extra
 
 
 def tiles_of(rows, width):
@@ -193,11 +212,16 @@
                     z * each + r : z * each + r + 8, c : c + 128
                 ]
     if sums_refs:
-        total = sums_refs[0][...]
-        for ref in sums_refs[1:]:
-            total += ref[...]
+        tile = sums_refs[0][...]
+        mixed, norm = tile[0:1, :], tile[1:2, :]
+        for ref in blocks[1:]:
+            extra = ref[rows:, 0:128].astype(f32)
+            mixed += extra[0:1] + extra[1:2] + extra[2:3]
+            norm += extra[3:4] + extra[4:5] + extra[5:6]
+        row = lax.broadcasted_iota(jnp.int32, tile.shape, 0)
+        whole = jnp.where(row == 0, mixed, norm)
         for z in range(peers):
-            out_ref[z, out_ref.shape[1] - 8 :, :] = total
+            out_ref[z, out_ref.shape[1] - 8 :, :] = whole
 
 
 def meet_kernel(got_ref, out_ref):
@@ -301,19 +325,21 @@
     adjoint = run(
         functools.partial(adjoint_kernel, lines), outs, specs, scratch, flops, limit=50
     )(left, right, *own_parts)
-    adjoint_got = along_y(to_ahead, adjoint[1:])
-    sums = run(
-        functools.partial(sums_kernel, lines), shape(8, 128), [VMEM] * (2 + 2 * lines)
+    longer = shape(block + 16, width, dtype=bf16)
+    sums, *sent = run(
+        functools.partial(sums_kernel, lines),
+        [shape(8, 128)] + [longer] * (lines - 1),
+        [VMEM] * (2 + 2 * lines),
     )(live, diag, *their_parts, *adjoint)
-    sums_got = along_y(to_ahead, [sums] * (lines - 1))
+    adjoint_got = along_y(to_ahead, sent)
     direct = run(
         functools.partial(direct_kernel, lines), outs, specs, scratch, flops, limit=50
     )(left, right, *their_parts)
     direct_got = along_y(to_ahead, direct[1:])
 
     adjoint_lines = run(
-        functools.partial(rows_kernel, lines), shape(peers, length + 8, 128), [VMEM] * (2 * lines)
-    )(adjoint[0], *adjoint_got, sums, *sums_got)
+        functools.partial(rows_kernel, lines), shape(peers, length + 8, 128), [VMEM] * (lines + 1)
+    )(adjoint[0], *adjoint_got, sums)
     adjoint_lines = lax.all_to_all(adjoint_lines, Z, 0, 0, tiled=True)
     adjoint_mine = run(meet_kernel, shape(length + 8, 128), [VMEM])(adjoint_lines)
     routed = [adjoint_mine] + [from_sector(adjoint_mine, step) for step in steps]

time: 143 us -> 145 us (1.014)
  waiting for transfers between devices: 47.3 us -> 51.3 us
  starting transfers between devices: 64.3 us -> 61.9 us
    ppermute x9 -> x6, waiting for transfers between devices: 24.4 us -> 27.2 us  [to_ahead(): lax.ppermute(value, Y, [(i, (i + steps) % peers) for i in range(peers)])]
    ppermute x9 -> x6, starting transfers between devices: 9.66 us -> 7.21 us  [to_ahead(): lax.ppermute(value, Y, [(i, (i + steps) % peers) for i in range(peers)])]
  transfers between devices with their start and end apart: 33 -> 30, of which waited for: 12 -> 13; matrix products, arithmetic and copies ran while one was open for 0% -> 0% of each run, Pallas kernels for 16% -> 16%
where the time goes in v2:
time: 145 us; the launch traced here: 142 us
  starting transfers between devices  61.9 us (43%)
  waiting for transfers between devices  51.3 us (35%)
  Pallas kernels  26.3 us (18%)
    ppermute x6, waiting for transfers between devices, to_ahead(): lax.ppermute(value, Y, [(i, (i + steps) % peers) for i in range(peers)])  27.2 us
    ppermute x14, starting transfers between devices, from_sector(): return lax.ppermute(value, SEC, pairs)  16.2 us
    pallas_call x1, Pallas kernels, per_device(): run(functools.partial(adjoint_kernel, lines), outs, specs, scratch, flops...  10.3 us
    pallas_call x1, Pallas kernels, per_device(): run(functools.partial(direct_kernel, lines), outs, specs, scratch, flops,...  10.2 us
    all_to_all x1, starting transfers between devices, per_device(): own = lax.all_to_all(copies, Z, 0, 0, tiled=True).reshape(block, width)  8.57 us
    ppermute x6, starting transfers between devices, from_ahead(): lax.ppermute(value, Y, [(i, (i - steps) % peers) for i in range(peers)])  8.26 us
    all_to_all x1, waiting for transfers between devices, per_device(): direct_mine = lax.all_to_all(direct_lines, Z, 0, 0, tiled=True)  7.9 us
    ppermute x6, starting transfers between devices, to_ahead(): lax.ppermute(value, Y, [(i, (i + steps) % peers) for i in range(peers)])  7.21 us
  transfers between devices with their start and end apart: 30, of which 13 were waited for; matrix products, arithmetic and copies ran while one was open for 0% of the time, Pallas kernels for 16%

profile of v2, /device:TPU:32, one launch (start us, length us, event | category | flops | bytes accessed | tf_op | source)
XLA Modules:
  0.0 142.3 jit_solution(10487492123176661448)
XLA Ops:
  2.8 8.6 %all-to-all-start.2 = ((bf16[8,24,768]{2,1,0:T(8,128)(2,1)}), bf16[8,24,768]{2,1,0:T(8,128)(2,1)S(1)}, u32[]{:S(2)}, u32[]{:S(2)}) async-start(bf16[8,24,768]{2,1,0:T(8,128)(2,1)} %get-tuple-element.23), calls=%async_computation.2 | async-start | bytes 589824 | tf_op jit(solution)/shard_map/all_to_all | solution.py:302
  11.4 1.5 %collective-permute-start.1 = (bf16[24,768]{1,0:T(8,128)(2,1)S(1)}, bf16[24,768]{1,0:T(8,128)(2,1)S(1)}, u32[]{:S(2)}, u32[]{:S(2)}) collective-permute-start(bf16[24,768]{1,0:T(8,128)(2,1)S(1)} %get-tuple-element.18.live_ref), channel_id=1, source_target_pairs={{0,64},{32,96},{64,128},{96,160},{128,192},{160,224},{192,0},{224,... | collective-permute-start | bytes 110600 | tf_op jit(solution)/shard_map/ppermute | solution.py:37
  14.2 1.7 %collective-permute-start.3 = (bf16[24,768]{1,0:T(8,128)(2,1)S(1)}, bf16[24,768]{1,0:T(8,128)(2,1)S(1)}, u32[]{:S(2)}, u32[]{:S(2)}) collective-permute-start(bf16[24,768]{1,0:T(8,128)(2,1)S(1)} %get-tuple-element.18.live_ref), channel_id=1, source_target_pairs={{0,128},{32,160},{64,192},{96,224},{128,0},{160,32},{192,64},{224,... | collective-permute-start | bytes 110600 | tf_op jit(solution)/shard_map/ppermute | solution.py:37
  15.9 1.4 collective-permute-start.4
  17.3 1.7 %collective-permute-start.5 = (bf16[24,768]{1,0:T(8,128)(2,1)S(1)}, bf16[24,768]{1,0:T(8,128)(2,1)S(1)}, u32[]{:S(2)}, u32[]{:S(2)}) collective-permute-start(bf16[24,768]{1,0:T(8,128)(2,1)S(1)} %get-tuple-element.18.live_ref), channel_id=1, source_target_pairs={{0,192},{32,224},{64,0},{96,32},{128,64},{160,96},{192,128},{224,1... | collective-permute-start | bytes 110600 | tf_op jit(solution)/shard_map/ppermute | solution.py:37
  24.5 7.2 %all-to-all-start = ((bf16[8,24,768]{2,1,0:T(8,128)(2,1)}), bf16[8,24,768]{2,1,0:T(8,128)(2,1)S(1)}, u32[]{:S(2)}, u32[]{:S(2)}) async-start(bf16[8,24,768]{2,1,0:T(8,128)(2,1)} %shard_map.78), calls=%async_computation | async-start | bytes 589824 | tf_op jit(solution)/shard_map/all_to_all | solution.py:311
  31.7 3.0 %collective-permute-start.13 = (bf16[192,768]{1,0:T(8,128)(2,1)S(1)}, bf16[192,768]{1,0:T(8,128)(2,1)S(1)}, u32[]{:S(2)}, u32[]{:S(2)}) collective-permute-start(bf16[192,768]{1,0:T(8,128)(2,1)S(1)} %bitcast.15), channel_id=1, source_target_pairs={{0,24},{8,0},{16,8},{24,16},{1,25},{9,1},{17,9},{25,17},{2,26},{10... | collective-permute-start | bytes 884744 | tf_op jit(solution)/shard_map/ppermute | solution.py:49
  36.3 6.9 %all-to-all-done = bf16[8,24,768]{2,1,0:T(8,128)(2,1)S(1)} async-done(((bf16[8,24,768]{2,1,0:T(8,128)(2,1)}), bf16[8,24,768]{2,1,0:T(8,128)(2,1)S(1)}, u32[]{:S(2)}, u32[]{:S(2)}) %all-to-all-start) | async-done | bytes 294944 | tf_op jit(solution)/shard_map/all_to_all | solution.py:311
  43.2 3.0 %collective-permute-start.7 = (bf16[192,768]{1,0:T(8,128)(2,1)S(1)}, bf16[192,768]{1,0:T(8,128)(2,1)S(1)}, u32[]{:S(2)}, u32[]{:S(2)}) collective-permute-start(bf16[192,768]{1,0:T(8,128)(2,1)S(1)} %bitcast.8), channel_id=1, source_target_pairs={{0,24},{8,0},{16,8},{24,16},{1,25},{9,1},{17,9},{25,17},{2,26},{10... | collective-permute-start | bytes 884744 | tf_op jit(solution)/shard_map/ppermute | solution.py:49
  46.8 1.6 %collective-permute-done.13.refs_1_ = bf16[192,768]{1,0:T(8,128)(2,1)S(1)} collective-permute-done((bf16[192,768]{1,0:T(8,128)(2,1)S(1)}, bf16[192,768]{1,0:T(8,128)(2,1)S(1)}, u32[]{:S(2)}, u32[]{:S(2)}) %collective-permute-start.13) | collective-permute-done | bytes 294944 | tf_op jit(solution)/shard_map/ppermute | solution.py:49
  48.4 4.1 %collective-permute-done.15.refs_3_ = bf16[192,768]{1,0:T(8,128)(2,1)S(1)} collective-permute-done((bf16[192,768]{1,0:T(8,128)(2,1)S(1)}, bf16[192,768]{1,0:T(8,128)(2,1)S(1)}, u32[]{:S(2)}, u32[]{:S(2)}) %collective-permute-start.15) | collective-permute-done | bytes 294944 | tf_op jit(solution)/shard_map/ppermute | solution.py:49
  52.5 10.3 %shard_map.81 = (f32[192,768]{1,0:T(8,128)S(1)}, bf16[192,768]{1,0:T(8,128)(2,1)S(1)}, bf16[192,768]{1,0:T(8,128)(2,1)S(1)}, bf16[192,768]{1,0:T(8,128)(2,1)S(1)}) custom-call(bf16[3,768,768]{2,1,0:T(8,128)(2,1)} %bitcast.20, bf16[3,768,768]{2,1,0:T(8,128)(2,1)} %bitcast.22, bf16[192,768]{1,0:T(8,128)(2,1)S(1)} %bitcast.18, ...), custom_call_target="tpu_custom_call" | custom-call | flops 5435817984 | bytes 1048576 | tf_op jit(solution)/shard_map/pallas_call | solution.py:325
  63.9 2.1 %collective-permute-start.17 = (bf16[208,768]{1,0:T(8,128)(2,1)S(1)}, bf16[208,768]{1,0:T(8,128)(2,1)S(1)}, u32[]{:S(2)}, u32[]{:S(2)}) collective-permute-start(bf16[208,768]{1,0:T(8,128)(2,1)S(1)} %get-tuple-element.29), channel_id=1, source_target_pairs={{0,16},{8,24},{16,0},{24,8},{1,17},{9,25},{17,1},{25,9},{2,18},{10... | collective-permute-start | bytes 958472 | tf_op jit(solution)/shard_map/ppermute | solution.py:54
  67.1 14.2 %collective-permute-done.16.refs_1_ = bf16[208,768]{1,0:T(8,128)(2,1)S(1)} collective-permute-done((bf16[208,768]{1,0:T(8,128)(2,1)S(1)}, bf16[208,768]{1,0:T(8,128)(2,1)S(1)}, u32[]{:S(2)}, u32[]{:S(2)}) %collective-permute-start.16) | collective-permute-done | bytes 319520 | tf_op jit(solution)/shard_map/ppermute | solution.py:54
  83.0 7.2 %all-to-all-start.3 = ((f32[8,152,128]{2,1,0:T(8,128)}), f32[8,152,128]{2,1,0:T(8,128)S(1)}, u32[]{:S(2)}, u32[]{:S(2)}) async-start(f32[8,152,128]{2,1,0:T(8,128)} %shard_map.83), calls=%async_computation.3 | async-start | bytes 1245184 | tf_op jit(solution)/shard_map/all_to_all | solution.py:343
  90.2 10.2 %shard_map.79 = (f32[192,768]{1,0:T(8,128)S(1)}, bf16[192,768]{1,0:T(8,128)(2,1)S(1)}, bf16[192,768]{1,0:T(8,128)(2,1)S(1)}, bf16[192,768]{1,0:T(8,128)(2,1)S(1)}) custom-call(bf16[3,768,768]{2,1,0:T(8,128)(2,1)} %bitcast.21, bf16[3,768,768]{2,1,0:T(8,128)(2,1)} %bitcast.23, bf16[192,768]{1,0:T(8,128)(2,1)S(1)} %bitcast.12, ...), custom_call_target="tpu_custom_call" | custom-call | flops 5435817984 | bytes 1048576 | tf_op jit(solution)/shard_map/pallas_call | solution.py:335
  100.7 3.6 %collective-permute-start.11 = (bf16[192,768]{1,0:T(8,128)(2,1)S(1)}, bf16[192,768]{1,0:T(8,128)(2,1)S(1)}, u32[]{:S(2)}, u32[]{:S(2)}) collective-permute-start(bf16[192,768]{1,0:T(8,128)(2,1)S(1)} %get-tuple-element.21), channel_id=1, source_target_pairs={{0,16},{8,24},{16,0},{24,8},{1,17},{9,25},{17,1},{25,9},{2,18},{10... | collective-permute-start | bytes 884744 | tf_op jit(solution)/shard_map/ppermute | solution.py:54
  104.3 5.5 %collective-permute-done.10.refs_1_ = bf16[192,768]{1,0:T(8,128)(2,1)S(1)} collective-permute-done((bf16[192,768]{1,0:T(8,128)(2,1)S(1)}, bf16[192,768]{1,0:T(8,128)(2,1)S(1)}, u32[]{:S(2)}, u32[]{:S(2)}) %collective-permute-start.10) | collective-permute-done | bytes 294944 | tf_op jit(solution)/shard_map/ppermute | solution.py:54
  109.8 6.9 %collective-permute-done.11.refs_2_ = bf16[192,768]{1,0:T(8,128)(2,1)S(1)} collective-permute-done((bf16[192,768]{1,0:T(8,128)(2,1)S(1)}, bf16[192,768]{1,0:T(8,128)(2,1)S(1)}, u32[]{:S(2)}, u32[]{:S(2)}) %collective-permute-start.11) | collective-permute-done | bytes 294944 | tf_op jit(solution)/shard_map/ppermute | solution.py:54
  117.6 7.2 %all-to-all-start.1 = ((f32[8,144,128]{2,1,0:T(8,128)}), f32[8,144,128]{2,1,0:T(8,128)S(1)}, u32[]{:S(2)}, u32[]{:S(2)}) async-start(f32[8,144,128]{2,1,0:T(8,128)} %shard_map.80), calls=%async_computation.1 | async-start | bytes 1179648 | tf_op jit(solution)/shard_map/all_to_all | solution.py:349
  126.3 3.2 %collective-permute-start.22 = (f32[152,128]{1,0:T(8,128)S(1)}, f32[152,128]{1,0:T(8,128)S(1)}, u32[]{:S(2)}, u32[]{:S(2)}) collective-permute-start(f32[152,128]{1,0:T(8,128)S(1)} %shard_map.84.refs_0_), channel_id=1, source_target_pairs={{0,128},{32,160},{64,192},{96,224},{128,0},{160,32},{192,64},{224,... | collective-permute-start | bytes 233480 | tf_op jit(solution)/shard_map/ppermute | solution.py:37
  129.5 2.7 %collective-permute-start.24 = (f32[152,128]{1,0:T(8,128)S(1)}, f32[152,128]{1,0:T(8,128)S(1)}, u32[]{:S(2)}, u32[]{:S(2)}) collective-permute-start(f32[152,128]{1,0:T(8,128)S(1)} %shard_map.84.refs_0_), channel_id=1, source_target_pairs={{0,192},{32,224},{64,0},{96,32},{128,64},{160,96},{192,128},{224,1... | collective-permute-start | bytes 233480 | tf_op jit(solution)/shard_map/ppermute | solution.py:37
  133.0 7.9 %all-to-all-done.1.direct_ref = f32[8,144,128]{2,1,0:T(8,128)S(1)} async-done(((f32[8,144,128]{2,1,0:T(8,128)}), f32[8,144,128]{2,1,0:T(8,128)S(1)}, u32[]{:S(2)}, u32[]{:S(2)}) %all-to-all-start.1) | async-done | bytes 589856 | tf_op jit(solution)/shard_map/all_to_all | solution.py:349
  141.0 1.4 shard_map.85
  (53 shorter events, 17.8 us)
Async XLA Ops:
  2.8 21.7 %all-to-all-start.2 = ((bf16[8,24,768]{2,1,0:T(8,128)(2,1)}), bf16[8,24,768]{2,1,0:T(8,128)(2,1)S(1)}, u32[]{:S(2)}, u32[]{:S(2)}) async-start(bf16[8,24,768]{2,1,0:T(8,128)(2,1)} %get-tuple-element.23), calls=%async_computation.2 | async-start | bytes 589824 | tf_op jit(solution)/shard_map/all_to_all | solution.py:302
  11.4 7.7 %collective-permute-start.1 = (bf16[24,768]{1,0:T(8,128)(2,1)S(1)}, bf16[24,768]{1,0:T(8,128)(2,1)S(1)}, u32[]{:S(2)}, u32[]{:S(2)}) collective-permute-start(bf16[24,768]{1,0:T(8,128)(2,1)S(1)} %get-tuple-element.18.live_ref), channel_id=1, source_target_pairs={{0,64},{32,96},{64,128},{96,160},{128,192},{160,224},{192,0},{224,... | collective-permute-start | bytes 110600 | tf_op jit(solution)/shard_map/ppermute | solution.py:37
  12.8 6.6 %collective-permute-start.2 = (bf16[24,768]{1,0:T(8,128)(2,1)S(1)}, bf16[24,768]{1,0:T(8,128)(2,1)S(1)}, u32[]{:S(2)}, u32[]{:S(2)}) collective-permute-start(bf16[24,768]{1,0:T(8,128)(2,1)S(1)} %get-tuple-element.18.live_ref), channel_id=1, source_target_pairs={{0,96},{32,64},{64,160},{96,128},{128,224},{160,192},{192,32},{224... | collective-permute-start | bytes 110600 | tf_op jit(solution)/shard_map/ppermute | solution.py:37
  24.5 18.7 %all-to-all-start = ((bf16[8,24,768]{2,1,0:T(8,128)(2,1)}), bf16[8,24,768]{2,1,0:T(8,128)(2,1)S(1)}, u32[]{:S(2)}, u32[]{:S(2)}) async-start(bf16[8,24,768]{2,1,0:T(8,128)(2,1)} %shard_map.78), calls=%async_computation | async-start | bytes 589824 | tf_op jit(solution)/shard_map/all_to_all | solution.py:311
  31.7 16.7 %collective-permute-start.13 = (bf16[192,768]{1,0:T(8,128)(2,1)S(1)}, bf16[192,768]{1,0:T(8,128)(2,1)S(1)}, u32[]{:S(2)}, u32[]{:S(2)}) collective-permute-start(bf16[192,768]{1,0:T(8,128)(2,1)S(1)} %bitcast.15), channel_id=1, source_target_pairs={{0,24},{8,0},{16,8},{24,16},{1,25},{9,1},{17,9},{25,17},{2,26},{10... | collective-permute-start | bytes 884744 | tf_op jit(solution)/shard_map/ppermute | solution.py:49
  34.7 13.7 %collective-permute-start.14 = (bf16[192,768]{1,0:T(8,128)(2,1)S(1)}, bf16[192,768]{1,0:T(8,128)(2,1)S(1)}, u32[]{:S(2)}, u32[]{:S(2)}) collective-permute-start(bf16[192,768]{1,0:T(8,128)(2,1)S(1)} %bitcast.16), channel_id=1, source_target_pairs={{0,16},{8,24},{16,0},{24,8},{1,17},{9,25},{17,1},{25,9},{2,18},{10... | collective-permute-start | bytes 884744 | tf_op jit(solution)/shard_map/ppermute | solution.py:49
  35.3 17.2 %collective-permute-start.15 = (bf16[192,768]{1,0:T(8,128)(2,1)S(1)}, bf16[192,768]{1,0:T(8,128)(2,1)S(1)}, u32[]{:S(2)}, u32[]{:S(2)}) collective-permute-start(bf16[192,768]{1,0:T(8,128)(2,1)S(1)} %bitcast.17), channel_id=1, source_target_pairs={{0,8},{8,16},{16,24},{24,0},{1,9},{9,17},{17,25},{25,1},{2,10},{10... | collective-permute-start | bytes 884744 | tf_op jit(solution)/shard_map/ppermute | solution.py:49
  43.2 19.6 %collective-permute-start.7 = (bf16[192,768]{1,0:T(8,128)(2,1)S(1)}, bf16[192,768]{1,0:T(8,128)(2,1)S(1)}, u32[]{:S(2)}, u32[]{:S(2)}) collective-permute-start(bf16[192,768]{1,0:T(8,128)(2,1)S(1)} %bitcast.8), channel_id=1, source_target_pairs={{0,24},{8,0},{16,8},{24,16},{1,25},{9,1},{17,9},{25,17},{2,26},{10... | collective-permute-start | bytes 884744 | tf_op jit(solution)/shard_map/ppermute | solution.py:49
  46.2 16.6 %collective-permute-start.8 = (bf16[192,768]{1,0:T(8,128)(2,1)S(1)}, bf16[192,768]{1,0:T(8,128)(2,1)S(1)}, u32[]{:S(2)}, u32[]{:S(2)}) collective-permute-start(bf16[192,768]{1,0:T(8,128)(2,1)S(1)} %bitcast.9), channel_id=1, source_target_pairs={{0,16},{8,24},{16,0},{24,8},{1,17},{9,25},{17,1},{25,9},{2,18},{10... | collective-permute-start | bytes 884744 | tf_op jit(solution)/shard_map/ppermute | solution.py:49
  48.4 15.0 %collective-permute-start.9 = (bf16[192,768]{1,0:T(8,128)(2,1)S(1)}, bf16[192,768]{1,0:T(8,128)(2,1)S(1)}, u32[]{:S(2)}, u32[]{:S(2)}) collective-permute-start(bf16[192,768]{1,0:T(8,128)(2,1)S(1)} %bitcast.10), channel_id=1, source_target_pairs={{0,8},{8,16},{16,24},{24,0},{1,9},{9,17},{17,25},{25,1},{2,10},{10... | collective-permute-start | bytes 884744 | tf_op jit(solution)/shard_map/ppermute | solution.py:49
  63.8 17.5 %collective-permute-start.16 = (bf16[208,768]{1,0:T(8,128)(2,1)S(1)}, bf16[208,768]{1,0:T(8,128)(2,1)S(1)}, u32[]{:S(2)}, u32[]{:S(2)}) collective-permute-start(bf16[208,768]{1,0:T(8,128)(2,1)S(1)} %get-tuple-element.28), channel_id=1, source_target_pairs={{0,8},{8,16},{16,24},{24,0},{1,9},{9,17},{17,25},{25,1},{2,10},{10... | collective-permute-start | bytes 958472 | tf_op jit(solution)/shard_map/ppermute | solution.py:54
  63.9 17.5 %collective-permute-start.17 = (bf16[208,768]{1,0:T(8,128)(2,1)S(1)}, bf16[208,768]{1,0:T(8,128)(2,1)S(1)}, u32[]{:S(2)}, u32[]{:S(2)}) collective-permute-start(bf16[208,768]{1,0:T(8,128)(2,1)S(1)} %get-tuple-element.29), channel_id=1, source_target_pairs={{0,16},{8,24},{16,0},{24,8},{1,17},{9,25},{17,1},{25,9},{2,18},{10... | collective-permute-start | bytes 958472 | tf_op jit(solution)/shard_map/ppermute | solution.py:54
  66.0 16.0 %collective-permute-start.18 = (bf16[208,768]{1,0:T(8,128)(2,1)S(1)}, bf16[208,768]{1,0:T(8,128)(2,1)S(1)}, u32[]{:S(2)}, u32[]{:S(2)}) collective-permute-start(bf16[208,768]{1,0:T(8,128)(2,1)S(1)} %get-tuple-element.30), channel_id=1, source_target_pairs={{0,24},{8,0},{16,8},{24,16},{1,25},{9,1},{17,9},{25,17},{2,26},{10... | collective-permute-start | bytes 958472 | tf_op jit(solution)/shard_map/ppermute | solution.py:54
  83.0 34.7 %all-to-all-start.3 = ((f32[8,152,128]{2,1,0:T(8,128)}), f32[8,152,128]{2,1,0:T(8,128)S(1)}, u32[]{:S(2)}, u32[]{:S(2)}) async-start(f32[8,152,128]{2,1,0:T(8,128)} %shard_map.83), calls=%async_computation.3 | async-start | bytes 1245184 | tf_op jit(solution)/shard_map/all_to_all | solution.py:343
  100.4 9.4 %collective-permute-start.10 = (bf16[192,768]{1,0:T(8,128)(2,1)S(1)}, bf16[192,768]{1,0:T(8,128)(2,1)S(1)}, u32[]{:S(2)}, u32[]{:S(2)}) collective-permute-start(bf16[192,768]{1,0:T(8,128)(2,1)S(1)} %get-tuple-element.20), channel_id=1, source_target_pairs={{0,8},{8,16},{16,24},{24,0},{1,9},{9,17},{17,25},{25,1},{2,10},{10... | collective-permute-start | bytes 884744 | tf_op jit(solution)/shard_map/ppermute | solution.py:54
  100.7 15.9 %collective-permute-start.11 = (bf16[192,768]{1,0:T(8,128)(2,1)S(1)}, bf16[192,768]{1,0:T(8,128)(2,1)S(1)}, u32[]{:S(2)}, u32[]{:S(2)}) collective-permute-start(bf16[192,768]{1,0:T(8,128)(2,1)S(1)} %get-tuple-element.21), channel_id=1, source_target_pairs={{0,16},{8,24},{16,0},{24,8},{1,17},{9,25},{17,1},{25,9},{2,18},{10... | collective-permute-start | bytes 884744 | tf_op jit(solution)/shard_map/ppermute | solution.py:54
  104.3 12.4 %collective-permute-start.12 = (bf16[192,768]{1,0:T(8,128)(2,1)S(1)}, bf16[192,768]{1,0:T(8,128)(2,1)S(1)}, u32[]{:S(2)}, u32[]{:S(2)}) collective-permute-start(bf16[192,768]{1,0:T(8,128)(2,1)S(1)} %get-tuple-element.22), channel_id=1, source_target_pairs={{0,24},{8,0},{16,8},{24,16},{1,25},{9,1},{17,9},{25,17},{2,26},{10... | collective-permute-start | bytes 884744 | tf_op jit(solution)/shard_map/ppermute | solution.py:54
  117.6 23.3 %all-to-all-start.1 = ((f32[8,144,128]{2,1,0:T(8,128)}), f32[8,144,128]{2,1,0:T(8,128)S(1)}, u32[]{:S(2)}, u32[]{:S(2)}) async-start(f32[8,144,128]{2,1,0:T(8,128)} %shard_map.80), calls=%async_computation.1 | async-start | bytes 1179648 | tf_op jit(solution)/shard_map/all_to_all | solution.py:349
  125.0 7.3 %collective-permute-start.20 = (f32[152,128]{1,0:T(8,128)S(1)}, f32[152,128]{1,0:T(8,128)S(1)}, u32[]{:S(2)}, u32[]{:S(2)}) collective-permute-start(f32[152,128]{1,0:T(8,128)S(1)} %shard_map.84.refs_0_), channel_id=1, source_target_pairs={{0,64},{32,96},{64,128},{96,160},{128,192},{160,224},{192,0},{224,... | collective-permute-start | bytes 233480 | tf_op jit(solution)/shard_map/ppermute | solution.py:37
  126.0 14.9 %collective-permute-start.21 = (f32[152,128]{1,0:T(8,128)S(1)}, f32[152,128]{1,0:T(8,128)S(1)}, u32[]{:S(2)}, u32[]{:S(2)}) collective-permute-start(f32[152,128]{1,0:T(8,128)S(1)} %shard_map.84.refs_0_), channel_id=1, source_target_pairs={{0,96},{32,64},{64,160},{96,128},{128,224},{160,192},{192,32},{224... | collective-permute-start | bytes 233480 | tf_op jit(solution)/shard_map/ppermute | solution.py:37
  126.3 14.7 %collective-permute-start.22 = (f32[152,128]{1,0:T(8,128)S(1)}, f32[152,128]{1,0:T(8,128)S(1)}, u32[]{:S(2)}, u32[]{:S(2)}) collective-permute-start(f32[152,128]{1,0:T(8,128)S(1)} %shard_map.84.refs_0_), channel_id=1, source_target_pairs={{0,128},{32,160},{64,192},{96,224},{128,0},{160,32},{192,64},{224,... | collective-permute-start | bytes 233480 | tf_op jit(solution)/shard_map/ppermute | solution.py:37
  129.5 11.4 %collective-permute-start.23 = (f32[152,128]{1,0:T(8,128)S(1)}, f32[152,128]{1,0:T(8,128)S(1)}, u32[]{:S(2)}, u32[]{:S(2)}) collective-permute-start(f32[152,128]{1,0:T(8,128)S(1)} %shard_map.84.refs_0_), channel_id=1, source_target_pairs={{0,160},{32,128},{64,224},{96,192},{128,32},{160,0},{192,96},{224,... | collective-permute-start | bytes 233480 | tf_op jit(solution)/shard_map/ppermute | solution.py:37
  129.5 11.4 %collective-permute-start.24 = (f32[152,128]{1,0:T(8,128)S(1)}, f32[152,128]{1,0:T(8,128)S(1)}, u32[]{:S(2)}, u32[]{:S(2)}) collective-permute-start(f32[152,128]{1,0:T(8,128)S(1)} %shard_map.84.refs_0_), channel_id=1, source_target_pairs={{0,192},{32,224},{64,0},{96,32},{128,64},{160,96},{192,128},{224,1... | collective-permute-start | bytes 233480 | tf_op jit(solution)/shard_map/ppermute | solution.py:37
  132.2 8.7 %collective-permute-start.25 = (f32[152,128]{1,0:T(8,128)S(1)}, f32[152,128]{1,0:T(8,128)S(1)}, u32[]{:S(2)}, u32[]{:S(2)}) collective-permute-start(f32[152,128]{1,0:T(8,128)S(1)} %shard_map.84.refs_0_), channel_id=1, source_target_pairs={{0,224},{32,192},{64,32},{96,0},{128,96},{160,64},{192,160},{224,1... | collective-permute-start | bytes 233480 | tf_op jit(solution)/shard_map/ppermute | solution.py:37
  (10 other events, 81.6 us)

commit v3 on v0

--- a/solution.py
+++ b/solution.py
@@ -61,7 +61,7 @@
     return moved
 
 
-def live_kernel(size_ref, wave_ref, live_ref, copies_ref):
+def live_kernel(steps, size_ref, partner_ref, wave_ref, live_ref, copies_ref, chosen_ref):
     rows, width = wave_ref.shape
     size = size_ref[0]
     row = lax.axis_index(OP) * rows + lax.broadcasted_iota(jnp.int32, (rows, width), 0)
@@ -71,49 +71,54 @@
     live_ref[...] = live
     for z in range(copies_ref.shape[0]):
         copies_ref[z] = live
-
-
-def choose_kernel(steps, partner_ref, live_ref, *refs):
+    me = lax.axis_index(SEC)
+    partner = partner_ref[me]
+    row = lax.broadcasted_iota(jnp.int32, chosen_ref.shape, 0)
+    chosen = jnp.zeros(chosen_ref.shape, f32)
+    for n, step in enumerate(steps):
+        sender = sector_behind(step)
+        gives = jnp.where(sender == partner, 1.0, 0.0)
+        takes = jnp.where(partner_ref[sender] == me, 1.0, 0.0)
+        chosen = jnp.where(row == n, gives, chosen)
+        chosen = jnp.where(row == len(steps) + n, takes, chosen)
+    chosen_ref[...] = chosen
+
+
+def choose_kernel(chosen_ref, *refs):
     got_refs, copies_ref = refs[:-1], refs[-1]
-    partner = partner_ref[lax.axis_index(SEC)]
-
-    def place(ref):
-        value = ref[...]
-        for z in range(copies_ref.shape[0]):
-            copies_ref[z] = value
-
-    @pl.when(partner == lax.axis_index(SEC))
-    def _():
-        place(live_ref)
-
-    for step, ref in zip(steps, got_refs):
-
-        @pl.when(partner == sector_behind(step))
-        def _(ref=ref):
-            place(ref)
+    chosen = chosen_ref[...]
+    value = None
+    for n, ref in enumerate(got_refs):
+        part = ref[...].astype(f32)
+        mark = jnp.broadcast_to(chosen[n : n + 1, 0:1], part.shape)
+        value = part if value is None else jnp.where(mark > 0.0, part, value)
+    value = value.astype(bf16)
+    for z in range(copies_ref.shape[0]):
+        copies_ref[z] = value
+
+
+def load_kernel(left_hbm, right_hbm, left_ref, right_ref, arrived):
+    copies = [
+        pltpu.make_async_copy(left_hbm, left_ref, arrived.at[0]),
+        pltpu.make_async_copy(right_hbm, right_ref, arrived.at[1]),
+    ]
+    for copy in copies:
+        copy.start()
+    for copy in copies:
+        copy.wait()
 
 
 def products(x_refs, operators, outs, scratch, first_dims, second_dims):
-    left_hbm, right_hbm = operators
-    x_all, half, left_ref, right_ref, arrived = scratch
+    left_ref, right_ref = operators
+    x_all, half = scratch
     count = len(x_refs)
     ahead = lax.axis_index(Y)
     rows = x_refs[0].shape[0]
     terms, width, _ = left_ref.shape
-    copies = [
-        pltpu.make_async_copy(hbm.at[k], ref.at[k], arrived.at[n, k])
-        for n, (hbm, ref) in enumerate(((left_hbm, left_ref), (right_hbm, right_ref)))
-        for k in range(terms)
-    ]
-    copies[0].start()
-    copies[1].start()
     for step, ref in enumerate(x_refs):
         place = pl.multiple_of(lax.rem(ahead + step, count) * rows, rows)
         x_all[pl.ds(place, rows), :] = ref[...]
     for k in range(terms):
-        copies[k].wait()
-        for later in copies[2 * k + 2 : 2 * k + 4]:
-            later.start()
         first = lax.dot_general(
             left_ref[k], x_all[...], first_dims, preferred_element_type=f32
         ).astype(bf16)
@@ -122,8 +127,6 @@
             half[pl.ds(place, rows), k * width : (k + 1) * width] = first[
                 block * rows : (block + 1) * rows
             ]
-    for copy in copies[terms:]:
-        copy.wait()
     if second_dims == NN:
         right = right_ref[...].reshape(terms * width, width)
         total = lax.dot_general(half[...], right, NN, preferred_element_type=f32)
@@ -141,15 +144,15 @@
         outs[step][...] = total[step * rows : (step + 1) * rows].astype(outs[step].dtype)
 
 
-def adjoint_kernel(count, left_hbm, right_hbm, *refs):
+def adjoint_kernel(count, left_ref, right_ref, *refs):
     products(
-        refs[:count], (left_hbm, right_hbm), refs[count : 2 * count], refs[2 * count :], TN, NN
-    )
-
-
-def direct_kernel(count, left_hbm, right_hbm, *refs):
+        refs[:count], (left_ref, right_ref), refs[count : 2 * count], refs[2 * count :], TN, NN
+    )
+
+
+def direct_kernel(count, left_ref, right_ref, *refs):
     products(
-        refs[:count], (left_hbm, right_hbm), refs[count : 2 * count], refs[2 * count :], NN, NT
+        refs[:count], (left_ref, right_ref), refs[count : 2 * count], refs[2 * count :], NN, NT
     )
 
 
@@ -205,22 +208,19 @@
     out_ref[...] = total
 
 
-def update_kernel(
-    steps, partner_ref, size_ref, direct_ref, diagonal_ref, live_ref, *refs
-):
+def update_kernel(size_ref, chosen_ref, direct_ref, diagonal_ref, live_ref, *refs):
     got_refs, (updated_ref, residual_ref, routed) = refs[:-3], refs[-3:]
     rows, width = live_ref.shape
     peers, length, _ = direct_ref.shape
-    me = lax.axis_index(SEC)
-    sums = None
-    for step, got_ref in zip([(0, 0)] + steps, got_refs):
-        part = got_ref[length:, :]
-        sums = part if sums is None else sums + part
-
-        @pl.when(partner_ref[sector_behind(step)] == me)
-        def _(got_ref=got_ref):
-            routed[...] = got_ref[:length, :]
-
+    chosen = chosen_ref[...]
+    value = sums = None
+    for n, got_ref in enumerate(got_refs):
+        part = got_ref[:length, :]
+        mark = jnp.broadcast_to(chosen[len(got_refs) + n : len(got_refs) + n + 1, :], part.shape)
+        value = part if value is None else jnp.where(mark > 0.0, part, value)
+        tile = got_ref[length:, :]
+        sums = tile if sums is None else sums + tile
+    routed[...] = value
     energy = sums[0:1, :] / sums[1:2, :]
     size = size_ref[0]
     base = lax.axis_index(OP) * rows
@@ -268,45 +268,53 @@
     def shape(*dims, dtype=f32):
         return jax.ShapeDtypeStruct(dims, dtype)
 
-    live, copies = run(
-        live_kernel,
-        [shape(rows, width, dtype=bf16), shape(peers, rows, width, dtype=bf16)],
-        [SMEM, VMEM],
-    )(sector_sizes, wavefunction[0])
+    every = [(0, 0)] + steps
+    live, copies, chosen = run(
+        functools.partial(live_kernel, every),
+        [
+            shape(rows, width, dtype=bf16),
+            shape(peers, rows, width, dtype=bf16),
+            shape(2 * len(every), 128),
+        ],
+        [SMEM, SMEM, VMEM],
+    )(sector_sizes, partner, wavefunction[0])
     own = lax.all_to_all(copies, Z, 0, 0, tiled=True).reshape(block, width)
     others = []
     for step in steps:
         others.append(from_sector(live, step))
     copies = run(
-        functools.partial(choose_kernel, steps),
-        shape(peers, rows, width, dtype=bf16),
-        [SMEM] + [VMEM] * (1 + len(steps)),
-    )(partner, live, *others)
+        choose_kernel, shape(peers, rows, width, dtype=bf16), [VMEM] * (1 + len(every))
+    )(chosen, live, *others)
     theirs = lax.all_to_all(copies, Z, 0, 0, tiled=True).reshape(block, width)
     own_parts = [own] + along_y(from_ahead, [own] * (lines - 1))
     their_parts = [theirs] + along_y(from_ahead, [theirs] * (lines - 1))
 
     flops = 4 * terms * width**3
-    scratch = [
-        pltpu.VMEM((width, width), bf16),
-        pltpu.VMEM((width, terms * width), bf16),
-        pltpu.VMEM((terms, width, width), bf16),
-        pltpu.VMEM((terms, width, width), bf16),
-        pltpu.SemaphoreType.DMA((2, terms)),
-    ]
+    scratch = [pltpu.VMEM((width, width), bf16), pltpu.VMEM((width, terms * width), bf16)]
+
+    def loaded():
+        return run(
+            load_kernel,
+            [shape(*left.shape, dtype=bf16), shape(*right.shape, dtype=bf16)],
+            [HBM, HBM],
+            [pltpu.SemaphoreType.DMA((2,))],
+            bytes_accessed=2 * (left.size + right.size),
+            limit=46,
+        )(left, right)
+
     outs = [shape(block, width)] + [shape(block, width, dtype=bf16)] * (lines - 1)
-    specs = [HBM, HBM] + [VMEM] * lines
+    specs = [VMEM] * (2 + lines)
     adjoint = run(
-        functools.partial(adjoint_kernel, lines), outs, specs, scratch, flops, limit=50
-    )(left, right, *own_parts)
+        functools.partial(adjoint_kernel, lines), outs, specs, scratch, flops, limit=44
+    )(*loaded(), *own_parts)
     adjoint_got = along_y(to_ahead, adjoint[1:])
     sums = run(
         functools.partial(sums_kernel, lines), shape(8, 128), [VMEM] * (2 + 2 * lines)
     )(live, diag, *their_parts, *adjoint)
     sums_got = along_y(to_ahead, [sums] * (lines - 1))
     direct = run(
-        functools.partial(direct_kernel, lines), outs, specs, scratch, flops, limit=50
-    )(left, right, *their_parts)
+        functools.partial(direct_kernel, lines), outs, specs, scratch, flops, limit=44
+    )(*loaded(), *their_parts)
     direct_got = along_y(to_ahead, direct[1:])
 
     adjoint_lines = run(
@@ -320,11 +328,11 @@
     )(direct[0], *direct_got)
     direct_mine = lax.all_to_all(direct_lines, Z, 0, 0, tiled=True)
     updated, residual = run(
-        functools.partial(update_kernel, steps),
+        update_kernel,
         [shape(rows, width)] * 2,
-        [SMEM, SMEM] + [VMEM] * (3 + len(routed)),
+        [SMEM] + [VMEM] * (4 + len(routed)),
         [pltpu.VMEM((length, 128), f32)],
-    )(partner, sector_sizes, direct_mine, diag, live, *routed)
+    )(sector_sizes, chosen, direct_mine, diag, live, *routed)
     return updated[None], residual[None]
 
 

time: 143 us -> 143 us (level)
  local copies, waits for them, and re-layouts: 1.43 us -> 13 us
  waiting for transfers between devices: 47.3 us -> 40.6 us
  Pallas kernels: 25.6 us -> 20.7 us
    unnamed x8 -> x18, local copies, waits for them, and re-layouts: 1.43 us -> 13 us
    all_to_all x1, waiting for transfers between devices: 6.9 us -> 0.25 us  [per_device(): theirs = lax.all_to_all(copies, Z, 0, 0, tiled=True).reshape(block, width)]
    pallas_call x1, Pallas kernels: 9.98 us -> 6.12 us  [per_device(): run(functools.partial(adjoint_kernel, lines), outs, specs, scratch, flops...]
    pallas_call x1, Pallas kernels: 9.9 us -> 6.24 us  [per_device(): run(functools.partial(direct_kernel, lines), outs, specs, scratch, flops,...]
    pallas_call x3 -> x4, Pallas kernels: 3.46 us -> 5.98 us  [the longest x1 3.1 us: loaded(): run(load_kernel, [shape(*left.shape, dtype=bf16), shape(*right.shape, dty...]
  transfers between devices with their start and end apart: 33 -> 33, of which waited for: 12 -> 12; matrix products, arithmetic and copies ran while one was open for 0% -> 0% of each run, Pallas kernels for 16% -> 13%
where the time goes in v3:
time: 143 us; the launch traced here: 140 us
  starting transfers between devices  64.4 us (45%)
  waiting for transfers between devices  40.6 us (28%)
  Pallas kernels  20.7 us (14%)
  local copies, waits for them, and re-layouts  13 us (9%)
    ppermute x9, waiting for transfers between devices, to_ahead(): lax.ppermute(value, Y, [(i, (i + steps) % peers) for i in range(peers)])  24.4 us
    ppermute x14, starting transfers between devices, from_sector(): return lax.ppermute(value, SEC, pairs)  16.2 us
    unnamed x18, local copies, waits for them, and re-layouts  13 us
    ppermute x9, starting transfers between devices, to_ahead(): lax.ppermute(value, Y, [(i, (i + steps) % peers) for i in range(peers)])  9.66 us
    all_to_all x1, starting transfers between devices, per_device(): own = lax.all_to_all(copies, Z, 0, 0, tiled=True).reshape(block, width)  8.57 us
    ppermute x6, starting transfers between devices, from_ahead(): lax.ppermute(value, Y, [(i, (i - steps) % peers) for i in range(peers)])  8.32 us
    all_to_all x1, waiting for transfers between devices, per_device(): direct_mine = lax.all_to_all(direct_lines, Z, 0, 0, tiled=True)  7.32 us
    all_to_all x1, starting transfers between devices, per_device(): adjoint_lines = lax.all_to_all(adjoint_lines, Z, 0, 0, tiled=True)  7.21 us
  transfers between devices with their start and end apart: 33, of which 12 were waited for; matrix products, arithmetic and copies ran while one was open for 0% of the time, Pallas kernels for 13%

profile of v3, /device:TPU:32, one launch (start us, length us, event | category | flops | bytes accessed | tf_op | source)
XLA Modules:
  0.0 140.1 jit_solution(16969578024580366721)
XLA Ops:
  4.0 8.6 %all-to-all-start.2 = ((bf16[8,24,768]{2,1,0:T(8,128)(2,1)}), bf16[8,24,768]{2,1,0:T(8,128)(2,1)S(1)}, u32[]{:S(2)}, u32[]{:S(2)}) async-start(bf16[8,24,768]{2,1,0:T(8,128)(2,1)} %get-tuple-element.25), calls=%async_computation.2 | async-start | bytes 589824 | tf_op jit(solution)/shard_map/all_to_all | solution.py:281
  24.5 7.2 %all-to-all-start = ((bf16[8,24,768]{2,1,0:T(8,128)(2,1)}), bf16[8,24,768]{2,1,0:T(8,128)(2,1)S(1)}, u32[]{:S(2)}, u32[]{:S(2)}) async-start(bf16[8,24,768]{2,1,0:T(8,128)(2,1)} %shard_map.79), calls=%async_computation | async-start | bytes 589824 | tf_op jit(solution)/shard_map/all_to_all | solution.py:288
  31.7 3.0 %collective-permute-start.13 = (bf16[192,768]{1,0:T(8,128)(2,1)S(1)}, bf16[192,768]{1,0:T(8,128)(2,1)S(1)}, u32[]{:S(2)}, u32[]{:S(2)}) collective-permute-start(bf16[192,768]{1,0:T(8,128)(2,1)S(1)} %bitcast.15), channel_id=1, source_target_pairs={{0,24},{8,0},{16,8},{24,16},{1,25},{9,1},{17,9},{25,17},{2,26},{10... | collective-permute-start | bytes 884744 | tf_op jit(solution)/shard_map/ppermute | solution.py:49
  36.3 3.1 %shard_map.78 = (bf16[3,768,768]{2,1,0:T(8,128)(2,1)S(1)}, bf16[3,768,768]{2,1,0:T(8,128)(2,1)S(1)}) custom-call(bf16[3,768,768]{2,1,0:T(8,128)(2,1)} %bitcast.20, bf16[3,768,768]{2,1,0:T(8,128)(2,1)} %bitcast.21), custom_call_target="tpu_custom_call" | custom-call | bytes 7077888 | tf_op jit(solution)/shard_map/pallas_call | solution.py:296
  41.2 1.8 %copy-done.6 = bf16[3,768,768]{2,1,0:T(8,128)(2,1)} copy-done((bf16[3,768,768]{2,1,0:T(8,128)(2,1)}, bf16[3,768,768]{2,1,0:T(8,128)(2,1)S(1)}, u32[]{:S(2)}) %copy-start.6) | copy-done | bytes 3538968
  43.2 3.0 %collective-permute-start.7 = (bf16[192,768]{1,0:T(8,128)(2,1)S(1)}, bf16[192,768]{1,0:T(8,128)(2,1)S(1)}, u32[]{:S(2)}, u32[]{:S(2)}) collective-permute-start(bf16[192,768]{1,0:T(8,128)(2,1)S(1)} %bitcast.8), channel_id=1, source_target_pairs={{0,24},{8,0},{16,8},{24,16},{1,25},{9,1},{17,9},{25,17},{2,26},{10... | collective-permute-start | bytes 884744 | tf_op jit(solution)/shard_map/ppermute | solution.py:49
  48.4 4.1 %collective-permute-done.15.refs_3_ = bf16[192,768]{1,0:T(8,128)(2,1)S(1)} collective-permute-done((bf16[192,768]{1,0:T(8,128)(2,1)S(1)}, bf16[192,768]{1,0:T(8,128)(2,1)S(1)}, u32[]{:S(2)}, u32[]{:S(2)}) %collective-permute-start.15) | collective-permute-done | bytes 294944 | tf_op jit(solution)/shard_map/ppermute | solution.py:49
  52.5 2.0 %copy-done.4 = bf16[3,768,768]{2,1,0:T(8,128)(2,1)S(1)} copy-done((bf16[3,768,768]{2,1,0:T(8,128)(2,1)S(1)}, bf16[3,768,768]{2,1,0:T(8,128)(2,1)}, u32[]{:S(2)}) %copy-start.4) | copy-done | bytes 3538968
  54.5 2.0 %copy-done.7 = bf16[3,768,768]{2,1,0:T(8,128)(2,1)S(1)} copy-done((bf16[3,768,768]{2,1,0:T(8,128)(2,1)S(1)}, bf16[3,768,768]{2,1,0:T(8,128)(2,1)}, u32[]{:S(2)}) %copy-start.7) | copy-done | bytes 3538968
  56.5 6.1 %shard_map.82 = (f32[192,768]{1,0:T(8,128)S(1)}, bf16[192,768]{1,0:T(8,128)(2,1)S(1)}, bf16[192,768]{1,0:T(8,128)(2,1)S(1)}, bf16[192,768]{1,0:T(8,128)(2,1)S(1)}) custom-call(bf16[3,768,768]{2,1,0:T(8,128)(2,1)S(1)} %copy-done.4, bf16[3,768,768]{2,1,0:T(8,128)(2,1)S(1)} %copy-done.7, bf16[192,768]{1,0:T(8,128)(2,1)S(1)} %bitcast.18, ...), custom_call_target="tpu_custom_call" | custom-call | flops 5435817984 | bytes 1048576 | tf_op jit(solution)/shard_map/pallas_call | solution.py:307
  62.7 1.9 %collective-permute-start.17 = (bf16[192,768]{1,0:T(8,128)(2,1)S(1)}, bf16[192,768]{1,0:T(8,128)(2,1)S(1)}, u32[]{:S(2)}, u32[]{:S(2)}) collective-permute-start(bf16[192,768]{1,0:T(8,128)(2,1)S(1)} %get-tuple-element.28.refs_6_), channel_id=1, source_target_pairs={{0,16},{8,24},{16,0},{24,8},{1,17},{9,25},{17,1},{25,9},{2,18},{10... | collective-permute-start | bytes 884744 | tf_op jit(solution)/shard_map/ppermute | solution.py:54
  67.2 2.1 %collective-permute-start.20 = (f32[8,128]{1,0:T(8,128)S(1)}, f32[8,128]{1,0:T(8,128)S(1)}, u32[]{:S(2)}, u32[]{:S(2)}) collective-permute-start(f32[8,128]{1,0:T(8,128)S(1)} %shard_map.83.refs_4_), channel_id=1, source_target_pairs={{0,16},{8,24},{16,0},{24,8},{1,17},{9,25},{17,1},{25,9},{2,18},{10... | collective-permute-start | bytes 12296 | tf_op jit(solution)/shard_map/ppermute | solution.py:54
  69.3 9.8 %collective-permute-done.19.refs_5_ = f32[8,128]{1,0:T(8,128)S(1)} collective-permute-done((f32[8,128]{1,0:T(8,128)S(1)}, f32[8,128]{1,0:T(8,128)S(1)}, u32[]{:S(2)}, u32[]{:S(2)}) %collective-permute-start.19) | collective-permute-done | bytes 4128 | tf_op jit(solution)/shard_map/ppermute | solution.py:54
  79.1 3.6 %collective-permute-done.21.refs_7_ = f32[8,128]{1,0:T(8,128)S(1)} collective-permute-done((f32[8,128]{1,0:T(8,128)S(1)}, f32[8,128]{1,0:T(8,128)S(1)}, u32[]{:S(2)}, u32[]{:S(2)}) %collective-permute-start.21) | collective-permute-done | bytes 4128 | tf_op jit(solution)/shard_map/ppermute | solution.py:54
  83.8 7.2 %all-to-all-start.3 = ((f32[8,152,128]{2,1,0:T(8,128)}), f32[8,152,128]{2,1,0:T(8,128)S(1)}, u32[]{:S(2)}, u32[]{:S(2)}) async-start(f32[8,152,128]{2,1,0:T(8,128)} %shard_map.84), calls=%async_computation.3 | async-start | bytes 1245184 | tf_op jit(solution)/shard_map/all_to_all | solution.py:323
  91.0 2.0 %copy-done.5 = bf16[3,768,768]{2,1,0:T(8,128)(2,1)S(1)} copy-done((bf16[3,768,768]{2,1,0:T(8,128)(2,1)S(1)}, bf16[3,768,768]{2,1,0:T(8,128)(2,1)}, u32[]{:S(2)}) %copy-start.5) | copy-done | bytes 3538968
  93.0 2.0 %copy-done.8 = bf16[3,768,768]{2,1,0:T(8,128)(2,1)S(1)} copy-done((bf16[3,768,768]{2,1,0:T(8,128)(2,1)S(1)}, bf16[3,768,768]{2,1,0:T(8,128)(2,1)}, u32[]{:S(2)}) %copy-start.8) | copy-done | bytes 3538968
  95.0 6.2 %shard_map.80 = (f32[192,768]{1,0:T(8,128)S(1)}, bf16[192,768]{1,0:T(8,128)(2,1)S(1)}, bf16[192,768]{1,0:T(8,128)(2,1)S(1)}, bf16[192,768]{1,0:T(8,128)(2,1)S(1)}) custom-call(bf16[3,768,768]{2,1,0:T(8,128)(2,1)S(1)} %copy-done.5, bf16[3,768,768]{2,1,0:T(8,128)(2,1)S(1)} %copy-done.8, bf16[192,768]{1,0:T(8,128)(2,1)S(1)} %bitcast.12, ...), custom_call_target="tpu_custom_call" | custom-call | flops 5435817984 | bytes 1048576 | tf_op jit(solution)/shard_map/pallas_call | solution.py:315
  101.3 2.7 %collective-permute-start.11 = (bf16[192,768]{1,0:T(8,128)(2,1)S(1)}, bf16[192,768]{1,0:T(8,128)(2,1)S(1)}, u32[]{:S(2)}, u32[]{:S(2)}) collective-permute-start(bf16[192,768]{1,0:T(8,128)(2,1)S(1)} %get-tuple-element.23), channel_id=1, source_target_pairs={{0,16},{8,24},{16,0},{24,8},{1,17},{9,25},{17,1},{25,9},{2,18},{10... | collective-permute-start | bytes 884744 | tf_op jit(solution)/shard_map/ppermute | solution.py:54
  104.5 10.7 %collective-permute-done.10.refs_1_ = bf16[192,768]{1,0:T(8,128)(2,1)S(1)} collective-permute-done((bf16[192,768]{1,0:T(8,128)(2,1)S(1)}, bf16[192,768]{1,0:T(8,128)(2,1)S(1)}, u32[]{:S(2)}, u32[]{:S(2)}) %collective-permute-start.10) | collective-permute-done | bytes 294944 | tf_op jit(solution)/shard_map/ppermute | solution.py:54
  116.5 7.2 %all-to-all-start.1 = ((f32[8,144,128]{2,1,0:T(8,128)}), f32[8,144,128]{2,1,0:T(8,128)S(1)}, u32[]{:S(2)}, u32[]{:S(2)}) async-start(f32[8,144,128]{2,1,0:T(8,128)} %shard_map.81), calls=%async_computation.1 | async-start | bytes 1179648 | tf_op jit(solution)/shard_map/all_to_all | solution.py:329
  125.2 3.2 %collective-permute-start.25 = (f32[152,128]{1,0:T(8,128)S(1)}, f32[152,128]{1,0:T(8,128)S(1)}, u32[]{:S(2)}, u32[]{:S(2)}) collective-permute-start(f32[152,128]{1,0:T(8,128)S(1)} %shard_map.85.refs_0_), channel_id=1, source_target_pairs={{0,128},{32,160},{64,192},{96,224},{128,0},{160,32},{192,64},{224,... | collective-permute-start | bytes 233480 | tf_op jit(solution)/shard_map/ppermute | solution.py:37
  128.4 2.8 %collective-permute-start.27 = (f32[152,128]{1,0:T(8,128)S(1)}, f32[152,128]{1,0:T(8,128)S(1)}, u32[]{:S(2)}, u32[]{:S(2)}) collective-permute-start(f32[152,128]{1,0:T(8,128)S(1)} %shard_map.85.refs_0_), channel_id=1, source_target_pairs={{0,192},{32,224},{64,0},{96,32},{128,64},{160,96},{192,128},{224,1... | collective-permute-start | bytes 233480 | tf_op jit(solution)/shard_map/ppermute | solution.py:37
  131.9 7.3 %all-to-all-done.1.direct_ref = f32[8,144,128]{2,1,0:T(8,128)S(1)} async-done(((f32[8,144,128]{2,1,0:T(8,128)}), f32[8,144,128]{2,1,0:T(8,128)S(1)}, u32[]{:S(2)}, u32[]{:S(2)}) %all-to-all-start.1) | async-done | bytes 589856 | tf_op jit(solution)/shard_map/all_to_all | solution.py:329
  (70 shorter events, 28.9 us)
Async XLA Ops:
  4.0 20.5 %all-to-all-start.2 = ((bf16[8,24,768]{2,1,0:T(8,128)(2,1)}), bf16[8,24,768]{2,1,0:T(8,128)(2,1)S(1)}, u32[]{:S(2)}, u32[]{:S(2)}) async-start(bf16[8,24,768]{2,1,0:T(8,128)(2,1)} %get-tuple-element.25), calls=%async_computation.2 | async-start | bytes 589824 | tf_op jit(solution)/shard_map/all_to_all | solution.py:281
  12.6 7.7 %collective-permute-start.1 = (bf16[24,768]{1,0:T(8,128)(2,1)S(1)}, bf16[24,768]{1,0:T(8,128)(2,1)S(1)}, u32[]{:S(2)}, u32[]{:S(2)}) collective-permute-start(bf16[24,768]{1,0:T(8,128)(2,1)S(1)} %get-tuple-element.20.refs_0_.live_ref), channel_id=1, source_target_pairs={{0,64},{32,96},{64,128},{96,160},{128,192},{160,224},{192,0},{224,... | collective-permute-start | bytes 110600 | tf_op jit(solution)/shard_map/ppermute | solution.py:37
  24.5 18.7 %all-to-all-start = ((bf16[8,24,768]{2,1,0:T(8,128)(2,1)}), bf16[8,24,768]{2,1,0:T(8,128)(2,1)S(1)}, u32[]{:S(2)}, u32[]{:S(2)}) async-start(bf16[8,24,768]{2,1,0:T(8,128)(2,1)} %shard_map.79), calls=%async_computation | async-start | bytes 589824 | tf_op jit(solution)/shard_map/all_to_all | solution.py:288
  31.7 16.7 %collective-permute-start.13 = (bf16[192,768]{1,0:T(8,128)(2,1)S(1)}, bf16[192,768]{1,0:T(8,128)(2,1)S(1)}, u32[]{:S(2)}, u32[]{:S(2)}) collective-permute-start(bf16[192,768]{1,0:T(8,128)(2,1)S(1)} %bitcast.15), channel_id=1, source_target_pairs={{0,24},{8,0},{16,8},{24,16},{1,25},{9,1},{17,9},{25,17},{2,26},{10... | collective-permute-start | bytes 884744 | tf_op jit(solution)/shard_map/ppermute | solution.py:49
  34.7 13.7 %collective-permute-start.14 = (bf16[192,768]{1,0:T(8,128)(2,1)S(1)}, bf16[192,768]{1,0:T(8,128)(2,1)S(1)}, u32[]{:S(2)}, u32[]{:S(2)}) collective-permute-start(bf16[192,768]{1,0:T(8,128)(2,1)S(1)} %bitcast.16), channel_id=1, source_target_pairs={{0,16},{8,24},{16,0},{24,8},{1,17},{9,25},{17,1},{25,9},{2,18},{10... | collective-permute-start | bytes 884744 | tf_op jit(solution)/shard_map/ppermute | solution.py:49
  35.3 17.2 %collective-permute-start.15 = (bf16[192,768]{1,0:T(8,128)(2,1)S(1)}, bf16[192,768]{1,0:T(8,128)(2,1)S(1)}, u32[]{:S(2)}, u32[]{:S(2)}) collective-permute-start(bf16[192,768]{1,0:T(8,128)(2,1)S(1)} %bitcast.17), channel_id=1, source_target_pairs={{0,8},{8,16},{16,24},{24,0},{1,9},{9,17},{17,25},{25,1},{2,10},{10... | collective-permute-start | bytes 884744 | tf_op jit(solution)/shard_map/ppermute | solution.py:49
  43.2 21.5 %collective-permute-start.7 = (bf16[192,768]{1,0:T(8,128)(2,1)S(1)}, bf16[192,768]{1,0:T(8,128)(2,1)S(1)}, u32[]{:S(2)}, u32[]{:S(2)}) collective-permute-start(bf16[192,768]{1,0:T(8,128)(2,1)S(1)} %bitcast.8), channel_id=1, source_target_pairs={{0,24},{8,0},{16,8},{24,16},{1,25},{9,1},{17,9},{25,17},{2,26},{10... | collective-permute-start | bytes 884744 | tf_op jit(solution)/shard_map/ppermute | solution.py:49
  46.2 20.2 %collective-permute-start.8 = (bf16[192,768]{1,0:T(8,128)(2,1)S(1)}, bf16[192,768]{1,0:T(8,128)(2,1)S(1)}, u32[]{:S(2)}, u32[]{:S(2)}) collective-permute-start(bf16[192,768]{1,0:T(8,128)(2,1)S(1)} %bitcast.9), channel_id=1, source_target_pairs={{0,16},{8,24},{16,0},{24,8},{1,17},{9,25},{17,1},{25,9},{2,18},{10... | collective-permute-start | bytes 884744 | tf_op jit(solution)/shard_map/ppermute | solution.py:49
  48.4 18.0 %collective-permute-start.9 = (bf16[192,768]{1,0:T(8,128)(2,1)S(1)}, bf16[192,768]{1,0:T(8,128)(2,1)S(1)}, u32[]{:S(2)}, u32[]{:S(2)}) collective-permute-start(bf16[192,768]{1,0:T(8,128)(2,1)S(1)} %bitcast.10), channel_id=1, source_target_pairs={{0,8},{8,16},{16,24},{24,0},{1,9},{9,17},{17,25},{25,1},{2,10},{10... | collective-permute-start | bytes 884744 | tf_op jit(solution)/shard_map/ppermute | solution.py:49
  62.6 20.1 %collective-permute-start.16 = (bf16[192,768]{1,0:T(8,128)(2,1)S(1)}, bf16[192,768]{1,0:T(8,128)(2,1)S(1)}, u32[]{:S(2)}, u32[]{:S(2)}) collective-permute-start(bf16[192,768]{1,0:T(8,128)(2,1)S(1)} %get-tuple-element.27.refs_5_), channel_id=1, source_target_pairs={{0,8},{8,16},{16,24},{24,0},{1,9},{9,17},{17,25},{25,1},{2,10},{10... | collective-permute-start | bytes 884744 | tf_op jit(solution)/shard_map/ppermute | solution.py:54
  62.7 20.0 %collective-permute-start.17 = (bf16[192,768]{1,0:T(8,128)(2,1)S(1)}, bf16[192,768]{1,0:T(8,128)(2,1)S(1)}, u32[]{:S(2)}, u32[]{:S(2)}) collective-permute-start(bf16[192,768]{1,0:T(8,128)(2,1)S(1)} %get-tuple-element.28.refs_6_), channel_id=1, source_target_pairs={{0,16},{8,24},{16,0},{24,8},{1,17},{9,25},{17,1},{25,9},{2,18},{10... | collective-permute-start | bytes 884744 | tf_op jit(solution)/shard_map/ppermute | solution.py:54
  64.7 18.0 %collective-permute-start.18 = (bf16[192,768]{1,0:T(8,128)(2,1)S(1)}, bf16[192,768]{1,0:T(8,128)(2,1)S(1)}, u32[]{:S(2)}, u32[]{:S(2)}) collective-permute-start(bf16[192,768]{1,0:T(8,128)(2,1)S(1)} %get-tuple-element.29.refs_7_), channel_id=1, source_target_pairs={{0,24},{8,0},{16,8},{24,16},{1,25},{9,1},{17,9},{25,17},{2,26},{10... | collective-permute-start | bytes 884744 | tf_op jit(solution)/shard_map/ppermute | solution.py:54
  66.8 12.3 %collective-permute-start.19 = (f32[8,128]{1,0:T(8,128)S(1)}, f32[8,128]{1,0:T(8,128)S(1)}, u32[]{:S(2)}, u32[]{:S(2)}) collective-permute-start(f32[8,128]{1,0:T(8,128)S(1)} %shard_map.83.refs_4_), channel_id=1, source_target_pairs={{0,8},{8,16},{16,24},{24,0},{1,9},{9,17},{17,25},{25,1},{2,10},{10... | collective-permute-start | bytes 12296 | tf_op jit(solution)/shard_map/ppermute | solution.py:54
  67.2 11.9 %collective-permute-start.20 = (f32[8,128]{1,0:T(8,128)S(1)}, f32[8,128]{1,0:T(8,128)S(1)}, u32[]{:S(2)}, u32[]{:S(2)}) collective-permute-start(f32[8,128]{1,0:T(8,128)S(1)} %shard_map.83.refs_4_), channel_id=1, source_target_pairs={{0,16},{8,24},{16,0},{24,8},{1,17},{9,25},{17,1},{25,9},{2,18},{10... | collective-permute-start | bytes 12296 | tf_op jit(solution)/shard_map/ppermute | solution.py:54
  83.8 32.8 %all-to-all-start.3 = ((f32[8,152,128]{2,1,0:T(8,128)}), f32[8,152,128]{2,1,0:T(8,128)S(1)}, u32[]{:S(2)}, u32[]{:S(2)}) async-start(f32[8,152,128]{2,1,0:T(8,128)} %shard_map.84), calls=%async_computation.3 | async-start | bytes 1245184 | tf_op jit(solution)/shard_map/all_to_all | solution.py:323
  101.2 14.0 %collective-permute-start.10 = (bf16[192,768]{1,0:T(8,128)(2,1)S(1)}, bf16[192,768]{1,0:T(8,128)(2,1)S(1)}, u32[]{:S(2)}, u32[]{:S(2)}) collective-permute-start(bf16[192,768]{1,0:T(8,128)(2,1)S(1)} %get-tuple-element.22), channel_id=1, source_target_pairs={{0,8},{8,16},{16,24},{24,0},{1,9},{9,17},{17,25},{25,1},{2,10},{10... | collective-permute-start | bytes 884744 | tf_op jit(solution)/shard_map/ppermute | solution.py:54
  101.3 13.9 %collective-permute-start.11 = (bf16[192,768]{1,0:T(8,128)(2,1)S(1)}, bf16[192,768]{1,0:T(8,128)(2,1)S(1)}, u32[]{:S(2)}, u32[]{:S(2)}) collective-permute-start(bf16[192,768]{1,0:T(8,128)(2,1)S(1)} %get-tuple-element.23), channel_id=1, source_target_pairs={{0,16},{8,24},{16,0},{24,8},{1,17},{9,25},{17,1},{25,9},{2,18},{10... | collective-permute-start | bytes 884744 | tf_op jit(solution)/shard_map/ppermute | solution.py:54
  104.0 11.6 %collective-permute-start.12 = (bf16[192,768]{1,0:T(8,128)(2,1)S(1)}, bf16[192,768]{1,0:T(8,128)(2,1)S(1)}, u32[]{:S(2)}, u32[]{:S(2)}) collective-permute-start(bf16[192,768]{1,0:T(8,128)(2,1)S(1)} %get-tuple-element.24), channel_id=1, source_target_pairs={{0,24},{8,0},{16,8},{24,16},{1,25},{9,1},{17,9},{25,17},{2,26},{10... | collective-permute-start | bytes 884744 | tf_op jit(solution)/shard_map/ppermute | solution.py:54
  116.5 22.7 %all-to-all-start.1 = ((f32[8,144,128]{2,1,0:T(8,128)}), f32[8,144,128]{2,1,0:T(8,128)S(1)}, u32[]{:S(2)}, u32[]{:S(2)}) async-start(f32[8,144,128]{2,1,0:T(8,128)} %shard_map.81), calls=%async_computation.1 | async-start | bytes 1179648 | tf_op jit(solution)/shard_map/all_to_all | solution.py:329
  125.0 14.2 %collective-permute-start.24 = (f32[152,128]{1,0:T(8,128)S(1)}, f32[152,128]{1,0:T(8,128)S(1)}, u32[]{:S(2)}, u32[]{:S(2)}) collective-permute-start(f32[152,128]{1,0:T(8,128)S(1)} %shard_map.85.refs_0_), channel_id=1, source_target_pairs={{0,96},{32,64},{64,160},{96,128},{128,224},{160,192},{192,32},{224... | collective-permute-start | bytes 233480 | tf_op jit(solution)/shard_map/ppermute | solution.py:37
  125.2 14.1 %collective-permute-start.25 = (f32[152,128]{1,0:T(8,128)S(1)}, f32[152,128]{1,0:T(8,128)S(1)}, u32[]{:S(2)}, u32[]{:S(2)}) collective-permute-start(f32[152,128]{1,0:T(8,128)S(1)} %shard_map.85.refs_0_), channel_id=1, source_target_pairs={{0,128},{32,160},{64,192},{96,224},{128,0},{160,32},{192,64},{224,... | collective-permute-start | bytes 233480 | tf_op jit(solution)/shard_map/ppermute | solution.py:37
  128.4 10.9 %collective-permute-start.26 = (f32[152,128]{1,0:T(8,128)S(1)}, f32[152,128]{1,0:T(8,128)S(1)}, u32[]{:S(2)}, u32[]{:S(2)}) collective-permute-start(f32[152,128]{1,0:T(8,128)S(1)} %shard_map.85.refs_0_), channel_id=1, source_target_pairs={{0,160},{32,128},{64,224},{96,192},{128,32},{160,0},{192,96},{224,... | collective-permute-start | bytes 233480 | tf_op jit(solution)/shard_map/ppermute | solution.py:37
  128.4 10.9 %collective-permute-start.27 = (f32[152,128]{1,0:T(8,128)S(1)}, f32[152,128]{1,0:T(8,128)S(1)}, u32[]{:S(2)}, u32[]{:S(2)}) collective-permute-start(f32[152,128]{1,0:T(8,128)S(1)} %shard_map.85.refs_0_), channel_id=1, source_target_pairs={{0,192},{32,224},{64,0},{96,32},{128,64},{160,96},{192,128},{224,1... | collective-permute-start | bytes 233480 | tf_op jit(solution)/shard_map/ppermute | solution.py:37
  131.2 8.0 %collective-permute-start.28 = (f32[152,128]{1,0:T(8,128)S(1)}, f32[152,128]{1,0:T(8,128)S(1)}, u32[]{:S(2)}, u32[]{:S(2)}) collective-permute-start(f32[152,128]{1,0:T(8,128)S(1)} %shard_map.85.refs_0_), channel_id=1, source_target_pairs={{0,224},{32,192},{64,32},{96,0},{128,96},{160,64},{192,160},{224,1... | collective-permute-start | bytes 233480 | tf_op jit(solution)/shard_map/ppermute | solution.py:37
  (18 other events, 69.1 us)

commit v4 on v3

--- a/solution.py
+++ b/solution.py
@@ -61,7 +61,7 @@
     return moved
 
 
-def live_kernel(steps, size_ref, partner_ref, wave_ref, live_ref, copies_ref, chosen_ref):
+def live_kernel(size_ref, wave_ref, live_ref, copies_ref):
     rows, width = wave_ref.shape
     size = size_ref[0]
     row = lax.axis_index(OP) * rows + lax.broadcasted_iota(jnp.int32, (rows, width), 0)
@@ -71,6 +71,9 @@
     live_ref[...] = live
     for z in range(copies_ref.shape[0]):
         copies_ref[z] = live
+
+
+def chosen_kernel(steps, partner_ref, chosen_ref):
     me = lax.axis_index(SEC)
     partner = partner_ref[me]
     row = lax.broadcasted_iota(jnp.int32, chosen_ref.shape, 0)
@@ -269,15 +272,14 @@
         return jax.ShapeDtypeStruct(dims, dtype)
 
     every = [(0, 0)] + steps
-    live, copies, chosen = run(
-        functools.partial(live_kernel, every),
-        [
-            shape(rows, width, dtype=bf16),
-            shape(peers, rows, width, dtype=bf16),
-            shape(2 * len(every), 128),
-        ],
-        [SMEM, SMEM, VMEM],
-    )(sector_sizes, partner, wavefunction[0])
+    live, copies = run(
+        live_kernel,
+        [shape(rows, width, dtype=bf16), shape(peers, rows, width, dtype=bf16)],
+        [SMEM, VMEM],
+    )(sector_sizes, wavefunction[0])
+    chosen = run(
+        functools.partial(chosen_kernel, every), shape(2 * len(every), 128), [SMEM]
+    )(partner)
     own = lax.all_to_all(copies, Z, 0, 0, tiled=True).reshape(block, width)
     others = []
     for step in steps:

time: 143 us -> 142 us (level)
  transfers between devices with their start and end apart: 33 -> 33, of which waited for: 12 -> 11; matrix products, arithmetic and copies ran while one was open for 0% -> 0% of each run, Pallas kernels for 13% -> 13%
where the time goes in v4:
time: 142 us; the launch traced here: 139 us
  starting transfers between devices  64.4 us (45%)
  waiting for transfers between devices  39.4 us (28%)
  Pallas kernels  20.7 us (15%)
  local copies, waits for them, and re-layouts  13 us (9%)
  between operations  1.43 us (1%)
    ppermute x9, waiting for transfers between devices, to_ahead(): lax.ppermute(value, Y, [(i, (i + steps) % peers) for i in range(peers)])  24.4 us
    ppermute x14, starting transfers between devices, from_sector(): return lax.ppermute(value, SEC, pairs)  16.2 us
    unnamed x18, local copies, waits for them, and re-layouts  13 us
    ppermute x9, starting transfers between devices, to_ahead(): lax.ppermute(value, Y, [(i, (i + steps) % peers) for i in range(peers)])  9.66 us
    all_to_all x1, starting transfers between devices, per_device(): own = lax.all_to_all(copies, Z, 0, 0, tiled=True).reshape(block, width)  8.57 us
    ppermute x6, starting transfers between devices, from_ahead(): lax.ppermute(value, Y, [(i, (i - steps) % peers) for i in range(peers)])  8.32 us
    all_to_all x1, waiting for transfers between devices, per_device(): direct_mine = lax.all_to_all(direct_lines, Z, 0, 0, tiled=True)  7.33 us
    all_to_all x1, starting transfers between devices, per_device(): adjoint_lines = lax.all_to_all(adjoint_lines, Z, 0, 0, tiled=True)  7.21 us
  transfers between devices with their start and end apart: 33, of which 11 were waited for; matrix products, arithmetic and copies ran while one was open for 0% of the time, Pallas kernels for 13%

profile of v4, /device:TPU:32, one launch (start us, length us, event | category | flops | bytes accessed | tf_op | source)
XLA Modules:
  0.0 138.8 jit_solution(8356510634764672339)
XLA Ops:
  2.8 8.6 %all-to-all-start.2 = ((bf16[8,24,768]{2,1,0:T(8,128)(2,1)}), bf16[8,24,768]{2,1,0:T(8,128)(2,1)S(1)}, u32[]{:S(2)}, u32[]{:S(2)}) async-start(bf16[8,24,768]{2,1,0:T(8,128)(2,1)} %get-tuple-element.23), calls=%async_computation.2 | async-start | bytes 589824 | tf_op jit(solution)/shard_map/all_to_all | solution.py:283
  23.3 7.2 %all-to-all-start = ((bf16[8,24,768]{2,1,0:T(8,128)(2,1)}), bf16[8,24,768]{2,1,0:T(8,128)(2,1)S(1)}, u32[]{:S(2)}, u32[]{:S(2)}) async-start(bf16[8,24,768]{2,1,0:T(8,128)(2,1)} %shard_map.80), calls=%async_computation | async-start | bytes 589824 | tf_op jit(solution)/shard_map/all_to_all | solution.py:290
  30.5 3.0 %collective-permute-start.13 = (bf16[192,768]{1,0:T(8,128)(2,1)S(1)}, bf16[192,768]{1,0:T(8,128)(2,1)S(1)}, u32[]{:S(2)}, u32[]{:S(2)}) collective-permute-start(bf16[192,768]{1,0:T(8,128)(2,1)S(1)} %bitcast.15), channel_id=1, source_target_pairs={{0,24},{8,0},{16,8},{24,16},{1,25},{9,1},{17,9},{25,17},{2,26},{10... | collective-permute-start | bytes 884744 | tf_op jit(solution)/shard_map/ppermute | solution.py:49
  35.1 3.1 %shard_map.78 = (bf16[3,768,768]{2,1,0:T(8,128)(2,1)S(1)}, bf16[3,768,768]{2,1,0:T(8,128)(2,1)S(1)}) custom-call(bf16[3,768,768]{2,1,0:T(8,128)(2,1)} %bitcast.20, bf16[3,768,768]{2,1,0:T(8,128)(2,1)} %bitcast.21), custom_call_target="tpu_custom_call" | custom-call | bytes 7077888 | tf_op jit(solution)/shard_map/pallas_call | solution.py:298
  40.0 1.8 %copy-done.6 = bf16[3,768,768]{2,1,0:T(8,128)(2,1)} copy-done((bf16[3,768,768]{2,1,0:T(8,128)(2,1)}, bf16[3,768,768]{2,1,0:T(8,128)(2,1)S(1)}, u32[]{:S(2)}) %copy-start.6) | copy-done | bytes 3538968
  42.0 3.0 %collective-permute-start.7 = (bf16[192,768]{1,0:T(8,128)(2,1)S(1)}, bf16[192,768]{1,0:T(8,128)(2,1)S(1)}, u32[]{:S(2)}, u32[]{:S(2)}) collective-permute-start(bf16[192,768]{1,0:T(8,128)(2,1)S(1)} %bitcast.8), channel_id=1, source_target_pairs={{0,24},{8,0},{16,8},{24,16},{1,25},{9,1},{17,9},{25,17},{2,26},{10... | collective-permute-start | bytes 884744 | tf_op jit(solution)/shard_map/ppermute | solution.py:49
  47.2 4.1 %collective-permute-done.15.refs_3_ = bf16[192,768]{1,0:T(8,128)(2,1)S(1)} collective-permute-done((bf16[192,768]{1,0:T(8,128)(2,1)S(1)}, bf16[192,768]{1,0:T(8,128)(2,1)S(1)}, u32[]{:S(2)}, u32[]{:S(2)}) %collective-permute-start.15) | collective-permute-done | bytes 294944 | tf_op jit(solution)/shard_map/ppermute | solution.py:49
  51.3 2.0 %copy-done.4 = bf16[3,768,768]{2,1,0:T(8,128)(2,1)S(1)} copy-done((bf16[3,768,768]{2,1,0:T(8,128)(2,1)S(1)}, bf16[3,768,768]{2,1,0:T(8,128)(2,1)}, u32[]{:S(2)}) %copy-start.4) | copy-done | bytes 3538968
  53.3 2.0 %copy-done.7 = bf16[3,768,768]{2,1,0:T(8,128)(2,1)S(1)} copy-done((bf16[3,768,768]{2,1,0:T(8,128)(2,1)S(1)}, bf16[3,768,768]{2,1,0:T(8,128)(2,1)}, u32[]{:S(2)}) %copy-start.7) | copy-done | bytes 3538968
  55.3 6.1 %shard_map.83 = (f32[192,768]{1,0:T(8,128)S(1)}, bf16[192,768]{1,0:T(8,128)(2,1)S(1)}, bf16[192,768]{1,0:T(8,128)(2,1)S(1)}, bf16[192,768]{1,0:T(8,128)(2,1)S(1)}) custom-call(bf16[3,768,768]{2,1,0:T(8,128)(2,1)S(1)} %copy-done.4, bf16[3,768,768]{2,1,0:T(8,128)(2,1)S(1)} %copy-done.7, bf16[192,768]{1,0:T(8,128)(2,1)S(1)} %bitcast.18, ...), custom_call_target="tpu_custom_call" | custom-call | flops 5435817984 | bytes 1048576 | tf_op jit(solution)/shard_map/pallas_call | solution.py:309
  61.5 1.9 %collective-permute-start.17 = (bf16[192,768]{1,0:T(8,128)(2,1)S(1)}, bf16[192,768]{1,0:T(8,128)(2,1)S(1)}, u32[]{:S(2)}, u32[]{:S(2)}) collective-permute-start(bf16[192,768]{1,0:T(8,128)(2,1)S(1)} %get-tuple-element.26.refs_6_), channel_id=1, source_target_pairs={{0,16},{8,24},{16,0},{24,8},{1,17},{9,25},{17,1},{25,9},{2,18},{10... | collective-permute-start | bytes 884744 | tf_op jit(solution)/shard_map/ppermute | solution.py:54
  66.0 2.1 %collective-permute-start.20 = (f32[8,128]{1,0:T(8,128)S(1)}, f32[8,128]{1,0:T(8,128)S(1)}, u32[]{:S(2)}, u32[]{:S(2)}) collective-permute-start(f32[8,128]{1,0:T(8,128)S(1)} %shard_map.84.refs_4_), channel_id=1, source_target_pairs={{0,16},{8,24},{16,0},{24,8},{1,17},{9,25},{17,1},{25,9},{2,18},{10... | collective-permute-start | bytes 12296 | tf_op jit(solution)/shard_map/ppermute | solution.py:54
  68.1 9.8 %collective-permute-done.19.refs_5_ = f32[8,128]{1,0:T(8,128)S(1)} collective-permute-done((f32[8,128]{1,0:T(8,128)S(1)}, f32[8,128]{1,0:T(8,128)S(1)}, u32[]{:S(2)}, u32[]{:S(2)}) %collective-permute-start.19) | collective-permute-done | bytes 4128 | tf_op jit(solution)/shard_map/ppermute | solution.py:54
  77.9 3.6 %collective-permute-done.21.refs_7_ = f32[8,128]{1,0:T(8,128)S(1)} collective-permute-done((f32[8,128]{1,0:T(8,128)S(1)}, f32[8,128]{1,0:T(8,128)S(1)}, u32[]{:S(2)}, u32[]{:S(2)}) %collective-permute-start.21) | collective-permute-done | bytes 4128 | tf_op jit(solution)/shard_map/ppermute | solution.py:54
  82.5 7.2 %all-to-all-start.3 = ((f32[8,152,128]{2,1,0:T(8,128)}), f32[8,152,128]{2,1,0:T(8,128)S(1)}, u32[]{:S(2)}, u32[]{:S(2)}) async-start(f32[8,152,128]{2,1,0:T(8,128)} %shard_map.85), calls=%async_computation.3 | async-start | bytes 1245184 | tf_op jit(solution)/shard_map/all_to_all | solution.py:325
  89.8 2.0 %copy-done.5 = bf16[3,768,768]{2,1,0:T(8,128)(2,1)S(1)} copy-done((bf16[3,768,768]{2,1,0:T(8,128)(2,1)S(1)}, bf16[3,768,768]{2,1,0:T(8,128)(2,1)}, u32[]{:S(2)}) %copy-start.5) | copy-done | bytes 3538968
  91.8 2.0 %copy-done.8 = bf16[3,768,768]{2,1,0:T(8,128)(2,1)S(1)} copy-done((bf16[3,768,768]{2,1,0:T(8,128)(2,1)S(1)}, bf16[3,768,768]{2,1,0:T(8,128)(2,1)}, u32[]{:S(2)}) %copy-start.8) | copy-done | bytes 3538968
  93.8 6.2 %shard_map.81 = (f32[192,768]{1,0:T(8,128)S(1)}, bf16[192,768]{1,0:T(8,128)(2,1)S(1)}, bf16[192,768]{1,0:T(8,128)(2,1)S(1)}, bf16[192,768]{1,0:T(8,128)(2,1)S(1)}) custom-call(bf16[3,768,768]{2,1,0:T(8,128)(2,1)S(1)} %copy-done.5, bf16[3,768,768]{2,1,0:T(8,128)(2,1)S(1)} %copy-done.8, bf16[192,768]{1,0:T(8,128)(2,1)S(1)} %bitcast.12, ...), custom_call_target="tpu_custom_call" | custom-call | flops 5435817984 | bytes 1048576 | tf_op jit(solution)/shard_map/pallas_call | solution.py:317
  100.1 2.7 %collective-permute-start.11 = (bf16[192,768]{1,0:T(8,128)(2,1)S(1)}, bf16[192,768]{1,0:T(8,128)(2,1)S(1)}, u32[]{:S(2)}, u32[]{:S(2)}) collective-permute-start(bf16[192,768]{1,0:T(8,128)(2,1)S(1)} %get-tuple-element.21), channel_id=1, source_target_pairs={{0,16},{8,24},{16,0},{24,8},{1,17},{9,25},{17,1},{25,9},{2,18},{10... | collective-permute-start | bytes 884744 | tf_op jit(solution)/shard_map/ppermute | solution.py:54
  103.3 10.7 %collective-permute-done.10.refs_1_ = bf16[192,768]{1,0:T(8,128)(2,1)S(1)} collective-permute-done((bf16[192,768]{1,0:T(8,128)(2,1)S(1)}, bf16[192,768]{1,0:T(8,128)(2,1)S(1)}, u32[]{:S(2)}, u32[]{:S(2)}) %collective-permute-start.10) | collective-permute-done | bytes 294944 | tf_op jit(solution)/shard_map/ppermute | solution.py:54
  115.3 7.2 %all-to-all-start.1 = ((f32[8,144,128]{2,1,0:T(8,128)}), f32[8,144,128]{2,1,0:T(8,128)S(1)}, u32[]{:S(2)}, u32[]{:S(2)}) async-start(f32[8,144,128]{2,1,0:T(8,128)} %shard_map.82), calls=%async_computation.1 | async-start | bytes 1179648 | tf_op jit(solution)/shard_map/all_to_all | solution.py:331
  124.0 3.2 %collective-permute-start.25 = (f32[152,128]{1,0:T(8,128)S(1)}, f32[152,128]{1,0:T(8,128)S(1)}, u32[]{:S(2)}, u32[]{:S(2)}) collective-permute-start(f32[152,128]{1,0:T(8,128)S(1)} %shard_map.86.refs_0_), channel_id=1, source_target_pairs={{0,128},{32,160},{64,192},{96,224},{128,0},{160,32},{192,64},{224,... | collective-permute-start | bytes 233480 | tf_op jit(solution)/shard_map/ppermute | solution.py:37
  127.2 2.8 %collective-permute-start.27 = (f32[152,128]{1,0:T(8,128)S(1)}, f32[152,128]{1,0:T(8,128)S(1)}, u32[]{:S(2)}, u32[]{:S(2)}) collective-permute-start(f32[152,128]{1,0:T(8,128)S(1)} %shard_map.86.refs_0_), channel_id=1, source_target_pairs={{0,192},{32,224},{64,0},{96,32},{128,64},{160,96},{192,128},{224,1... | collective-permute-start | bytes 233480 | tf_op jit(solution)/shard_map/ppermute | solution.py:37
  130.7 7.3 %all-to-all-done.1.direct_ref = f32[8,144,128]{2,1,0:T(8,128)S(1)} async-done(((f32[8,144,128]{2,1,0:T(8,128)}), f32[8,144,128]{2,1,0:T(8,128)S(1)}, u32[]{:S(2)}, u32[]{:S(2)}) %all-to-all-start.1) | async-done | bytes 589856 | tf_op jit(solution)/shard_map/all_to_all | solution.py:331
  (71 shorter events, 27.6 us)
Async XLA Ops:
  2.8 20.5 %all-to-all-start.2 = ((bf16[8,24,768]{2,1,0:T(8,128)(2,1)}), bf16[8,24,768]{2,1,0:T(8,128)(2,1)S(1)}, u32[]{:S(2)}, u32[]{:S(2)}) async-start(bf16[8,24,768]{2,1,0:T(8,128)(2,1)} %get-tuple-element.23), calls=%async_computation.2 | async-start | bytes 589824 | tf_op jit(solution)/shard_map/all_to_all | solution.py:283
  12.9 7.8 %collective-permute-start.2 = (bf16[24,768]{1,0:T(8,128)(2,1)S(1)}, bf16[24,768]{1,0:T(8,128)(2,1)S(1)}, u32[]{:S(2)}, u32[]{:S(2)}) collective-permute-start(bf16[24,768]{1,0:T(8,128)(2,1)S(1)} %get-tuple-element.18.refs_0_.live_ref), channel_id=1, source_target_pairs={{0,96},{32,64},{64,160},{96,128},{128,224},{160,192},{192,32},{224... | collective-permute-start | bytes 110600 | tf_op jit(solution)/shard_map/ppermute | solution.py:37
  23.3 18.7 %all-to-all-start = ((bf16[8,24,768]{2,1,0:T(8,128)(2,1)}), bf16[8,24,768]{2,1,0:T(8,128)(2,1)S(1)}, u32[]{:S(2)}, u32[]{:S(2)}) async-start(bf16[8,24,768]{2,1,0:T(8,128)(2,1)} %shard_map.80), calls=%async_computation | async-start | bytes 589824 | tf_op jit(solution)/shard_map/all_to_all | solution.py:290
  30.5 16.7 %collective-permute-start.13 = (bf16[192,768]{1,0:T(8,128)(2,1)S(1)}, bf16[192,768]{1,0:T(8,128)(2,1)S(1)}, u32[]{:S(2)}, u32[]{:S(2)}) collective-permute-start(bf16[192,768]{1,0:T(8,128)(2,1)S(1)} %bitcast.15), channel_id=1, source_target_pairs={{0,24},{8,0},{16,8},{24,16},{1,25},{9,1},{17,9},{25,17},{2,26},{10... | collective-permute-start | bytes 884744 | tf_op jit(solution)/shard_map/ppermute | solution.py:49
  33.5 13.7 %collective-permute-start.14 = (bf16[192,768]{1,0:T(8,128)(2,1)S(1)}, bf16[192,768]{1,0:T(8,128)(2,1)S(1)}, u32[]{:S(2)}, u32[]{:S(2)}) collective-permute-start(bf16[192,768]{1,0:T(8,128)(2,1)S(1)} %bitcast.16), channel_id=1, source_target_pairs={{0,16},{8,24},{16,0},{24,8},{1,17},{9,25},{17,1},{25,9},{2,18},{10... | collective-permute-start | bytes 884744 | tf_op jit(solution)/shard_map/ppermute | solution.py:49
  34.1 17.2 %collective-permute-start.15 = (bf16[192,768]{1,0:T(8,128)(2,1)S(1)}, bf16[192,768]{1,0:T(8,128)(2,1)S(1)}, u32[]{:S(2)}, u32[]{:S(2)}) collective-permute-start(bf16[192,768]{1,0:T(8,128)(2,1)S(1)} %bitcast.17), channel_id=1, source_target_pairs={{0,8},{8,16},{16,24},{24,0},{1,9},{9,17},{17,25},{25,1},{2,10},{10... | collective-permute-start | bytes 884744 | tf_op jit(solution)/shard_map/ppermute | solution.py:49
  42.0 21.5 %collective-permute-start.7 = (bf16[192,768]{1,0:T(8,128)(2,1)S(1)}, bf16[192,768]{1,0:T(8,128)(2,1)S(1)}, u32[]{:S(2)}, u32[]{:S(2)}) collective-permute-start(bf16[192,768]{1,0:T(8,128)(2,1)S(1)} %bitcast.8), channel_id=1, source_target_pairs={{0,24},{8,0},{16,8},{24,16},{1,25},{9,1},{17,9},{25,17},{2,26},{10... | collective-permute-start | bytes 884744 | tf_op jit(solution)/shard_map/ppermute | solution.py:49
  45.0 20.2 %collective-permute-start.8 = (bf16[192,768]{1,0:T(8,128)(2,1)S(1)}, bf16[192,768]{1,0:T(8,128)(2,1)S(1)}, u32[]{:S(2)}, u32[]{:S(2)}) collective-permute-start(bf16[192,768]{1,0:T(8,128)(2,1)S(1)} %bitcast.9), channel_id=1, source_target_pairs={{0,16},{8,24},{16,0},{24,8},{1,17},{9,25},{17,1},{25,9},{2,18},{10... | collective-permute-start | bytes 884744 | tf_op jit(solution)/shard_map/ppermute | solution.py:49
  47.2 18.0 %collective-permute-start.9 = (bf16[192,768]{1,0:T(8,128)(2,1)S(1)}, bf16[192,768]{1,0:T(8,128)(2,1)S(1)}, u32[]{:S(2)}, u32[]{:S(2)}) collective-permute-start(bf16[192,768]{1,0:T(8,128)(2,1)S(1)} %bitcast.10), channel_id=1, source_target_pairs={{0,8},{8,16},{16,24},{24,0},{1,9},{9,17},{17,25},{25,1},{2,10},{10... | collective-permute-start | bytes 884744 | tf_op jit(solution)/shard_map/ppermute | solution.py:49
  61.4 20.1 %collective-permute-start.16 = (bf16[192,768]{1,0:T(8,128)(2,1)S(1)}, bf16[192,768]{1,0:T(8,128)(2,1)S(1)}, u32[]{:S(2)}, u32[]{:S(2)}) collective-permute-start(bf16[192,768]{1,0:T(8,128)(2,1)S(1)} %get-tuple-element.25.refs_5_), channel_id=1, source_target_pairs={{0,8},{8,16},{16,24},{24,0},{1,9},{9,17},{17,25},{25,1},{2,10},{10... | collective-permute-start | bytes 884744 | tf_op jit(solution)/shard_map/ppermute | solution.py:54
  61.5 20.0 %collective-permute-start.17 = (bf16[192,768]{1,0:T(8,128)(2,1)S(1)}, bf16[192,768]{1,0:T(8,128)(2,1)S(1)}, u32[]{:S(2)}, u32[]{:S(2)}) collective-permute-start(bf16[192,768]{1,0:T(8,128)(2,1)S(1)} %get-tuple-element.26.refs_6_), channel_id=1, source_target_pairs={{0,16},{8,24},{16,0},{24,8},{1,17},{9,25},{17,1},{25,9},{2,18},{10... | collective-permute-start | bytes 884744 | tf_op jit(solution)/shard_map/ppermute | solution.py:54
  63.5 18.0 %collective-permute-start.18 = (bf16[192,768]{1,0:T(8,128)(2,1)S(1)}, bf16[192,768]{1,0:T(8,128)(2,1)S(1)}, u32[]{:S(2)}, u32[]{:S(2)}) collective-permute-start(bf16[192,768]{1,0:T(8,128)(2,1)S(1)} %get-tuple-element.27.refs_7_), channel_id=1, source_target_pairs={{0,24},{8,0},{16,8},{24,16},{1,25},{9,1},{17,9},{25,17},{2,26},{10... | collective-permute-start | bytes 884744 | tf_op jit(solution)/shard_map/ppermute | solution.py:54
  65.6 12.3 %collective-permute-start.19 = (f32[8,128]{1,0:T(8,128)S(1)}, f32[8,128]{1,0:T(8,128)S(1)}, u32[]{:S(2)}, u32[]{:S(2)}) collective-permute-start(f32[8,128]{1,0:T(8,128)S(1)} %shard_map.84.refs_4_), channel_id=1, source_target_pairs={{0,8},{8,16},{16,24},{24,0},{1,9},{9,17},{17,25},{25,1},{2,10},{10... | collective-permute-start | bytes 12296 | tf_op jit(solution)/shard_map/ppermute | solution.py:54
  66.0 11.9 %collective-permute-start.20 = (f32[8,128]{1,0:T(8,128)S(1)}, f32[8,128]{1,0:T(8,128)S(1)}, u32[]{:S(2)}, u32[]{:S(2)}) collective-permute-start(f32[8,128]{1,0:T(8,128)S(1)} %shard_map.84.refs_4_), channel_id=1, source_target_pairs={{0,16},{8,24},{16,0},{24,8},{1,17},{9,25},{17,1},{25,9},{2,18},{10... | collective-permute-start | bytes 12296 | tf_op jit(solution)/shard_map/ppermute | solution.py:54
  82.5 32.8 %all-to-all-start.3 = ((f32[8,152,128]{2,1,0:T(8,128)}), f32[8,152,128]{2,1,0:T(8,128)S(1)}, u32[]{:S(2)}, u32[]{:S(2)}) async-start(f32[8,152,128]{2,1,0:T(8,128)} %shard_map.85), calls=%async_computation.3 | async-start | bytes 1245184 | tf_op jit(solution)/shard_map/all_to_all | solution.py:325
  100.0 14.0 %collective-permute-start.10 = (bf16[192,768]{1,0:T(8,128)(2,1)S(1)}, bf16[192,768]{1,0:T(8,128)(2,1)S(1)}, u32[]{:S(2)}, u32[]{:S(2)}) collective-permute-start(bf16[192,768]{1,0:T(8,128)(2,1)S(1)} %get-tuple-element.20), channel_id=1, source_target_pairs={{0,8},{8,16},{16,24},{24,0},{1,9},{9,17},{17,25},{25,1},{2,10},{10... | collective-permute-start | bytes 884744 | tf_op jit(solution)/shard_map/ppermute | solution.py:54
  100.1 13.9 %collective-permute-start.11 = (bf16[192,768]{1,0:T(8,128)(2,1)S(1)}, bf16[192,768]{1,0:T(8,128)(2,1)S(1)}, u32[]{:S(2)}, u32[]{:S(2)}) collective-permute-start(bf16[192,768]{1,0:T(8,128)(2,1)S(1)} %get-tuple-element.21), channel_id=1, source_target_pairs={{0,16},{8,24},{16,0},{24,8},{1,17},{9,25},{17,1},{25,9},{2,18},{10... | collective-permute-start | bytes 884744 | tf_op jit(solution)/shard_map/ppermute | solution.py:54
  102.8 11.6 %collective-permute-start.12 = (bf16[192,768]{1,0:T(8,128)(2,1)S(1)}, bf16[192,768]{1,0:T(8,128)(2,1)S(1)}, u32[]{:S(2)}, u32[]{:S(2)}) collective-permute-start(bf16[192,768]{1,0:T(8,128)(2,1)S(1)} %get-tuple-element.22), channel_id=1, source_target_pairs={{0,24},{8,0},{16,8},{24,16},{1,25},{9,1},{17,9},{25,17},{2,26},{10... | collective-permute-start | bytes 884744 | tf_op jit(solution)/shard_map/ppermute | solution.py:54
  115.3 22.7 %all-to-all-start.1 = ((f32[8,144,128]{2,1,0:T(8,128)}), f32[8,144,128]{2,1,0:T(8,128)S(1)}, u32[]{:S(2)}, u32[]{:S(2)}) async-start(f32[8,144,128]{2,1,0:T(8,128)} %shard_map.82), calls=%async_computation.1 | async-start | bytes 1179648 | tf_op jit(solution)/shard_map/all_to_all | solution.py:331
  123.8 14.3 %collective-permute-start.24 = (f32[152,128]{1,0:T(8,128)S(1)}, f32[152,128]{1,0:T(8,128)S(1)}, u32[]{:S(2)}, u32[]{:S(2)}) collective-permute-start(f32[152,128]{1,0:T(8,128)S(1)} %shard_map.86.refs_0_), channel_id=1, source_target_pairs={{0,96},{32,64},{64,160},{96,128},{128,224},{160,192},{192,32},{224... | collective-permute-start | bytes 233480 | tf_op jit(solution)/shard_map/ppermute | solution.py:37
  124.0 14.1 %collective-permute-start.25 = (f32[152,128]{1,0:T(8,128)S(1)}, f32[152,128]{1,0:T(8,128)S(1)}, u32[]{:S(2)}, u32[]{:S(2)}) collective-permute-start(f32[152,128]{1,0:T(8,128)S(1)} %shard_map.86.refs_0_), channel_id=1, source_target_pairs={{0,128},{32,160},{64,192},{96,224},{128,0},{160,32},{192,64},{224,... | collective-permute-start | bytes 233480 | tf_op jit(solution)/shard_map/ppermute | solution.py:37
  127.2 10.9 %collective-permute-start.26 = (f32[152,128]{1,0:T(8,128)S(1)}, f32[152,128]{1,0:T(8,128)S(1)}, u32[]{:S(2)}, u32[]{:S(2)}) collective-permute-start(f32[152,128]{1,0:T(8,128)S(1)} %shard_map.86.refs_0_), channel_id=1, source_target_pairs={{0,160},{32,128},{64,224},{96,192},{128,32},{160,0},{192,96},{224,... | collective-permute-start | bytes 233480 | tf_op jit(solution)/shard_map/ppermute | solution.py:37
  127.2 10.9 %collective-permute-start.27 = (f32[152,128]{1,0:T(8,128)S(1)}, f32[152,128]{1,0:T(8,128)S(1)}, u32[]{:S(2)}, u32[]{:S(2)}) collective-permute-start(f32[152,128]{1,0:T(8,128)S(1)} %shard_map.86.refs_0_), channel_id=1, source_target_pairs={{0,192},{32,224},{64,0},{96,32},{128,64},{160,96},{192,128},{224,1... | collective-permute-start | bytes 233480 | tf_op jit(solution)/shard_map/ppermute | solution.py:37
  130.0 8.1 %collective-permute-start.28 = (f32[152,128]{1,0:T(8,128)S(1)}, f32[152,128]{1,0:T(8,128)S(1)}, u32[]{:S(2)}, u32[]{:S(2)}) collective-permute-start(f32[152,128]{1,0:T(8,128)S(1)} %shard_map.86.refs_0_), channel_id=1, source_target_pairs={{0,224},{32,192},{64,32},{96,0},{128,96},{160,64},{192,160},{224,1... | collective-permute-start | bytes 233480 | tf_op jit(solution)/shard_map/ppermute | solution.py:37
  (18 other events, 71.3 us)

commit v5 on v4

--- a/solution.py
+++ b/solution.py
@@ -24,7 +24,8 @@
 
 def other_sectors():
     far, near = (lax.axis_size(name) for name in SEC)
-    return [(i, j) for i in range(far) for j in range(near) if i or j]
+    steps = [(i, j) for i in range(far) for j in range(near) if i or j]
+    return sorted(steps, key=lambda step: (min(step[0], far - step[0]), step[1]))
 
 
 def from_sector(value, step):
@@ -192,10 +193,12 @@
         for ref in blocks[1:]:
             total += ref[part, :].astype(f32)
         for z in range(2):
+            lines = total[z * each : (z + 1) * each]
+            if not sums_refs:
+                out_ref[pair + z] = lines.astype(out_ref.dtype)
+                continue
             for n, (r, c) in enumerate(tiles_of(each, width)):
-                out_ref[pair + z, 8 * n : 8 * n + 8, :] = total[
-                    z * each + r : z * each + r + 8, c : c + 128
-                ]
+                out_ref[pair + z, 8 * n : 8 * n + 8, :] = lines[r : r + 8, c : c + 128]
     if sums_refs:
         total = sums_refs[0][...]
         for ref in sums_refs[1:]:
@@ -214,7 +217,10 @@
 def update_kernel(size_ref, chosen_ref, direct_ref, diagonal_ref, live_ref, *refs):
     got_refs, (updated_ref, residual_ref, routed) = refs[:-3], refs[-3:]
     rows, width = live_ref.shape
-    peers, length, _ = direct_ref.shape
+    length = routed.shape[0]
+    direct_all = direct_ref[0].astype(f32)
+    for z in range(1, direct_ref.shape[0]):
+        direct_all += direct_ref[z].astype(f32)
     chosen = chosen_ref[...]
     value = sums = None
     for n, got_ref in enumerate(got_refs):
@@ -233,9 +239,7 @@
         wave = live_ref[r : r + 8, c : c + 128].astype(f32)
         diagonal = diagonal_ref[r : r + 8, c : c + 128]
         part = slice(8 * n, 8 * n + 8)
-        direct = direct_ref[0, part, :]
-        for z in range(1, peers):
-            direct += direct_ref[z, part, :]
+        direct = direct_all[r : r + 8, c : c + 128]
         sigma = direct + routed[part, :] + diagonal * wave
         sigma = jnp.where((where_row < size) & (where_col < size), sigma, 0.0)
         residual = sigma - energy * wave
@@ -326,7 +330,7 @@
     adjoint_mine = run(meet_kernel, shape(length + 8, 128), [VMEM])(adjoint_lines)
     routed = [adjoint_mine] + [from_sector(adjoint_mine, step) for step in steps]
     direct_lines = run(
-        functools.partial(rows_kernel, lines), shape(peers, length, 128), [VMEM] * lines
+        functools.partial(rows_kernel, lines), shape(peers, rows, width, dtype=bf16), [VMEM] * lines
     )(direct[0], *direct_got)
     direct_mine = lax.all_to_all(direct_lines, Z, 0, 0, tiled=True)
     updated, residual = run(

time: 142 us -> 139 us (0.979)
  waiting for transfers between devices: 39.4 us -> 35.8 us
  starting transfers between devices: 64.4 us -> 66.3 us
    all_to_all x1, waiting for transfers between devices: 7.33 us -> 0.25 us  [per_device(): direct_mine = lax.all_to_all(direct_lines, Z, 0, 0, tiled=True)]
    ppermute x14, waiting for transfers between devices: 1.78 us -> 5.36 us  [from_sector(): return lax.ppermute(value, SEC, pairs)]
    ppermute x14, starting transfers between devices: 16.2 us -> 18.1 us  [from_sector(): return lax.ppermute(value, SEC, pairs)]
  transfers between devices with their start and end apart: 33 -> 33, of which waited for: 11 -> 12; matrix products, arithmetic and copies ran while one was open for 0% -> 0% of each run, Pallas kernels for 13% -> 13%
where the time goes in v5:
time: 139 us; the launch traced here: 137 us
  starting transfers between devices  66.3 us (48%)
  waiting for transfers between devices  35.8 us (26%)
  Pallas kernels  20.6 us (15%)
  local copies, waits for them, and re-layouts  13 us (9%)
  between operations  1.42 us (1%)
    ppermute x9, waiting for transfers between devices, to_ahead(): lax.ppermute(value, Y, [(i, (i + steps) % peers) for i in range(peers)])  24.4 us
    ppermute x14, starting transfers between devices, from_sector(): return lax.ppermute(value, SEC, pairs)  18.1 us
    unnamed x18, local copies, waits for them, and re-layouts  13 us
    ppermute x9, starting transfers between devices, to_ahead(): lax.ppermute(value, Y, [(i, (i + steps) % peers) for i in range(peers)])  9.66 us
    all_to_all x1, starting transfers between devices, per_device(): own = lax.all_to_all(copies, Z, 0, 0, tiled=True).reshape(block, width)  8.57 us
    ppermute x6, starting transfers between devices, from_ahead(): lax.ppermute(value, Y, [(i, (i - steps) % peers) for i in range(peers)])  8.36 us
    all_to_all x1, starting transfers between devices, per_device(): adjoint_lines = lax.all_to_all(adjoint_lines, Z, 0, 0, tiled=True)  7.21 us
    all_to_all x1, starting transfers between devices, per_device(): theirs = lax.all_to_all(copies, Z, 0, 0, tiled=True).reshape(block, width)  7.21 us
  transfers between devices with their start and end apart: 33, of which 12 were waited for; matrix products, arithmetic and copies ran while one was open for 0% of the time, Pallas kernels for 13%

profile of v5, /device:TPU:32, one launch (start us, length us, event | category | flops | bytes accessed | tf_op | source)
XLA Modules:
  0.0 137.1 jit_solution(18337503009112935858)
XLA Ops:
  2.8 8.6 %all-to-all-start.2 = ((bf16[8,24,768]{2,1,0:T(8,128)(2,1)}), bf16[8,24,768]{2,1,0:T(8,128)(2,1)S(1)}, u32[]{:S(2)}, u32[]{:S(2)}) async-start(bf16[8,24,768]{2,1,0:T(8,128)(2,1)} %get-tuple-element.23), calls=%async_computation.2 | async-start | bytes 589824 | tf_op jit(solution)/shard_map/all_to_all | solution.py:287
  14.6 3.0 %collective-permute-start.4 = (bf16[24,768]{1,0:T(8,128)(2,1)S(1)}, bf16[24,768]{1,0:T(8,128)(2,1)S(1)}, u32[]{:S(2)}, u32[]{:S(2)}) collective-permute-start(bf16[24,768]{1,0:T(8,128)(2,1)S(1)} %get-tuple-element.18.refs_0_.live_ref), channel_id=1, source_target_pairs={{0,224},{32,192},{64,32},{96,0},{128,96},{160,64},{192,160},{224,1... | collective-permute-start | bytes 110600 | tf_op jit(solution)/shard_map/ppermute | solution.py:38
  18.2 2.2 %collective-permute-start.6 = (bf16[24,768]{1,0:T(8,128)(2,1)S(1)}, bf16[24,768]{1,0:T(8,128)(2,1)S(1)}, u32[]{:S(2)}, u32[]{:S(2)}) collective-permute-start(bf16[24,768]{1,0:T(8,128)(2,1)S(1)} %get-tuple-element.18.refs_0_.live_ref), channel_id=1, source_target_pairs={{0,160},{32,128},{64,224},{96,192},{128,32},{160,0},{192,96},{224,... | collective-permute-start | bytes 110600 | tf_op jit(solution)/shard_map/ppermute | solution.py:38
  24.3 7.2 %all-to-all-start = ((bf16[8,24,768]{2,1,0:T(8,128)(2,1)}), bf16[8,24,768]{2,1,0:T(8,128)(2,1)S(1)}, u32[]{:S(2)}, u32[]{:S(2)}) async-start(bf16[8,24,768]{2,1,0:T(8,128)(2,1)} %shard_map.80), calls=%async_computation | async-start | bytes 589824 | tf_op jit(solution)/shard_map/all_to_all | solution.py:294
  31.5 3.0 %collective-permute-start.13 = (bf16[192,768]{1,0:T(8,128)(2,1)S(1)}, bf16[192,768]{1,0:T(8,128)(2,1)S(1)}, u32[]{:S(2)}, u32[]{:S(2)}) collective-permute-start(bf16[192,768]{1,0:T(8,128)(2,1)S(1)} %bitcast.15), channel_id=1, source_target_pairs={{0,24},{8,0},{16,8},{24,16},{1,25},{9,1},{17,9},{25,17},{2,26},{10... | collective-permute-start | bytes 884744 | tf_op jit(solution)/shard_map/ppermute | solution.py:50
  36.1 3.1 %shard_map.78 = (bf16[3,768,768]{2,1,0:T(8,128)(2,1)S(1)}, bf16[3,768,768]{2,1,0:T(8,128)(2,1)S(1)}) custom-call(bf16[3,768,768]{2,1,0:T(8,128)(2,1)} %bitcast.20, bf16[3,768,768]{2,1,0:T(8,128)(2,1)} %bitcast.21), custom_call_target="tpu_custom_call" | custom-call | bytes 7077888 | tf_op jit(solution)/shard_map/pallas_call | solution.py:302
  42.9 3.0 %collective-permute-start.7 = (bf16[192,768]{1,0:T(8,128)(2,1)S(1)}, bf16[192,768]{1,0:T(8,128)(2,1)S(1)}, u32[]{:S(2)}, u32[]{:S(2)}) collective-permute-start(bf16[192,768]{1,0:T(8,128)(2,1)S(1)} %bitcast.8), channel_id=1, source_target_pairs={{0,24},{8,0},{16,8},{24,16},{1,25},{9,1},{17,9},{25,17},{2,26},{10... | collective-permute-start | bytes 884744 | tf_op jit(solution)/shard_map/ppermute | solution.py:50
  48.2 4.1 %collective-permute-done.15.refs_3_ = bf16[192,768]{1,0:T(8,128)(2,1)S(1)} collective-permute-done((bf16[192,768]{1,0:T(8,128)(2,1)S(1)}, bf16[192,768]{1,0:T(8,128)(2,1)S(1)}, u32[]{:S(2)}, u32[]{:S(2)}) %collective-permute-start.15) | collective-permute-done | bytes 294944 | tf_op jit(solution)/shard_map/ppermute | solution.py:50
  52.3 2.0 %copy-done.4 = bf16[3,768,768]{2,1,0:T(8,128)(2,1)S(1)} copy-done((bf16[3,768,768]{2,1,0:T(8,128)(2,1)S(1)}, bf16[3,768,768]{2,1,0:T(8,128)(2,1)}, u32[]{:S(2)}) %copy-start.4) | copy-done | bytes 3538968
  54.3 2.0 %copy-done.7 = bf16[3,768,768]{2,1,0:T(8,128)(2,1)S(1)} copy-done((bf16[3,768,768]{2,1,0:T(8,128)(2,1)S(1)}, bf16[3,768,768]{2,1,0:T(8,128)(2,1)}, u32[]{:S(2)}) %copy-start.7) | copy-done | bytes 3538968
  56.3 6.1 %shard_map.83 = (f32[192,768]{1,0:T(8,128)S(1)}, bf16[192,768]{1,0:T(8,128)(2,1)S(1)}, bf16[192,768]{1,0:T(8,128)(2,1)S(1)}, bf16[192,768]{1,0:T(8,128)(2,1)S(1)}) custom-call(bf16[3,768,768]{2,1,0:T(8,128)(2,1)S(1)} %copy-done.4, bf16[3,768,768]{2,1,0:T(8,128)(2,1)S(1)} %copy-done.7, bf16[192,768]{1,0:T(8,128)(2,1)S(1)} %bitcast.18, ...), custom_call_target="tpu_custom_call" | custom-call | flops 5435817984 | bytes 1048576 | tf_op jit(solution)/shard_map/pallas_call | solution.py:313
  67.0 2.1 %collective-permute-start.20 = (f32[8,128]{1,0:T(8,128)S(1)}, f32[8,128]{1,0:T(8,128)S(1)}, u32[]{:S(2)}, u32[]{:S(2)}) collective-permute-start(f32[8,128]{1,0:T(8,128)S(1)} %shard_map.84.refs_4_), channel_id=1, source_target_pairs={{0,16},{8,24},{16,0},{24,8},{1,17},{9,25},{17,1},{25,9},{2,18},{10... | collective-permute-start | bytes 12296 | tf_op jit(solution)/shard_map/ppermute | solution.py:55
  69.1 9.8 %collective-permute-done.19.refs_5_ = f32[8,128]{1,0:T(8,128)S(1)} collective-permute-done((f32[8,128]{1,0:T(8,128)S(1)}, f32[8,128]{1,0:T(8,128)S(1)}, u32[]{:S(2)}, u32[]{:S(2)}) %collective-permute-start.19) | collective-permute-done | bytes 4128 | tf_op jit(solution)/shard_map/ppermute | solution.py:55
  78.9 3.6 %collective-permute-done.21.refs_7_ = f32[8,128]{1,0:T(8,128)S(1)} collective-permute-done((f32[8,128]{1,0:T(8,128)S(1)}, f32[8,128]{1,0:T(8,128)S(1)}, u32[]{:S(2)}, u32[]{:S(2)}) %collective-permute-start.21) | collective-permute-done | bytes 4128 | tf_op jit(solution)/shard_map/ppermute | solution.py:55
  83.5 7.2 %all-to-all-start.3 = ((f32[8,152,128]{2,1,0:T(8,128)}), f32[8,152,128]{2,1,0:T(8,128)S(1)}, u32[]{:S(2)}, u32[]{:S(2)}) async-start(f32[8,152,128]{2,1,0:T(8,128)} %shard_map.85), calls=%async_computation.3 | async-start | bytes 1245184 | tf_op jit(solution)/shard_map/all_to_all | solution.py:329
  90.7 2.0 %copy-done.5 = bf16[3,768,768]{2,1,0:T(8,128)(2,1)S(1)} copy-done((bf16[3,768,768]{2,1,0:T(8,128)(2,1)S(1)}, bf16[3,768,768]{2,1,0:T(8,128)(2,1)}, u32[]{:S(2)}) %copy-start.5) | copy-done | bytes 3538968
  94.7 6.2 %shard_map.81 = (f32[192,768]{1,0:T(8,128)S(1)}, bf16[192,768]{1,0:T(8,128)(2,1)S(1)}, bf16[192,768]{1,0:T(8,128)(2,1)S(1)}, bf16[192,768]{1,0:T(8,128)(2,1)S(1)}) custom-call(bf16[3,768,768]{2,1,0:T(8,128)(2,1)S(1)} %copy-done.5, bf16[3,768,768]{2,1,0:T(8,128)(2,1)S(1)} %copy-done.8, bf16[192,768]{1,0:T(8,128)(2,1)S(1)} %bitcast.12, ...), custom_call_target="tpu_custom_call" | custom-call | flops 5435817984 | bytes 1048576 | tf_op jit(solution)/shard_map/pallas_call | solution.py:321
  101.1 2.7 %collective-permute-start.11 = (bf16[192,768]{1,0:T(8,128)(2,1)S(1)}, bf16[192,768]{1,0:T(8,128)(2,1)S(1)}, u32[]{:S(2)}, u32[]{:S(2)}) collective-permute-start(bf16[192,768]{1,0:T(8,128)(2,1)S(1)} %get-tuple-element.21), channel_id=1, source_target_pairs={{0,16},{8,24},{16,0},{24,8},{1,17},{9,25},{17,1},{25,9},{2,18},{10... | collective-permute-start | bytes 884744 | tf_op jit(solution)/shard_map/ppermute | solution.py:55
  104.3 10.7 %collective-permute-done.10.refs_1_ = bf16[192,768]{1,0:T(8,128)(2,1)S(1)} collective-permute-done((bf16[192,768]{1,0:T(8,128)(2,1)S(1)}, bf16[192,768]{1,0:T(8,128)(2,1)S(1)}, u32[]{:S(2)}, u32[]{:S(2)}) %collective-permute-start.10) | collective-permute-done | bytes 294944 | tf_op jit(solution)/shard_map/ppermute | solution.py:55
  116.2 7.2 %all-to-all-start.1 = ((bf16[8,24,768]{2,1,0:T(8,128)(2,1)}), bf16[8,24,768]{2,1,0:T(8,128)(2,1)S(1)}, u32[]{:S(2)}, u32[]{:S(2)}) async-start(bf16[8,24,768]{2,1,0:T(8,128)(2,1)} %shard_map.82), calls=%async_computation.1 | async-start | bytes 589824 | tf_op jit(solution)/shard_map/all_to_all | solution.py:335
  124.1 2.7 %collective-permute-start.24 = (f32[152,128]{1,0:T(8,128)S(1)}, f32[152,128]{1,0:T(8,128)S(1)}, u32[]{:S(2)}, u32[]{:S(2)}) collective-permute-start(f32[152,128]{1,0:T(8,128)S(1)} %shard_map.86.refs_0_), channel_id=1, source_target_pairs={{0,192},{32,224},{64,0},{96,32},{128,64},{160,96},{192,128},{224,1... | collective-permute-start | bytes 233480 | tf_op jit(solution)/shard_map/ppermute | solution.py:38
  126.8 3.0 %collective-permute-start.26 = (f32[152,128]{1,0:T(8,128)S(1)}, f32[152,128]{1,0:T(8,128)S(1)}, u32[]{:S(2)}, u32[]{:S(2)}) collective-permute-start(f32[152,128]{1,0:T(8,128)S(1)} %shard_map.86.refs_0_), channel_id=1, source_target_pairs={{0,224},{32,192},{64,32},{96,0},{128,96},{160,64},{192,160},{224,1... | collective-permute-start | bytes 233480 | tf_op jit(solution)/shard_map/ppermute | solution.py:38
  130.1 2.4 %collective-permute-start.28 = (f32[152,128]{1,0:T(8,128)S(1)}, f32[152,128]{1,0:T(8,128)S(1)}, u32[]{:S(2)}, u32[]{:S(2)}) collective-permute-start(f32[152,128]{1,0:T(8,128)S(1)} %shard_map.86.refs_0_), channel_id=1, source_target_pairs={{0,160},{32,128},{64,224},{96,192},{128,32},{160,0},{192,96},{224,... | collective-permute-start | bytes 233480 | tf_op jit(solution)/shard_map/ppermute | solution.py:38
  132.8 2.3 %collective-permute-done.26.refs_5_ = f32[152,128]{1,0:T(8,128)S(1)} collective-permute-done((f32[152,128]{1,0:T(8,128)S(1)}, f32[152,128]{1,0:T(8,128)S(1)}, u32[]{:S(2)}, u32[]{:S(2)}) %collective-permute-start.26) | collective-permute-done | bytes 77856 | tf_op jit(solution)/shard_map/ppermute | solution.py:38
  (71 shorter events, 29.5 us)
Async XLA Ops:
  2.8 21.5 %all-to-all-start.2 = ((bf16[8,24,768]{2,1,0:T(8,128)(2,1)}), bf16[8,24,768]{2,1,0:T(8,128)(2,1)S(1)}, u32[]{:S(2)}, u32[]{:S(2)}) async-start(bf16[8,24,768]{2,1,0:T(8,128)(2,1)} %get-tuple-element.23), calls=%async_computation.2 | async-start | bytes 589824 | tf_op jit(solution)/shard_map/all_to_all | solution.py:287
  11.4 6.8 %collective-permute-start.1 = (bf16[24,768]{1,0:T(8,128)(2,1)S(1)}, bf16[24,768]{1,0:T(8,128)(2,1)S(1)}, u32[]{:S(2)}, u32[]{:S(2)}) collective-permute-start(bf16[24,768]{1,0:T(8,128)(2,1)S(1)} %get-tuple-element.18.refs_0_.live_ref), channel_id=1, source_target_pairs={{0,64},{32,96},{64,128},{96,160},{128,192},{160,224},{192,0},{224,... | collective-permute-start | bytes 110600 | tf_op jit(solution)/shard_map/ppermute | solution.py:38
  12.9 8.8 %collective-permute-start.2 = (bf16[24,768]{1,0:T(8,128)(2,1)S(1)}, bf16[24,768]{1,0:T(8,128)(2,1)S(1)}, u32[]{:S(2)}, u32[]{:S(2)}) collective-permute-start(bf16[24,768]{1,0:T(8,128)(2,1)S(1)} %get-tuple-element.18.refs_0_.live_ref), channel_id=1, source_target_pairs={{0,192},{32,224},{64,0},{96,32},{128,64},{160,96},{192,128},{224,1... | collective-permute-start | bytes 110600 | tf_op jit(solution)/shard_map/ppermute | solution.py:38
  14.6 7.0 %collective-permute-start.3 = (bf16[24,768]{1,0:T(8,128)(2,1)S(1)}, bf16[24,768]{1,0:T(8,128)(2,1)S(1)}, u32[]{:S(2)}, u32[]{:S(2)}) collective-permute-start(bf16[24,768]{1,0:T(8,128)(2,1)S(1)} %get-tuple-element.18.refs_0_.live_ref), channel_id=1, source_target_pairs={{0,96},{32,64},{64,160},{96,128},{128,224},{160,192},{192,32},{224... | collective-permute-start | bytes 110600 | tf_op jit(solution)/shard_map/ppermute | solution.py:38
  14.6 7.0 %collective-permute-start.4 = (bf16[24,768]{1,0:T(8,128)(2,1)S(1)}, bf16[24,768]{1,0:T(8,128)(2,1)S(1)}, u32[]{:S(2)}, u32[]{:S(2)}) collective-permute-start(bf16[24,768]{1,0:T(8,128)(2,1)S(1)} %get-tuple-element.18.refs_0_.live_ref), channel_id=1, source_target_pairs={{0,224},{32,192},{64,32},{96,0},{128,96},{160,64},{192,160},{224,1... | collective-permute-start | bytes 110600 | tf_op jit(solution)/shard_map/ppermute | solution.py:38
  24.3 18.7 %all-to-all-start = ((bf16[8,24,768]{2,1,0:T(8,128)(2,1)}), bf16[8,24,768]{2,1,0:T(8,128)(2,1)S(1)}, u32[]{:S(2)}, u32[]{:S(2)}) async-start(bf16[8,24,768]{2,1,0:T(8,128)(2,1)} %shard_map.80), calls=%async_computation | async-start | bytes 589824 | tf_op jit(solution)/shard_map/all_to_all | solution.py:294
  31.5 16.7 %collective-permute-start.13 = (bf16[192,768]{1,0:T(8,128)(2,1)S(1)}, bf16[192,768]{1,0:T(8,128)(2,1)S(1)}, u32[]{:S(2)}, u32[]{:S(2)}) collective-permute-start(bf16[192,768]{1,0:T(8,128)(2,1)S(1)} %bitcast.15), channel_id=1, source_target_pairs={{0,24},{8,0},{16,8},{24,16},{1,25},{9,1},{17,9},{25,17},{2,26},{10... | collective-permute-start | bytes 884744 | tf_op jit(solution)/shard_map/ppermute | solution.py:50
  34.5 13.7 %collective-permute-start.14 = (bf16[192,768]{1,0:T(8,128)(2,1)S(1)}, bf16[192,768]{1,0:T(8,128)(2,1)S(1)}, u32[]{:S(2)}, u32[]{:S(2)}) collective-permute-start(bf16[192,768]{1,0:T(8,128)(2,1)S(1)} %bitcast.16), channel_id=1, source_target_pairs={{0,16},{8,24},{16,0},{24,8},{1,17},{9,25},{17,1},{25,9},{2,18},{10... | collective-permute-start | bytes 884744 | tf_op jit(solution)/shard_map/ppermute | solution.py:50
  35.1 17.2 %collective-permute-start.15 = (bf16[192,768]{1,0:T(8,128)(2,1)S(1)}, bf16[192,768]{1,0:T(8,128)(2,1)S(1)}, u32[]{:S(2)}, u32[]{:S(2)}) collective-permute-start(bf16[192,768]{1,0:T(8,128)(2,1)S(1)} %bitcast.17), channel_id=1, source_target_pairs={{0,8},{8,16},{16,24},{24,0},{1,9},{9,17},{17,25},{25,1},{2,10},{10... | collective-permute-start | bytes 884744 | tf_op jit(solution)/shard_map/ppermute | solution.py:50
  42.9 21.5 %collective-permute-start.7 = (bf16[192,768]{1,0:T(8,128)(2,1)S(1)}, bf16[192,768]{1,0:T(8,128)(2,1)S(1)}, u32[]{:S(2)}, u32[]{:S(2)}) collective-permute-start(bf16[192,768]{1,0:T(8,128)(2,1)S(1)} %bitcast.8), channel_id=1, source_target_pairs={{0,24},{8,0},{16,8},{24,16},{1,25},{9,1},{17,9},{25,17},{2,26},{10... | collective-permute-start | bytes 884744 | tf_op jit(solution)/shard_map/ppermute | solution.py:50
  46.0 20.3 %collective-permute-start.8 = (bf16[192,768]{1,0:T(8,128)(2,1)S(1)}, bf16[192,768]{1,0:T(8,128)(2,1)S(1)}, u32[]{:S(2)}, u32[]{:S(2)}) collective-permute-start(bf16[192,768]{1,0:T(8,128)(2,1)S(1)} %bitcast.9), channel_id=1, source_target_pairs={{0,16},{8,24},{16,0},{24,8},{1,17},{9,25},{17,1},{25,9},{2,18},{10... | collective-permute-start | bytes 884744 | tf_op jit(solution)/shard_map/ppermute | solution.py:50
  48.2 18.0 %collective-permute-start.9 = (bf16[192,768]{1,0:T(8,128)(2,1)S(1)}, bf16[192,768]{1,0:T(8,128)(2,1)S(1)}, u32[]{:S(2)}, u32[]{:S(2)}) collective-permute-start(bf16[192,768]{1,0:T(8,128)(2,1)S(1)} %bitcast.10), channel_id=1, source_target_pairs={{0,8},{8,16},{16,24},{24,0},{1,9},{9,17},{17,25},{25,1},{2,10},{10... | collective-permute-start | bytes 884744 | tf_op jit(solution)/shard_map/ppermute | solution.py:50
  62.4 20.1 %collective-permute-start.16 = (bf16[192,768]{1,0:T(8,128)(2,1)S(1)}, bf16[192,768]{1,0:T(8,128)(2,1)S(1)}, u32[]{:S(2)}, u32[]{:S(2)}) collective-permute-start(bf16[192,768]{1,0:T(8,128)(2,1)S(1)} %get-tuple-element.25.refs_5_), channel_id=1, source_target_pairs={{0,8},{8,16},{16,24},{24,0},{1,9},{9,17},{17,25},{25,1},{2,10},{10... | collective-permute-start | bytes 884744 | tf_op jit(solution)/shard_map/ppermute | solution.py:55
  62.5 20.0 %collective-permute-start.17 = (bf16[192,768]{1,0:T(8,128)(2,1)S(1)}, bf16[192,768]{1,0:T(8,128)(2,1)S(1)}, u32[]{:S(2)}, u32[]{:S(2)}) collective-permute-start(bf16[192,768]{1,0:T(8,128)(2,1)S(1)} %get-tuple-element.26.refs_6_), channel_id=1, source_target_pairs={{0,16},{8,24},{16,0},{24,8},{1,17},{9,25},{17,1},{25,9},{2,18},{10... | collective-permute-start | bytes 884744 | tf_op jit(solution)/shard_map/ppermute | solution.py:55
  64.5 18.0 %collective-permute-start.18 = (bf16[192,768]{1,0:T(8,128)(2,1)S(1)}, bf16[192,768]{1,0:T(8,128)(2,1)S(1)}, u32[]{:S(2)}, u32[]{:S(2)}) collective-permute-start(bf16[192,768]{1,0:T(8,128)(2,1)S(1)} %get-tuple-element.27.refs_7_), channel_id=1, source_target_pairs={{0,24},{8,0},{16,8},{24,16},{1,25},{9,1},{17,9},{25,17},{2,26},{10... | collective-permute-start | bytes 884744 | tf_op jit(solution)/shard_map/ppermute | solution.py:55
  66.6 12.3 %collective-permute-start.19 = (f32[8,128]{1,0:T(8,128)S(1)}, f32[8,128]{1,0:T(8,128)S(1)}, u32[]{:S(2)}, u32[]{:S(2)}) collective-permute-start(f32[8,128]{1,0:T(8,128)S(1)} %shard_map.84.refs_4_), channel_id=1, source_target_pairs={{0,8},{8,16},{16,24},{24,0},{1,9},{9,17},{17,25},{25,1},{2,10},{10... | collective-permute-start | bytes 12296 | tf_op jit(solution)/shard_map/ppermute | solution.py:55
  67.0 11.9 %collective-permute-start.20 = (f32[8,128]{1,0:T(8,128)S(1)}, f32[8,128]{1,0:T(8,128)S(1)}, u32[]{:S(2)}, u32[]{:S(2)}) collective-permute-start(f32[8,128]{1,0:T(8,128)S(1)} %shard_map.84.refs_4_), channel_id=1, source_target_pairs={{0,16},{8,24},{16,0},{24,8},{1,17},{9,25},{17,1},{25,9},{2,18},{10... | collective-permute-start | bytes 12296 | tf_op jit(solution)/shard_map/ppermute | solution.py:55
  83.5 32.7 %all-to-all-start.3 = ((f32[8,152,128]{2,1,0:T(8,128)}), f32[8,152,128]{2,1,0:T(8,128)S(1)}, u32[]{:S(2)}, u32[]{:S(2)}) async-start(f32[8,152,128]{2,1,0:T(8,128)} %shard_map.85), calls=%async_computation.3 | async-start | bytes 1245184 | tf_op jit(solution)/shard_map/all_to_all | solution.py:329
  101.0 14.0 %collective-permute-start.10 = (bf16[192,768]{1,0:T(8,128)(2,1)S(1)}, bf16[192,768]{1,0:T(8,128)(2,1)S(1)}, u32[]{:S(2)}, u32[]{:S(2)}) collective-permute-start(bf16[192,768]{1,0:T(8,128)(2,1)S(1)} %get-tuple-element.20), channel_id=1, source_target_pairs={{0,8},{8,16},{16,24},{24,0},{1,9},{9,17},{17,25},{25,1},{2,10},{10... | collective-permute-start | bytes 884744 | tf_op jit(solution)/shard_map/ppermute | solution.py:55
  101.1 13.9 %collective-permute-start.11 = (bf16[192,768]{1,0:T(8,128)(2,1)S(1)}, bf16[192,768]{1,0:T(8,128)(2,1)S(1)}, u32[]{:S(2)}, u32[]{:S(2)}) collective-permute-start(bf16[192,768]{1,0:T(8,128)(2,1)S(1)} %get-tuple-element.21), channel_id=1, source_target_pairs={{0,16},{8,24},{16,0},{24,8},{1,17},{9,25},{17,1},{25,9},{2,18},{10... | collective-permute-start | bytes 884744 | tf_op jit(solution)/shard_map/ppermute | solution.py:55
  103.8 11.6 %collective-permute-start.12 = (bf16[192,768]{1,0:T(8,128)(2,1)S(1)}, bf16[192,768]{1,0:T(8,128)(2,1)S(1)}, u32[]{:S(2)}, u32[]{:S(2)}) collective-permute-start(bf16[192,768]{1,0:T(8,128)(2,1)S(1)} %get-tuple-element.22), channel_id=1, source_target_pairs={{0,24},{8,0},{16,8},{24,16},{1,25},{9,1},{17,9},{25,17},{2,26},{10... | collective-permute-start | bytes 884744 | tf_op jit(solution)/shard_map/ppermute | solution.py:55
  116.2 16.6 %all-to-all-start.1 = ((bf16[8,24,768]{2,1,0:T(8,128)(2,1)}), bf16[8,24,768]{2,1,0:T(8,128)(2,1)S(1)}, u32[]{:S(2)}, u32[]{:S(2)}) async-start(bf16[8,24,768]{2,1,0:T(8,128)(2,1)} %shard_map.82), calls=%async_computation.1 | async-start | bytes 589824 | tf_op jit(solution)/shard_map/all_to_all | solution.py:335
  124.1 8.6 %collective-permute-start.24 = (f32[152,128]{1,0:T(8,128)S(1)}, f32[152,128]{1,0:T(8,128)S(1)}, u32[]{:S(2)}, u32[]{:S(2)}) collective-permute-start(f32[152,128]{1,0:T(8,128)S(1)} %shard_map.86.refs_0_), channel_id=1, source_target_pairs={{0,192},{32,224},{64,0},{96,32},{128,64},{160,96},{192,128},{224,1... | collective-permute-start | bytes 233480 | tf_op jit(solution)/shard_map/ppermute | solution.py:38
  126.8 8.2 %collective-permute-start.26 = (f32[152,128]{1,0:T(8,128)S(1)}, f32[152,128]{1,0:T(8,128)S(1)}, u32[]{:S(2)}, u32[]{:S(2)}) collective-permute-start(f32[152,128]{1,0:T(8,128)S(1)} %shard_map.86.refs_0_), channel_id=1, source_target_pairs={{0,224},{32,192},{64,32},{96,0},{128,96},{160,64},{192,160},{224,1... | collective-permute-start | bytes 233480 | tf_op jit(solution)/shard_map/ppermute | solution.py:38
  (18 other events, 75.4 us)
